TPU v7x, 8 devices: a whole 2x2x1 slice. The times are simulated.
8 devices in a mesh: dp: 1 (over z), col: 2 (over y), row: 4 (over x, core).
Axes of the slice: x: 2, y: 2, z: 1, core: 2. Of those that a mesh axis runs over, the one named last changes fastest.
Arguments:
- a_mat: bfloat16 [8192, 8192], P(('dp', 'row'), 'col')
- b_mat: bfloat16 [8192, 28672], P('row', 'col')
Outputs:
- output: bfloat16 [8192, 28672], P(('dp', 'row'), 'col')
All inputs are finite; a program needn't handle non-finite values.
Results may differ from a plain program's by a relative error of at most 0.001.
Values are sent between devices in bfloat16 or wider.
A program may use at most 1 GiB of HBM per device.

v0:
```python
import jax
import jax.numpy as jnp
from jax import lax
from jax.sharding import PartitionSpec as P


def solution(mesh):
    num_rows = mesh.shape["row"]
    num_cols = mesh.shape["col"]
    num_steps = max(num_rows, num_cols)
    per_col = num_steps // num_cols
    per_row = num_steps // num_rows

    def local_product(a_blk, b_blk):
        row_id = lax.axis_index("row")
        col_id = lax.axis_index("col")
        panel_width = a_blk.shape[1] // per_col

        def update_step(k_step, c_accum):
            a_src = lax.dynamic_slice_in_dim(a_blk, (k_step % per_col) * panel_width, panel_width, axis=1)
            a_panel = lax.psum(jnp.where(col_id == k_step // per_col, a_src, jnp.zeros_like(a_src)), "col")
            b_src = lax.dynamic_slice_in_dim(b_blk, (k_step % per_row) * panel_width, panel_width, axis=0)
            b_panel = lax.psum(jnp.where(row_id == k_step // per_row, b_src, jnp.zeros_like(b_src)), "row")
            return c_accum + jnp.dot(a_panel, b_panel, preferred_element_type=jnp.float32)

        c_init = jnp.zeros((a_blk.shape[0], b_blk.shape[1]), jnp.float32)
        c_accum = lax.fori_loop(0, num_steps, update_step, c_init)
        return c_accum.astype(jnp.bfloat16)

    return jax.shard_map(local_product, mesh=mesh, in_specs=(P(("dp", "row"), "col"), P("row", "col")), out_specs=P(("dp", "row"), "col"), check_vma=False)
```

profile of v0, /device:TPU:0, one launch (start us, length us, event | category | flops | bytes accessed | tf_op | source)
XLA Modules:
  0.0 5257.7 jit_solution(12073119022769063850)
XLA Ops:
  6.5 5188.6 %while.17 = (s32[]{:T(128)}, f32[2048,14336]{1,0:T(8,128)}, s32[]{:T(128)}, bf16[2048,4096]{1,0:T(8,128)(2,1)}, s32[]{:T(128)}, /*index=5*/bf16[2048,14336]{1,0:...) while((s32[]{:T(128)}, f32[2048,14336]{1,0:T(8,128)}, ...), condition=%wide.region_3.4_spmd.clone, body=%wide.region_0.3_spmd.clone.sunk | while | flops 120384913408 | bytes 838861184 | solution.py:27
  6.5 0.0 all-reduce.3.cloned.1.call-start
  6.5 9.7 dynamic-slice_select_fusion.2
  16.2 0.0 all-reduce.3.cloned.1.call-update
  16.2 0.0 all-reduce.5.cloned.1.call-start
  16.3 39.0 broadcast_select_fusion.2
  55.3 0.0 all-reduce.5.cloned.1.call-update
  55.3 156.0 %all-reduce.3.cloned.1.call-done = bf16[2048,2048]{1,0:T(8,128)(2,1)} async-done(((bf16[2048,2048]{1,0:T(8,128)(2,1)}), bf16[2048,2048]{1,0:T(8,128)(2,1)}) %all-reduce.3.cloned.1.call-update) | async-done | bytes 8388624 | tf_op jit(solution)/shard_map/while/body/eval_jaxpr/psum | solution.py:21
  211.4 959.5 %all-reduce.5.cloned.1.call-done = bf16[2048,14336]{1,0:T(8,128)(2,1)} async-done(((bf16[2048,14336]{1,0:T(8,128)(2,1)}), bf16[2048,14336]{1,0:T(8,128)(2,1)}) %all-reduce.5.cloned.1.call-update) | async-done | bytes 58720272 | tf_op jit(solution)/shard_map/while/body/eval_jaxpr/psum | solution.py:23
  1170.9 133.0 %select_add_fusion.2 = f32[2048,14336]{1,0:T(8,128)} fusion(f32[2048,14336]{1,0:T(8,128)} %get-tuple-element.276, bf16[2048,2048]{1,0:T(8,128)(2,1)} %all-reduce.3.cloned.1.call-done, bf16[2048,14336]{1,0:T(8,128)(2,1)} %all-reduce.5.cloned.1.call-done, pred[]{:T(512)S(6)} %compare.21), kind=kOutput, calls=%fused_computation.clone.1 | convolution fusion | flops 120317804544 | bytes 301989888 | tf_op jit(solution)/shard_map/while/body/eval_jaxpr/dot_general | solution.py:24
  1303.9 0.0 all-reduce.3.cloned.1.call-start
  1303.9 9.7 dynamic-slice_select_fusion.2
  1313.5 0.0 all-reduce.3.cloned.1.call-update
  1313.6 0.0 all-reduce.5.cloned.1.call-start
  1313.6 18.8 broadcast_select_fusion.2
  1332.4 0.0 all-reduce.5.cloned.1.call-update
  1332.5 173.7 %all-reduce.3.cloned.1.call-done = bf16[2048,2048]{1,0:T(8,128)(2,1)} async-done(((bf16[2048,2048]{1,0:T(8,128)(2,1)}), bf16[2048,2048]{1,0:T(8,128)(2,1)}) %all-reduce.3.cloned.1.call-update) | async-done | bytes 8388624 | tf_op jit(solution)/shard_map/while/body/eval_jaxpr/psum | solution.py:21
  1506.2 959.3 %all-reduce.5.cloned.1.call-done = bf16[2048,14336]{1,0:T(8,128)(2,1)} async-done(((bf16[2048,14336]{1,0:T(8,128)(2,1)}), bf16[2048,14336]{1,0:T(8,128)(2,1)}) %all-reduce.5.cloned.1.call-update) | async-done | bytes 58720272 | tf_op jit(solution)/shard_map/while/body/eval_jaxpr/psum | solution.py:23
  2465.5 135.4 %select_add_fusion.2 = f32[2048,14336]{1,0:T(8,128)} fusion(f32[2048,14336]{1,0:T(8,128)} %get-tuple-element.276, bf16[2048,2048]{1,0:T(8,128)(2,1)} %all-reduce.3.cloned.1.call-done, bf16[2048,14336]{1,0:T(8,128)(2,1)} %all-reduce.5.cloned.1.call-done, pred[]{:T(512)S(6)} %compare.21), kind=kOutput, calls=%fused_computation.clone.1 | convolution fusion | flops 120317804544 | bytes 301989888 | tf_op jit(solution)/shard_map/while/body/eval_jaxpr/dot_general | solution.py:24
  2600.9 0.0 all-reduce.3.cloned.1.call-start
  2600.9 9.7 dynamic-slice_select_fusion.2
  2610.6 0.0 all-reduce.3.cloned.1.call-update
  2610.6 0.0 all-reduce.5.cloned.1.call-start
  2610.6 18.8 broadcast_select_fusion.2
  2629.5 0.0 all-reduce.5.cloned.1.call-update
  2629.5 173.7 %all-reduce.3.cloned.1.call-done = bf16[2048,2048]{1,0:T(8,128)(2,1)} async-done(((bf16[2048,2048]{1,0:T(8,128)(2,1)}), bf16[2048,2048]{1,0:T(8,128)(2,1)}) %all-reduce.3.cloned.1.call-update) | async-done | bytes 8388624 | tf_op jit(solution)/shard_map/while/body/eval_jaxpr/psum | solution.py:21
  2803.2 959.3 %all-reduce.5.cloned.1.call-done = bf16[2048,14336]{1,0:T(8,128)(2,1)} async-done(((bf16[2048,14336]{1,0:T(8,128)(2,1)}), bf16[2048,14336]{1,0:T(8,128)(2,1)}) %all-reduce.5.cloned.1.call-update) | async-done | bytes 58720272 | tf_op jit(solution)/shard_map/while/body/eval_jaxpr/psum | solution.py:23
  3762.5 135.4 %select_add_fusion.2 = f32[2048,14336]{1,0:T(8,128)} fusion(f32[2048,14336]{1,0:T(8,128)} %get-tuple-element.276, bf16[2048,2048]{1,0:T(8,128)(2,1)} %all-reduce.3.cloned.1.call-done, bf16[2048,14336]{1,0:T(8,128)(2,1)} %all-reduce.5.cloned.1.call-done, pred[]{:T(512)S(6)} %compare.21), kind=kOutput, calls=%fused_computation.clone.1 | convolution fusion | flops 120317804544 | bytes 301989888 | tf_op jit(solution)/shard_map/while/body/eval_jaxpr/dot_general | solution.py:24
  3897.9 0.0 all-reduce.3.cloned.1.call-start
  3897.9 9.7 dynamic-slice_select_fusion.2
  3907.6 0.0 all-reduce.3.cloned.1.call-update
  3907.6 0.0 all-reduce.5.cloned.1.call-start
  3907.7 18.8 broadcast_select_fusion.2
  3926.5 0.0 all-reduce.5.cloned.1.call-update
  3926.5 173.7 %all-reduce.3.cloned.1.call-done = bf16[2048,2048]{1,0:T(8,128)(2,1)} async-done(((bf16[2048,2048]{1,0:T(8,128)(2,1)}), bf16[2048,2048]{1,0:T(8,128)(2,1)}) %all-reduce.3.cloned.1.call-update) | async-done | bytes 8388624 | tf_op jit(solution)/shard_map/while/body/eval_jaxpr/psum | solution.py:21
  4100.2 959.5 %all-reduce.5.cloned.1.call-done = bf16[2048,14336]{1,0:T(8,128)(2,1)} async-done(((bf16[2048,14336]{1,0:T(8,128)(2,1)}), bf16[2048,14336]{1,0:T(8,128)(2,1)}) %all-reduce.5.cloned.1.call-update) | async-done | bytes 58720272 | tf_op jit(solution)/shard_map/while/body/eval_jaxpr/psum | solution.py:23
  5059.7 135.4 %select_add_fusion.2 = f32[2048,14336]{1,0:T(8,128)} fusion(f32[2048,14336]{1,0:T(8,128)} %get-tuple-element.276, bf16[2048,2048]{1,0:T(8,128)(2,1)} %all-reduce.3.cloned.1.call-done, bf16[2048,14336]{1,0:T(8,128)(2,1)} %all-reduce.5.cloned.1.call-done, pred[]{:T(512)S(6)} %compare.21), kind=kOutput, calls=%fused_computation.clone.1 | convolution fusion | flops 120317804544 | bytes 301989888 | tf_op jit(solution)/shard_map/while/body/eval_jaxpr/dot_general | solution.py:24
  5195.1 55.8 %convert_element_type.3 = bf16[2048,14336]{1,0:T(8,128)(2,1)} convert(f32[2048,14336]{1,0:T(8,128)} %get-tuple-element.192) | non-fusion elementwise | flops 29360128 | bytes 176160768 | tf_op jit(solution)/shard_map/convert_element_type | solution.py:28
  (1 shorter events, 0.0 us)
Async XLA Ops:
  6.5 204.9 %all-reduce.3.cloned.1.call-start = ((), (), s32[]{:S(2)}) async-start(), calls=%async_computation | async-start | bytes 16777216 | tf_op jit(solution)/shard_map/while/body/eval_jaxpr/psum | solution.py:21
  16.2 1154.6 %all-reduce.5.cloned.1.call-start = ((), (), s32[]{:S(2)}) async-start(), calls=%async_computation.1 | async-start | bytes 117440512 | tf_op jit(solution)/shard_map/while/body/eval_jaxpr/psum | solution.py:23
  1303.9 202.3 %all-reduce.3.cloned.1.call-start = ((), (), s32[]{:S(2)}) async-start(), calls=%async_computation | async-start | bytes 16777216 | tf_op jit(solution)/shard_map/while/body/eval_jaxpr/psum | solution.py:21
  1313.6 1151.9 %all-reduce.5.cloned.1.call-start = ((), (), s32[]{:S(2)}) async-start(), calls=%async_computation.1 | async-start | bytes 117440512 | tf_op jit(solution)/shard_map/while/body/eval_jaxpr/psum | solution.py:23
  2600.9 202.3 %all-reduce.3.cloned.1.call-start = ((), (), s32[]{:S(2)}) async-start(), calls=%async_computation | async-start | bytes 16777216 | tf_op jit(solution)/shard_map/while/body/eval_jaxpr/psum | solution.py:21
  2610.6 1151.9 %all-reduce.5.cloned.1.call-start = ((), (), s32[]{:S(2)}) async-start(), calls=%async_computation.1 | async-start | bytes 117440512 | tf_op jit(solution)/shard_map/while/body/eval_jaxpr/psum | solution.py:23
  3897.9 202.3 %all-reduce.3.cloned.1.call-start = ((), (), s32[]{:S(2)}) async-start(), calls=%async_computation | async-start | bytes 16777216 | tf_op jit(solution)/shard_map/while/body/eval_jaxpr/psum | solution.py:21
  3907.6 1152.1 %all-reduce.5.cloned.1.call-start = ((), (), s32[]{:S(2)}) async-start(), calls=%async_computation.1 | async-start | bytes 117440512 | tf_op jit(solution)/shard_map/while/body/eval_jaxpr/psum | solution.py:23
Sparse Core Ops, SparseCore 0:
  16.4 194.9 all-reduce.2
  213.9 956.9 all-reduce.4
  1313.7 192.4 all-reduce.2
  1508.5 956.9 all-reduce.4
  2610.7 192.4 all-reduce.2
  2805.5 956.9 all-reduce.4
  3907.7 192.4 all-reduce.2
  4102.7 956.9 all-reduce.4
where the time goes:
time: 5260 us
  waiting for transfers between devices  4510 us (86%)
  matrix products  539 us (10%)
  other arithmetic  190 us (4%)
    psum x4, waiting for transfers between devices, update_step(): lax.psum(jnp.where(row_id == k_step // per_row, b_src, jnp.zeros_like(b_s...  3840 us
    psum x4, waiting for transfers between devices, update_step(): lax.psum(jnp.where(col_id == k_step // per_col, a_src, jnp.zeros_like(a_s...  677 us
    dot_general x4, matrix products, update_step(): jnp.dot(a_panel, b_panel, preferred_element_type=jnp.float32)  539 us
  transfers between devices with their start and end apart: 8, of which 8 were waited for; matrix products, arithmetic and copies ran while one was open for 2% of the time, Pallas kernels for 0%

commit v1 on v0

v1 whole, which is shorter than its diff:
```python
import jax
import jax.numpy as jnp
from jax import lax
from jax.experimental import pallas as pl
from jax.experimental.pallas import tpu as pltpu
from jax.sharding import PartitionSpec as P


UNIT = 256
PIECES = (2, 8, 10, 10, 10, 8, 4, 2, 1, 1)


def product_body(core_ref, a0, a1, a2, a3, b0, b1, b2, b3, *rest):
    c_ref = rest[-1]
    total = jnp.dot(a0[...], b0[...], preferred_element_type=jnp.float32)
    total += jnp.dot(a1[...], b1[...], preferred_element_type=jnp.float32)
    total += jnp.dot(a2[...], b2[...], preferred_element_type=jnp.float32)
    total += jnp.dot(a3[...], b3[...], preferred_element_type=jnp.float32)
    c_ref[...] = total.astype(c_ref.dtype)


def product(core, a_near, a_far, b_own, b_pair, x_own, x_pair, c_prev, start, tm=512):
    rows = a_near.shape[0]
    depth, columns = b_own.shape
    width = x_own.shape[1]
    tn = 512 if width % 512 == 0 and start % 512 == 0 else 256
    first = start // tn
    a_mine = pl.BlockSpec((tm, depth), lambda n, m, core: (m, core[0]))
    a_other = pl.BlockSpec((tm, depth), lambda n, m, core: (m, 1 - core[0]))
    b_whole = pl.BlockSpec((depth, tn), lambda n, m, core: (0, first + n))
    b_piece = pl.BlockSpec((depth, tn), lambda n, m, core: (0, n))
    in_specs = [a_mine, a_other, a_mine, a_other, b_whole, b_whole, b_piece, b_piece]
    args = [a_near, a_near, a_far, a_far, b_own, b_pair, x_own, x_pair]
    aliases = {}
    if c_prev is not None:
        in_specs.append(pl.BlockSpec(memory_space=pl.ANY))
        aliases = {1 + len(args): 0}
        args.append(c_prev)
    return pl.pallas_call(
        product_body,
        grid_spec=pltpu.PrefetchScalarGridSpec(
            num_scalar_prefetch=1,
            grid=(width // tn, rows // tm),
            in_specs=in_specs,
            out_specs=pl.BlockSpec((tm, tn), lambda n, m, core: (m, first + n)),
        ),
        out_shape=jax.ShapeDtypeStruct((rows, columns), jnp.bfloat16),
        input_output_aliases=aliases,
        cost_estimate=pl.CostEstimate(
            flops=2 * rows * 4 * depth * width,
            bytes_accessed=2 * (rows * 4 * depth * (width // tn) + 4 * depth * width + rows * width),
            transcendentals=0,
        ),
        compiler_params=pltpu.CompilerParams(vmem_limit_bytes=62 * 1024 * 1024),
    )(core, *args)


def solution(mesh):
    across = [(0, 2), (2, 0), (1, 3), (3, 1)]
    beside = [(0, 1), (1, 0), (2, 3), (3, 2)]
    pieces = []
    start = 0
    for n in PIECES:
        pieces.append((start, n * UNIT))
        start += n * UNIT

    def local_product(a_blk, b_blk):
        row_id = lax.axis_index("row")
        core = lax.rem(row_id, 2).astype(jnp.int32).reshape(1)
        aligned = lax.div(row_id, 2) == lax.axis_index("col")
        x_own = []
        for s, w in pieces:
            piece = lax.slice_in_dim(b_blk, s, s + w, axis=1)
            x_own.append(lax.ppermute(piece, "row", across))
        a_recv = lax.ppermute(a_blk, "col", [(0, 1), (1, 0)])
        b_pair = lax.ppermute(b_blk, "row", beside)
        a_near = jnp.where(aligned, a_blk, a_recv)
        a_far = jnp.where(aligned, a_recv, a_blk)
        c = None
        for j, (s, w) in enumerate(pieces):
            x = x_own[j]
            if j:
                x, c = lax.optimization_barrier((x, c))
            x_pair = lax.ppermute(x, "row", beside)
            c = product(core, a_near, a_far, b_blk, b_pair, x, x_pair, c, s)
        return c

    return jax.shard_map(
        local_product,
        mesh=mesh,
        in_specs=(P(("dp", "row"), "col"), P("row", "col")),
        out_specs=P(("dp", "row"), "col"),
        check_vma=False,
    )
```

time: 5260 us -> 1530 us (0.29)
  waiting for transfers between devices: 4510 us -> 828 us
  Pallas kernels: 0 us -> 613 us
  matrix products: 539 us -> 0 us
  other arithmetic: 190 us -> 22.6 us
    psum x8 -> x0, waiting for transfers between devices: 4510 us -> none  [the longest x4 3840 us: update_step(): lax.psum(jnp.where(row_id == k_step // per_row, b_src, jnp.zeros_like(b_s...]
    ppermute x0 -> x22, waiting for transfers between devices: none -> 828 us  [the longest x10 645 us: local_product(): x_own.append(lax.ppermute(piece, 'row', across))]
    pallas_call x0 -> x10, Pallas kernels: none -> 613 us  [product(): pl.pallas_call(product_body, grid_spec=pltpu.PrefetchScalarGridSpec(num_s...]
    dot_general x4 -> x0, matrix products: 539 us -> none  [update_step(): jnp.dot(a_panel, b_panel, preferred_element_type=jnp.float32)]
    select_n x8 -> x1, other arithmetic: 134 us -> 22.6 us  [local_product(): a_far = jnp.where(aligned, a_recv, a_blk)]
    convert_element_type x1 -> x0, other arithmetic: 55.8 us -> none  [local_product(): return c_accum.astype(jnp.bfloat16)]
  transfers between devices with their start and end apart: 8 -> 22, of which waited for: 8 -> 14; matrix products, arithmetic and copies ran while one was open for 2% -> 5% of each run, Pallas kernels for 0% -> 39%
where the time goes in v1:
time: 1530 us
  waiting for transfers between devices  828 us (54%)
  Pallas kernels  613 us (40%)
  local copies, waits for them, and re-layouts  48.7 us (3%)
  other arithmetic  22.6 us (1%)
  starting transfers between devices  19.1 us (1%)
    ppermute x10, waiting for transfers between devices, local_product(): x_own.append(lax.ppermute(piece, 'row', across))  645 us
    pallas_call x10, Pallas kernels, product(): pl.pallas_call(product_body, grid_spec=pltpu.PrefetchScalarGridSpec(num_s...  613 us
    ppermute x1, waiting for transfers between devices, local_product(): a_recv = lax.ppermute(a_blk, 'col', [(0, 1), (1, 0)])  122 us
    ppermute x10, waiting for transfers between devices, local_product(): x_pair = lax.ppermute(x, 'row', beside)  61.4 us
    slice x5, local copies, waits for them, and re-layouts, local_product(): piece = lax.slice_in_dim(b_blk, s, s + w, axis=1)  46.4 us
  transfers between devices with their start and end apart: 22, of which 14 were waited for; matrix products, arithmetic and copies ran while one was open for 5% of the time, Pallas kernels for 39%

profile of v1, /device:TPU:0, one launch (start us, length us, event | category | flops | bytes accessed | tf_op | source)
XLA Modules:
  0.0 1531.5 jit_solution(11037576526894078611)
XLA Ops:
  0.0 0.8 collective-permute-start.1
  0.8 2.5 collective-permute-start
  3.3 11.9 fusion.1
  15.2 1.5 collective-permute-start.10
  16.7 4.5 fusion
  21.3 0.5 collective-permute-start.11
  21.8 221.2 %collective-permute-done.11.b2 = bf16[2048,512]{1,0:T(8,128)(2,1)S(1)} collective-permute-done((bf16[2048,512]{1,0:T(8,128)(2,1)}, bf16[2048,512]{1,0:T(8,128)(2,1)S(1)}, u32[]{:S(2)}, u32[]{:S(2)}) %collective-permute-start.11) | collective-permute-done | bytes 2097184 | tf_op jit(solution)/shard_map/ppermute | solution.py:74
  243.0 121.6 %collective-permute-done = bf16[2048,4096]{1,0:T(8,128)(2,1)} collective-permute-done((bf16[2048,4096]{1,0:T(8,128)(2,1)}, bf16[2048,4096]{1,0:T(8,128)(2,1)}, u32[]{:S(2)}, u32[]{:S(2)}) %collective-permute-start) | collective-permute-done | bytes 16777248 | tf_op jit(solution)/shard_map/ppermute | solution.py:75
  364.5 22.6 %broadcast_select_fusion = (bf16[2048,4096]{1,0:T(8,128)(2,1)}, bf16[2048,4096]{1,0:T(8,128)(2,1)}) fusion(bf16[2048,4096]{1,0:T(8,128)(2,1)} %collective-permute-done, bf16[2048,4096]{1,0:T(8,128)(2,1)} %param.2, pred[]{:T(512)S(6)} %eq.3), kind=kLoop, calls=%fused_computation | loop fusion | flops 16777216 | bytes 67108864 | tf_op jit(solution)/shard_map/jit(_where)/select_n | solution.py:78
  387.1 1.3 copy-done.1
  388.4 25.5 %shard_map.28.rest_0_ = bf16[2048,14336]{1,0:T(8,128)(2,1)} custom-call(s32[1]{0:T(128)} %bitcast.core_ref, bf16[2048,4096]{1,0:T(8,128)(2,1)} %get-tuple-element.51.a0.a1, bf16[2048,4096]{1,0:T(8,128)(2,1)} %get-tuple-element.51.a0.a1, bf16[2048,4096]{1,0:T(8,128)(2,1)} %get-tuple-element.50.a2.a3, bf16[2048,4096]{1,0:T(8,128)(2,1)} %get-tuple-element.50.a2.a3, ...), custom_call_target="tpu_custom_call" | custom-call | flops 17179869184 | bytes 44040192 | tf_op jit(solution)/shard_map/pallas_call | solution.py:39
  413.9 0.0 collective-permute-start.13
  413.9 22.2 %fusion.2 = (bf16[2048,2560]{1,0:T(8,128)(2,1)}, bf16[2048,2560]{1,0:T(8,128)(2,1)}, bf16[2048,2560]{1,0:T(8,128)(2,1)}) fusion(bf16[2048,14336]{1,0:T(8,128)(2,1)} %b0.19), kind=kLoop, calls=%fused_computation.4 | loop fusion | bytes 62914560 | tf_op jit(solution)/shard_map/slice | solution.py:73
  436.2 1.7 collective-permute-start.9
  437.9 84.8 %shard_map.29.rest_0_ = bf16[2048,14336]{1,0:T(8,128)(2,1)} custom-call(s32[1]{0:T(128)} %bitcast.core_ref, bf16[2048,4096]{1,0:T(8,128)(2,1)} %get-tuple-element.51.a0.a1, bf16[2048,4096]{1,0:T(8,128)(2,1)} %get-tuple-element.51.a0.a1, bf16[2048,4096]{1,0:T(8,128)(2,1)} %get-tuple-element.50.a2.a3, ...), custom_call_target="tpu_custom_call", output_to_operand_aliasing={{}: (9, {})} | custom-call | flops 68719476736 | bytes 176160768 | tf_op jit(solution)/shard_map/pallas_call | solution.py:39
  522.7 141.6 %collective-permute-done.9.b2 = bf16[2048,2560]{1,0:T(8,128)(2,1)} collective-permute-done((bf16[2048,2560]{1,0:T(8,128)(2,1)}, bf16[2048,2560]{1,0:T(8,128)(2,1)}, u32[]{:S(2)}, u32[]{:S(2)}) %collective-permute-start.9) | collective-permute-done | bytes 10485792 | tf_op jit(solution)/shard_map/ppermute | solution.py:74
  664.3 1.7 collective-permute-start.8
  666.0 14.8 collective-permute-done.14.b3
  680.8 104.7 %shard_map.30.rest_0_ = bf16[2048,14336]{1,0:T(8,128)(2,1)} custom-call(s32[1]{0:T(128)} %bitcast.core_ref, bf16[2048,4096]{1,0:T(8,128)(2,1)} %get-tuple-element.51.a0.a1, bf16[2048,4096]{1,0:T(8,128)(2,1)} %get-tuple-element.51.a0.a1, bf16[2048,4096]{1,0:T(8,128)(2,1)} %get-tuple-element.50.a2.a3, ...), custom_call_target="tpu_custom_call", output_to_operand_aliasing={{}: (9, {})} | custom-call | flops 85899345920 | bytes 220200960 | tf_op jit(solution)/shard_map/pallas_call | solution.py:39
  785.5 106.9 %collective-permute-done.8.b2 = bf16[2048,2560]{1,0:T(8,128)(2,1)} collective-permute-done((bf16[2048,2560]{1,0:T(8,128)(2,1)}, bf16[2048,2560]{1,0:T(8,128)(2,1)}, u32[]{:S(2)}, u32[]{:S(2)}) %collective-permute-start.8) | collective-permute-done | bytes 10485792 | tf_op jit(solution)/shard_map/ppermute | solution.py:74
  892.4 1.7 collective-permute-start.7
  894.1 14.8 collective-permute-done.15.b3
  908.9 104.7 %shard_map.31.rest_0_ = bf16[2048,14336]{1,0:T(8,128)(2,1)} custom-call(s32[1]{0:T(128)} %bitcast.core_ref, bf16[2048,4096]{1,0:T(8,128)(2,1)} %get-tuple-element.51.a0.a1, bf16[2048,4096]{1,0:T(8,128)(2,1)} %get-tuple-element.51.a0.a1, bf16[2048,4096]{1,0:T(8,128)(2,1)} %get-tuple-element.50.a2.a3, ...), custom_call_target="tpu_custom_call", output_to_operand_aliasing={{}: (9, {})} | custom-call | flops 85899345920 | bytes 220200960 | tf_op jit(solution)/shard_map/pallas_call | solution.py:39
  1013.6 106.9 %collective-permute-done.7.b2 = bf16[2048,2560]{1,0:T(8,128)(2,1)} collective-permute-done((bf16[2048,2560]{1,0:T(8,128)(2,1)}, bf16[2048,2560]{1,0:T(8,128)(2,1)}, u32[]{:S(2)}, u32[]{:S(2)}) %collective-permute-start.7) | collective-permute-done | bytes 10485792 | tf_op jit(solution)/shard_map/ppermute | solution.py:74
  1120.5 1.7 collective-permute-start.6
  1122.2 14.8 collective-permute-done.16.b3
  1137.0 104.7 %shard_map.32.rest_0_ = bf16[2048,14336]{1,0:T(8,128)(2,1)} custom-call(s32[1]{0:T(128)} %bitcast.core_ref, bf16[2048,4096]{1,0:T(8,128)(2,1)} %get-tuple-element.51.a0.a1, bf16[2048,4096]{1,0:T(8,128)(2,1)} %get-tuple-element.51.a0.a1, bf16[2048,4096]{1,0:T(8,128)(2,1)} %get-tuple-element.50.a2.a3, ...), custom_call_target="tpu_custom_call", output_to_operand_aliasing={{}: (9, {})} | custom-call | flops 85899345920 | bytes 220200960 | tf_op jit(solution)/shard_map/pallas_call | solution.py:39
  1241.8 61.9 %collective-permute-done.6.b2 = bf16[2048,2048]{1,0:T(8,128)(2,1)} collective-permute-done((bf16[2048,2048]{1,0:T(8,128)(2,1)}, bf16[2048,2048]{1,0:T(8,128)(2,1)}, u32[]{:S(2)}, u32[]{:S(2)}) %collective-permute-start.6) | collective-permute-done | bytes 8388640 | tf_op jit(solution)/shard_map/ppermute | solution.py:74
  1303.7 4.7 slice.33
  1308.4 1.7 collective-permute-start.5
  1310.1 7.1 collective-permute-done.17.b3
  1317.2 84.7 %shard_map.33.rest_0_ = bf16[2048,14336]{1,0:T(8,128)(2,1)} custom-call(s32[1]{0:T(128)} %bitcast.core_ref, bf16[2048,4096]{1,0:T(8,128)(2,1)} %get-tuple-element.51.a0.a1, bf16[2048,4096]{1,0:T(8,128)(2,1)} %get-tuple-element.51.a0.a1, bf16[2048,4096]{1,0:T(8,128)(2,1)} %get-tuple-element.50.a2.a3, ...), custom_call_target="tpu_custom_call", output_to_operand_aliasing={{}: (9, {})} | custom-call | flops 68719476736 | bytes 176160768 | tf_op jit(solution)/shard_map/pallas_call | solution.py:39
  1402.0 0.2 collective-permute-start.18
  1402.1 1.7 collective-permute-start.4
  1403.8 5.7 collective-permute-done.18.b3
  1409.5 44.9 %shard_map.34.rest_0_ = bf16[2048,14336]{1,0:T(8,128)(2,1)} custom-call(s32[1]{0:T(128)} %bitcast.core_ref, bf16[2048,4096]{1,0:T(8,128)(2,1)} %get-tuple-element.51.a0.a1, bf16[2048,4096]{1,0:T(8,128)(2,1)} %get-tuple-element.51.a0.a1, bf16[2048,4096]{1,0:T(8,128)(2,1)} %get-tuple-element.50.a2.a3, ...), custom_call_target="tpu_custom_call", output_to_operand_aliasing={{}: (9, {})} | custom-call | flops 34359738368 | bytes 88080384 | tf_op jit(solution)/shard_map/pallas_call | solution.py:39
  1454.4 0.2 collective-permute-start.19
  1454.5 3.1 fusion.3
  1457.6 1.7 collective-permute-start.3
  1459.3 25.5 %shard_map.35.rest_0_ = bf16[2048,14336]{1,0:T(8,128)(2,1)} custom-call(s32[1]{0:T(128)} %bitcast.core_ref, bf16[2048,4096]{1,0:T(8,128)(2,1)} %get-tuple-element.51.a0.a1, bf16[2048,4096]{1,0:T(8,128)(2,1)} %get-tuple-element.51.a0.a1, bf16[2048,4096]{1,0:T(8,128)(2,1)} %get-tuple-element.50.a2.a3, ...), custom_call_target="tpu_custom_call", output_to_operand_aliasing={{}: (9, {})} | custom-call | flops 17179869184 | bytes 44040192 | tf_op jit(solution)/shard_map/pallas_call | solution.py:39
  1484.8 0.1 collective-permute-start.20
  1484.9 1.3 collective-permute-start.2
  1486.2 1.4 collective-permute-done.20.b3
  1487.6 16.9 %shard_map.36.rest_0_ = bf16[2048,14336]{1,0:T(8,128)(2,1)} custom-call(s32[1]{0:T(128)} %bitcast.core_ref, bf16[2048,4096]{1,0:T(8,128)(2,1)} %get-tuple-element.51.a0.a1, bf16[2048,4096]{1,0:T(8,128)(2,1)} %get-tuple-element.51.a0.a1, bf16[2048,4096]{1,0:T(8,128)(2,1)} %get-tuple-element.50.a2.a3, ...), custom_call_target="tpu_custom_call", output_to_operand_aliasing={{}: (9, {})} | custom-call | flops 8589934592 | bytes 38797312 | tf_op jit(solution)/shard_map/pallas_call | solution.py:39
  1504.5 6.2 collective-permute-done.2.b2
  1510.7 2.9 collective-permute-done.21.b3
  1513.6 1.0 copy-done.3
  1514.6 16.9 %shard_map.37 = bf16[2048,14336]{1,0:T(8,128)(2,1)} custom-call(s32[1]{0:T(128)} %bitcast.core_ref, bf16[2048,4096]{1,0:T(8,128)(2,1)} %get-tuple-element.51.a0.a1, bf16[2048,4096]{1,0:T(8,128)(2,1)} %get-tuple-element.51.a0.a1, bf16[2048,4096]{1,0:T(8,128)(2,1)} %get-tuple-element.50.a2.a3, ...), custom_call_target="tpu_custom_call", output_to_operand_aliasing={{}: (9, {})} | custom-call | flops 8589934592 | bytes 38797312 | tf_op jit(solution)/shard_map/pallas_call | solution.py:39
  (20 shorter events, 0.0 us)
Async XLA Ops:
  0.0 388.4 %collective-permute-start.1 = (bf16[2048,14336]{1,0:T(8,128)(2,1)}, bf16[2048,14336]{1,0:T(8,128)(2,1)}, u32[]{:S(2)}, u32[]{:S(2)}) collective-permute-start(bf16[2048,14336]{1,0:T(8,128)(2,1)} %b0.19), channel_id=1, source_target_pairs={{0,1},{1,0},{2,3},{3,2},{4,5},{5,4},{6,7},{7,6}} | collective-permute-start | bytes 176160768 | tf_op jit(solution)/shard_map/ppermute | solution.py:76
  0.8 363.7 %collective-permute-start = (bf16[2048,4096]{1,0:T(8,128)(2,1)}, bf16[2048,4096]{1,0:T(8,128)(2,1)}, u32[]{:S(2)}, u32[]{:S(2)}) collective-permute-start(bf16[2048,4096]{1,0:T(8,128)(2,1)} %param.2), channel_id=1, source_target_pairs={{0,4},{4,0},{1,5},{5,1},{2,6},{6,2},{3,7},{7,3}} | collective-permute-start | bytes 50331656 | tf_op jit(solution)/shard_map/ppermute | solution.py:75
  15.2 398.7 %collective-permute-start.10 = (bf16[2048,2048]{1,0:T(8,128)(2,1)}, bf16[2048,2048]{1,0:T(8,128)(2,1)}, u32[]{:S(2)}, u32[]{:S(2)}) collective-permute-start(bf16[2048,2048]{1,0:T(8,128)(2,1)} %get-tuple-element.43), channel_id=1, source_target_pairs={{0,2},{2,0},{1,3},{3,1},{4,6},{6,4},{5,7},{7,5}} | collective-permute-start | bytes 25165832 | tf_op jit(solution)/shard_map/ppermute | solution.py:74
  21.3 221.7 %collective-permute-start.11 = (bf16[2048,512]{1,0:T(8,128)(2,1)}, bf16[2048,512]{1,0:T(8,128)(2,1)S(1)}, u32[]{:S(2)}, u32[]{:S(2)}) collective-permute-start(bf16[2048,512]{1,0:T(8,128)(2,1)} %get-tuple-element.41), channel_id=1, source_target_pairs={{0,2},{2,0},{1,3},{3,1},{4,6},{6,4},{5,7},{7,5}} | collective-permute-start | bytes 6291464 | tf_op jit(solution)/shard_map/ppermute | solution.py:74
  243.0 144.1 %copy-start = (bf16[2048,512]{1,0:T(8,128)(2,1)}, bf16[2048,512]{1,0:T(8,128)(2,1)S(1)}, u32[]{:S(2)}) copy-start(bf16[2048,512]{1,0:T(8,128)(2,1)S(1)} %collective-permute-done.11.b2) | copy-start | bytes 6291460
  243.0 144.1 %collective-permute-start.12 = (bf16[2048,512]{1,0:T(8,128)(2,1)S(1)}, bf16[2048,512]{1,0:T(8,128)(2,1)S(1)}, u32[]{:S(2)}, u32[]{:S(2)}) collective-permute-start(bf16[2048,512]{1,0:T(8,128)(2,1)S(1)} %collective-permute-done.11.b2), channel_id=1, source_target_pairs={{0,1},{1,0},{2,3},{3,2},{4,5},{5,4},{6,7},{7,6}} | collective-permute-start | bytes 6291464 | tf_op jit(solution)/shard_map/ppermute | solution.py:84
  387.1 1.3 copy-start.1
  413.9 24.0 %collective-permute-start.13 = (bf16[2048,2048]{1,0:T(8,128)(2,1)}, bf16[2048,2048]{1,0:T(8,128)(2,1)}, u32[]{:S(2)}, u32[]{:S(2)}) collective-permute-start(bf16[2048,2048]{1,0:T(8,128)(2,1)} %collective-permute-done.10.b2), channel_id=1, source_target_pairs={{0,1},{1,0},{2,3},{3,2},{4,5},{5,4},{6,7},{7,6}} | collective-permute-start | bytes 25165832 | tf_op jit(solution)/shard_map/ppermute | solution.py:84
  436.2 228.1 %collective-permute-start.9 = (bf16[2048,2560]{1,0:T(8,128)(2,1)}, bf16[2048,2560]{1,0:T(8,128)(2,1)}, u32[]{:S(2)}, u32[]{:S(2)}) collective-permute-start(bf16[2048,2560]{1,0:T(8,128)(2,1)} %get-tuple-element.45), channel_id=1, source_target_pairs={{0,2},{2,0},{1,3},{3,1},{4,6},{6,4},{5,7},{7,5}} | collective-permute-start | bytes 31457288 | tf_op jit(solution)/shard_map/ppermute | solution.py:74
  664.3 16.5 %collective-permute-start.14 = (bf16[2048,2560]{1,0:T(8,128)(2,1)}, bf16[2048,2560]{1,0:T(8,128)(2,1)}, u32[]{:S(2)}, u32[]{:S(2)}) collective-permute-start(bf16[2048,2560]{1,0:T(8,128)(2,1)} %collective-permute-done.9.b2), channel_id=1, source_target_pairs={{0,1},{1,0},{2,3},{3,2},{4,5},{5,4},{6,7},{7,6}} | collective-permute-start | bytes 31457288 | tf_op jit(solution)/shard_map/ppermute | solution.py:84
  664.3 228.1 %collective-permute-start.8 = (bf16[2048,2560]{1,0:T(8,128)(2,1)}, bf16[2048,2560]{1,0:T(8,128)(2,1)}, u32[]{:S(2)}, u32[]{:S(2)}) collective-permute-start(bf16[2048,2560]{1,0:T(8,128)(2,1)} %get-tuple-element.46), channel_id=1, source_target_pairs={{0,2},{2,0},{1,3},{3,1},{4,6},{6,4},{5,7},{7,5}} | collective-permute-start | bytes 31457288 | tf_op jit(solution)/shard_map/ppermute | solution.py:74
  892.4 16.5 %collective-permute-start.15 = (bf16[2048,2560]{1,0:T(8,128)(2,1)}, bf16[2048,2560]{1,0:T(8,128)(2,1)}, u32[]{:S(2)}, u32[]{:S(2)}) collective-permute-start(bf16[2048,2560]{1,0:T(8,128)(2,1)} %collective-permute-done.8.b2), channel_id=1, source_target_pairs={{0,1},{1,0},{2,3},{3,2},{4,5},{5,4},{6,7},{7,6}} | collective-permute-start | bytes 31457288 | tf_op jit(solution)/shard_map/ppermute | solution.py:84
  892.4 228.1 %collective-permute-start.7 = (bf16[2048,2560]{1,0:T(8,128)(2,1)}, bf16[2048,2560]{1,0:T(8,128)(2,1)}, u32[]{:S(2)}, u32[]{:S(2)}) collective-permute-start(bf16[2048,2560]{1,0:T(8,128)(2,1)} %get-tuple-element.47), channel_id=1, source_target_pairs={{0,2},{2,0},{1,3},{3,1},{4,6},{6,4},{5,7},{7,5}} | collective-permute-start | bytes 31457288 | tf_op jit(solution)/shard_map/ppermute | solution.py:74
  1120.5 16.5 %collective-permute-start.16 = (bf16[2048,2560]{1,0:T(8,128)(2,1)}, bf16[2048,2560]{1,0:T(8,128)(2,1)}, u32[]{:S(2)}, u32[]{:S(2)}) collective-permute-start(bf16[2048,2560]{1,0:T(8,128)(2,1)} %collective-permute-done.7.b2), channel_id=1, source_target_pairs={{0,1},{1,0},{2,3},{3,2},{4,5},{5,4},{6,7},{7,6}} | collective-permute-start | bytes 31457288 | tf_op jit(solution)/shard_map/ppermute | solution.py:84
  1120.5 183.2 %collective-permute-start.6 = (bf16[2048,2048]{1,0:T(8,128)(2,1)}, bf16[2048,2048]{1,0:T(8,128)(2,1)}, u32[]{:S(2)}, u32[]{:S(2)}) collective-permute-start(bf16[2048,2048]{1,0:T(8,128)(2,1)} %get-tuple-element.44), channel_id=1, source_target_pairs={{0,2},{2,0},{1,3},{3,1},{4,6},{6,4},{5,7},{7,5}} | collective-permute-start | bytes 25165832 | tf_op jit(solution)/shard_map/ppermute | solution.py:74
  1303.7 13.5 collective-permute-start.17
  1308.4 93.6 %collective-permute-start.5 = (bf16[2048,1024]{1,0:T(8,128)(2,1)}, bf16[2048,1024]{1,0:T(8,128)(2,1)}, u32[]{:S(2)}, u32[]{:S(2)}) collective-permute-start(bf16[2048,1024]{1,0:T(8,128)(2,1)} %slice.33), channel_id=1, source_target_pairs={{0,2},{2,0},{1,3},{3,1},{4,6},{6,4},{5,7},{7,5}} | collective-permute-start | bytes 12582920 | tf_op jit(solution)/shard_map/ppermute | solution.py:74
  1402.0 7.5 collective-permute-start.18
  1402.1 52.2 %collective-permute-start.4 = (bf16[2048,512]{1,0:T(8,128)(2,1)}, bf16[2048,512]{1,0:T(8,128)(2,1)}, u32[]{:S(2)}, u32[]{:S(2)}) collective-permute-start(bf16[2048,512]{1,0:T(8,128)(2,1)} %get-tuple-element.42), channel_id=1, source_target_pairs={{0,2},{2,0},{1,3},{3,1},{4,6},{6,4},{5,7},{7,5}} | collective-permute-start | bytes 6291464 | tf_op jit(solution)/shard_map/ppermute | solution.py:74
  1454.4 5.0 collective-permute-start.19
  1457.6 27.2 %collective-permute-start.3 = (bf16[2048,256]{1,0:T(8,128)(2,1)}, bf16[2048,256]{1,0:T(8,128)(2,1)S(1)}, u32[]{:S(2)}, u32[]{:S(2)}) collective-permute-start(bf16[2048,256]{1,0:T(8,128)(2,1)} %get-tuple-element.48), channel_id=1, source_target_pairs={{0,2},{2,0},{1,3},{3,1},{4,6},{6,4},{5,7},{7,5}} | collective-permute-start | bytes 3145736 | tf_op jit(solution)/shard_map/ppermute | solution.py:74
  1484.8 2.8 copy-start.2
  1484.8 2.8 collective-permute-start.20
  1484.9 25.8 %collective-permute-start.2 = (bf16[2048,256]{1,0:T(8,128)(2,1)}, bf16[2048,256]{1,0:T(8,128)(2,1)}, u32[]{:S(2)}, u32[]{:S(2)}) collective-permute-start(bf16[2048,256]{1,0:T(8,128)(2,1)} %get-tuple-element.49), channel_id=1, source_target_pairs={{0,2},{2,0},{1,3},{3,1},{4,6},{6,4},{5,7},{7,5}} | collective-permute-start | bytes 3145736 | tf_op jit(solution)/shard_map/ppermute | solution.py:74
  1510.7 2.9 collective-permute-start.21
  1513.6 1.0 copy-start.3

commit v2 on v1

v2 whole, which is shorter than its diff:
```python
import jax
import jax.numpy as jnp
from jax import lax
from jax.experimental import pallas as pl
from jax.experimental.pallas import tpu as pltpu
from jax.sharding import PartitionSpec as P


PIECES = (
    (128, 0, 1), (896, 0, 1), (2560, 0, 1), (2560, 0, 1), (2560, 0, 1), (2048, 0, 1), (1536, 0, 1),
    (1024, 0, 1), (512, 0, 1), (256, 0, 1), (256, 0, 2), (256, 1, 2),
)
TAIL = 7
NEAR_AFTER = 4
MIB = 1024 * 1024


def matmul_cost(rows, depth, width, tiles):
    return pl.CostEstimate(
        flops=2 * rows * depth * width,
        bytes_accessed=2 * (rows * depth * tiles + depth * width + rows * width),
        transcendentals=0,
    )


def whole_body(core_ref, a0, a1, a2, a3, b0, b1, b2, b3, *rest):
    c_ref = rest[-1]
    total = jnp.dot(a0[...], b0[...], preferred_element_type=jnp.float32)
    total += jnp.dot(a1[...], b1[...], preferred_element_type=jnp.float32)
    total += jnp.dot(a2[...], b2[...], preferred_element_type=jnp.float32)
    total += jnp.dot(a3[...], b3[...], preferred_element_type=jnp.float32)
    c_ref[...] = total.astype(c_ref.dtype)


def tile_of(start, width):
    for tn in (512, 256, 128):
        if start % tn == 0 and width % tn == 0:
            return tn


def whole_product(core, a_near, a_far, b_own, b_pair, x_own, x_pair, c_prev, start, tm=512):
    rows = a_near.shape[0]
    depth, columns = b_own.shape
    width = x_own.shape[1]
    tn = tile_of(start, width)
    first = start // tn
    a_mine = pl.BlockSpec((tm, depth), lambda n, m, core: (m, core[0]))
    a_other = pl.BlockSpec((tm, depth), lambda n, m, core: (m, 1 - core[0]))
    b_whole = pl.BlockSpec((depth, tn), lambda n, m, core: (0, first + n))
    b_piece = pl.BlockSpec((depth, tn), lambda n, m, core: (0, n))
    in_specs = [a_mine, a_other, a_mine, a_other, b_whole, b_whole, b_piece, b_piece]
    args = [a_near, a_near, a_far, a_far, b_own, b_pair, x_own, x_pair]
    aliases = {}
    if c_prev is not None:
        in_specs.append(pl.BlockSpec(memory_space=pl.ANY))
        aliases = {1 + len(args): 0}
        args.append(c_prev)
    return pl.pallas_call(
        whole_body,
        grid_spec=pltpu.PrefetchScalarGridSpec(
            num_scalar_prefetch=1,
            grid=(width // tn, rows // tm),
            in_specs=in_specs,
            out_specs=pl.BlockSpec((tm, tn), lambda n, m, core: (m, first + n)),
        ),
        out_shape=jax.ShapeDtypeStruct((rows, columns), jnp.bfloat16),
        input_output_aliases=aliases,
        cost_estimate=matmul_cost(rows, 4 * depth, width, width // tn),
        compiler_params=pltpu.CompilerParams(vmem_limit_bytes=62 * MIB),
    )(core, *args)


def near_body(core_ref, a0, a1, b0, b1, s_ref):
    s_ref[...] = jnp.dot(a0[...], b0[...], preferred_element_type=jnp.float32)
    s_ref[...] += jnp.dot(a1[...], b1[...], preferred_element_type=jnp.float32)


def near_sums(core, a_near, b_own, b_pair, start, tm=512, tn=512):
    rows = a_near.shape[0]
    depth, columns = b_own.shape
    width = columns - start
    first = start // tn
    b_whole = pl.BlockSpec((depth, tn), lambda n, m, core: (0, first + n))
    return pl.pallas_call(
        near_body,
        grid_spec=pltpu.PrefetchScalarGridSpec(
            num_scalar_prefetch=1,
            grid=(width // tn, rows // tm),
            in_specs=[
                pl.BlockSpec((tm, depth), lambda n, m, core: (m, core[0])),
                pl.BlockSpec((tm, depth), lambda n, m, core: (m, 1 - core[0])),
                b_whole,
                b_whole,
            ],
            out_specs=pl.BlockSpec((tm, tn), lambda n, m, core: (m, n)),
        ),
        out_shape=jax.ShapeDtypeStruct((rows, width), jnp.float32),
        cost_estimate=matmul_cost(rows, 2 * depth, width, width // tn),
        compiler_params=pltpu.CompilerParams(vmem_limit_bytes=62 * MIB),
        name="near",
    )(core, a_near, a_near, b_own, b_pair)


def far_body(core_ref, a0, a1, b0, b1, s_ref, *rest):
    out_ref = rest[-1]
    total = s_ref[...]
    total += jnp.dot(a0[...], b0[...], preferred_element_type=jnp.float32)
    total += jnp.dot(a1[...], b1[...], preferred_element_type=jnp.float32)
    out_ref[...] = total.astype(out_ref.dtype)


def far_product(core, a_far, x_own, x_pair, sums, sums_start, part, parts, c_prev, start, tm=256):
    rows = a_far.shape[0]
    depth, width = x_own.shape
    tn = tile_of(start, width)
    first = start // tn
    sums_first = sums_start // tn
    a_mine = pl.BlockSpec((tm, depth), lambda n, m, core: (m, core[0] * parts + part))
    a_other = pl.BlockSpec((tm, depth), lambda n, m, core: (m, (1 - core[0]) * parts + part))
    b_piece = pl.BlockSpec((depth, tn), lambda n, m, core: (0, n))
    in_specs = [
        a_mine, a_other, b_piece, b_piece, pl.BlockSpec((tm, tn), lambda n, m, core: (m, sums_first + n)),
    ]
    args = [a_far, a_far, x_own, x_pair, sums]
    if c_prev is None:
        out_specs = pl.BlockSpec((tm, tn), lambda n, m, core: (m, n))
        out_shape = jax.ShapeDtypeStruct((rows, width), jnp.float32)
        aliases = {}
    else:
        in_specs.append(pl.BlockSpec(memory_space=pl.ANY))
        aliases = {1 + len(args): 0}
        args.append(c_prev)
        out_specs = pl.BlockSpec((tm, tn), lambda n, m, core: (m, first + n))
        out_shape = jax.ShapeDtypeStruct(c_prev.shape, c_prev.dtype)
    return pl.pallas_call(
        far_body,
        grid_spec=pltpu.PrefetchScalarGridSpec(
            num_scalar_prefetch=1,
            grid=(width // tn, rows // tm),
            in_specs=in_specs,
            out_specs=out_specs,
        ),
        out_shape=out_shape,
        input_output_aliases=aliases,
        cost_estimate=matmul_cost(rows, 2 * depth, width, width // tn),
        compiler_params=pltpu.CompilerParams(vmem_limit_bytes=FAR_VMEM * MIB),
    )(core, *args)


FAR_VMEM = 28


def solution(mesh):
    across = [(0, 2), (2, 0), (1, 3), (3, 1)]
    beside = [(0, 1), (1, 0), (2, 3), (3, 2)]

    def local_product(a_blk, b_blk):
        depth = b_blk.shape[0]
        row_id = lax.axis_index("row")
        core = lax.rem(row_id, 2).astype(jnp.int32).reshape(1)
        aligned = lax.div(row_id, 2) == lax.axis_index("col")
        starts = []
        x_own = []
        begin = 0
        for width, part, parts in PIECES:
            starts.append(begin)
            rows = depth // parts
            piece = lax.slice(b_blk, (part * rows, begin), ((part + 1) * rows, begin + width))
            x_own.append(lax.ppermute(piece, "row", across))
            if part == parts - 1:
                begin += width
        a_recv = lax.ppermute(a_blk, "col", [(0, 1), (1, 0)])
        b_pair = lax.ppermute(b_blk, "row", beside)
        a_near = jnp.where(aligned, a_blk, a_recv)
        a_far = jnp.where(aligned, a_recv, a_blk)
        c = None
        half = None
        for j, (width, part, parts) in enumerate(PIECES):
            x = x_own[j]
            if half is not None:
                x, half = lax.optimization_barrier((x, half))
            elif j:
                x, c = lax.optimization_barrier((x, c))
            x_pair = lax.ppermute(x, "row", beside)
            if j < TAIL:
                c = whole_product(core, a_near, a_far, b_blk, b_pair, x, x_pair, c, starts[j])
            elif part < parts - 1:
                half = far_product(core, a_far, x, x_pair, sums, starts[j] - starts[TAIL], part, parts, None, starts[j])
            elif half is not None:
                c = far_product(core, a_far, x, x_pair, half, 0, part, parts, c, starts[j])
                half = None
            else:
                c = far_product(core, a_far, x, x_pair, sums, starts[j] - starts[TAIL], part, parts, c, starts[j])
            if j == NEAR_AFTER:
                core, c = lax.optimization_barrier((core, c))
                sums = near_sums(core, a_near, b_blk, b_pair, starts[TAIL])
        return c

    return jax.shard_map(
        local_product,
        mesh=mesh,
        in_specs=(P(("dp", "row"), "col"), P("row", "col")),
        out_specs=P(("dp", "row"), "col"),
        check_vma=False,
    )
```

time: 1530 us -> 1540 us (level)
  Pallas kernels: 613 us -> 680 us
  waiting for transfers between devices: 828 us -> 761 us
    ppermute x10 -> x12, waiting for transfers between devices: 645 us -> 371 us  [local_product(): x_own.append(lax.ppermute(piece, 'row', across))]
    ppermute x1, waiting for transfers between devices: 122 us -> 330 us  [local_product(): a_recv = lax.ppermute(a_blk, 'col', [(0, 1), (1, 0)])]
    pallas_call x10 -> x13, Pallas kernels: 613 us -> 680 us  [the longest x7 570 us: whole_product(): pl.pallas_call(whole_body, grid_spec=pltpu.PrefetchScalarGridSpec(num_sca...]
    slice x5 -> x9, local copies, waits for them, and re-layouts: 46.4 us -> 51.7 us  [local_product(): lax.slice(b_blk, (part * rows, begin), ((part + 1) * rows, begin + width))]
    ppermute x10 -> x12, waiting for transfers between devices: 61.4 us -> 59.9 us  [local_product(): x_pair = lax.ppermute(x, 'row', beside)]
  transfers between devices with their start and end apart: 22 -> 26, of which waited for: 14 -> 19; matrix products, arithmetic and copies ran while one was open for 5% -> 5% of each run, Pallas kernels for 39% -> 44%
where the time goes in v2:
time: 1540 us
  waiting for transfers between devices  761 us (49%)
  Pallas kernels  680 us (44%)
  local copies, waits for them, and re-layouts  58.3 us (4%)
  other arithmetic  22.6 us (1%)
  starting transfers between devices  18.6 us (1%)
    pallas_call x7, Pallas kernels, whole_product(): pl.pallas_call(whole_body, grid_spec=pltpu.PrefetchScalarGridSpec(num_sca...  570 us
    ppermute x12, waiting for transfers between devices, local_product(): x_own.append(lax.ppermute(piece, 'row', across))  371 us
    ppermute x1, waiting for transfers between devices, local_product(): a_recv = lax.ppermute(a_blk, 'col', [(0, 1), (1, 0)])  330 us
    pallas_call x5, Pallas kernels, far_product(): pl.pallas_call(far_body, grid_spec=pltpu.PrefetchScalarGridSpec(num_scala...  61.2 us
    ppermute x12, waiting for transfers between devices, local_product(): x_pair = lax.ppermute(x, 'row', beside)  59.9 us
    slice x9, local copies, waits for them, and re-layouts, local_product(): lax.slice(b_blk, (part * rows, begin), ((part + 1) * rows, begin + width))  51.7 us
    pallas_call x1, Pallas kernels, near_sums(): pl.pallas_call(near_body, grid_spec=pltpu.PrefetchScalarGridSpec(num_scal...  48.7 us
  transfers between devices with their start and end apart: 26, of which 19 were waited for; matrix products, arithmetic and copies ran while one was open for 5% of the time, Pallas kernels for 44%

profile of v2, /device:TPU:0, one launch (start us, length us, event | category | flops | bytes accessed | tf_op | source)
XLA Modules:
  0.0 1540.6 jit_solution(2233956963880367680)
XLA Ops:
  0.8 2.5 collective-permute-start
  4.4 1.5 collective-permute-start.6
  5.9 22.2 %fusion.1 = (bf16[2048,2560]{1,0:T(8,128)(2,1)}, bf16[2048,2560]{1,0:T(8,128)(2,1)}, bf16[2048,2560]{1,0:T(8,128)(2,1)}) fusion(bf16[2048,14336]{1,0:T(8,128)(2,1)} %b0.15), kind=kLoop, calls=%fused_computation.3 | loop fusion | bytes 62914560 | tf_op jit(solution)/shard_map/slice | solution.py:168
  28.7 4.1 slice.39
  32.8 1.5 collective-permute-start.5
  34.4 330.2 %collective-permute-done = bf16[2048,4096]{1,0:T(8,128)(2,1)} collective-permute-done((bf16[2048,4096]{1,0:T(8,128)(2,1)}, bf16[2048,4096]{1,0:T(8,128)(2,1)}, u32[]{:S(2)}, u32[]{:S(2)}) %collective-permute-start) | collective-permute-done | bytes 16777248 | tf_op jit(solution)/shard_map/ppermute | solution.py:172
  364.5 22.6 %broadcast_select_fusion = (bf16[2048,4096]{1,0:T(8,128)(2,1)}, bf16[2048,4096]{1,0:T(8,128)(2,1)}) fusion(bf16[2048,4096]{1,0:T(8,128)(2,1)} %collective-permute-done, bf16[2048,4096]{1,0:T(8,128)(2,1)} %param.2, pred[]{:T(512)S(6)} %eq.3), kind=kLoop, calls=%fused_computation | loop fusion | flops 16777216 | bytes 67108864 | tf_op jit(solution)/shard_map/jit(_where)/select_n | solution.py:175
  388.0 16.1 %shard_map.28.rest_0_ = bf16[2048,14336]{1,0:T(8,128)(2,1)} custom-call(s32[1]{0:T(128)} %bitcast.core_ref, bf16[2048,4096]{1,0:T(8,128)(2,1)} %get-tuple-element.59.a0.a1, bf16[2048,4096]{1,0:T(8,128)(2,1)} %get-tuple-element.59.a0.a1, bf16[2048,4096]{1,0:T(8,128)(2,1)} %get-tuple-element.58.a2.a3.a0.a1, bf16[2048,4096]{1,0:T(8,128)(2,1)} %get-tuple-element.58.a2.a3.a0.a1, ...), custom_call_target="tpu_custom_call" | custom-call | flops 4294967296 | bytes 36175872 | tf_op jit(solution)/shard_map/pallas_call | solution.py:58
  404.1 6.7 collective-permute-done.8.b3
  410.8 90.0 %shard_map.29.rest_0_ = bf16[2048,14336]{1,0:T(8,128)(2,1)} custom-call(s32[1]{0:T(128)} %bitcast.core_ref, bf16[2048,4096]{1,0:T(8,128)(2,1)} %get-tuple-element.59.a0.a1, bf16[2048,4096]{1,0:T(8,128)(2,1)} %get-tuple-element.59.a0.a1, bf16[2048,4096]{1,0:T(8,128)(2,1)} %get-tuple-element.58.a2.a3.a0.a1, ...), custom_call_target="tpu_custom_call", output_to_operand_aliasing={{}: (9, {})} | custom-call | flops 30064771072 | bytes 253231104 | tf_op jit(solution)/shard_map/pallas_call | solution.py:58
  500.9 1.7 collective-permute-start.3
  502.7 14.7 collective-permute-done.9.b3
  517.3 104.7 %shard_map.30.rest_0_ = bf16[2048,14336]{1,0:T(8,128)(2,1)} custom-call(s32[1]{0:T(128)} %bitcast.core_ref, bf16[2048,4096]{1,0:T(8,128)(2,1)} %get-tuple-element.59.a0.a1, bf16[2048,4096]{1,0:T(8,128)(2,1)} %get-tuple-element.59.a0.a1, bf16[2048,4096]{1,0:T(8,128)(2,1)} %get-tuple-element.58.a2.a3.a0.a1, ...), custom_call_target="tpu_custom_call", output_to_operand_aliasing={{}: (9, {})} | custom-call | flops 85899345920 | bytes 220200960 | tf_op jit(solution)/shard_map/pallas_call | solution.py:58
  622.0 106.9 %collective-permute-done.3.b2 = bf16[2048,2560]{1,0:T(8,128)(2,1)} collective-permute-done((bf16[2048,2560]{1,0:T(8,128)(2,1)}, bf16[2048,2560]{1,0:T(8,128)(2,1)}, u32[]{:S(2)}, u32[]{:S(2)}) %collective-permute-start.3) | collective-permute-done | bytes 10485792 | tf_op jit(solution)/shard_map/ppermute | solution.py:169
  728.9 1.7 collective-permute-start.2
  730.7 14.8 collective-permute-done.10.b3
  745.4 104.7 %shard_map.31.rest_0_ = bf16[2048,14336]{1,0:T(8,128)(2,1)} custom-call(s32[1]{0:T(128)} %bitcast.core_ref, bf16[2048,4096]{1,0:T(8,128)(2,1)} %get-tuple-element.59.a0.a1, bf16[2048,4096]{1,0:T(8,128)(2,1)} %get-tuple-element.59.a0.a1, bf16[2048,4096]{1,0:T(8,128)(2,1)} %get-tuple-element.58.a2.a3.a0.a1, ...), custom_call_target="tpu_custom_call", output_to_operand_aliasing={{}: (9, {})} | custom-call | flops 85899345920 | bytes 220200960 | tf_op jit(solution)/shard_map/pallas_call | solution.py:58
  850.2 106.9 %collective-permute-done.2.b2 = bf16[2048,2560]{1,0:T(8,128)(2,1)} collective-permute-done((bf16[2048,2560]{1,0:T(8,128)(2,1)}, bf16[2048,2560]{1,0:T(8,128)(2,1)}, u32[]{:S(2)}, u32[]{:S(2)}) %collective-permute-start.2) | collective-permute-done | bytes 10485792 | tf_op jit(solution)/shard_map/ppermute | solution.py:169
  957.1 8.3 slice.47
  965.4 1.7 collective-permute-start.18
  967.1 6.5 collective-permute-done.11.b3
  973.6 104.7 %shard_map.32.rest_0_ = bf16[2048,14336]{1,0:T(8,128)(2,1)} custom-call(s32[1]{0:T(128)} %bitcast.core_ref, bf16[2048,4096]{1,0:T(8,128)(2,1)} %get-tuple-element.59.a0.a1, bf16[2048,4096]{1,0:T(8,128)(2,1)} %get-tuple-element.59.a0.a1, bf16[2048,4096]{1,0:T(8,128)(2,1)} %get-tuple-element.58.a2.a3.a0.a1, ...), custom_call_target="tpu_custom_call", output_to_operand_aliasing={{}: (9, {})} | custom-call | flops 85899345920 | bytes 220200960 | tf_op jit(solution)/shard_map/pallas_call | solution.py:58
  1078.3 70.3 %collective-permute-done.18.b2 = bf16[2048,2048]{1,0:T(8,128)(2,1)} collective-permute-done((bf16[2048,2048]{1,0:T(8,128)(2,1)}, bf16[2048,2048]{1,0:T(8,128)(2,1)}, u32[]{:S(2)}, u32[]{:S(2)}) %collective-permute-start.18) | collective-permute-done | bytes 8388640 | tf_op jit(solution)/shard_map/ppermute | solution.py:169
  1148.5 5.8 slice.46
  1154.3 1.7 collective-permute-start.17
  1156.0 6.0 collective-permute-done.19.b3
  1162.0 84.7 %shard_map.33.rest_0_ = bf16[2048,14336]{1,0:T(8,128)(2,1)} custom-call(s32[1]{0:T(128)} %bitcast.core_ref, bf16[2048,4096]{1,0:T(8,128)(2,1)} %get-tuple-element.59.a0.a1, bf16[2048,4096]{1,0:T(8,128)(2,1)} %get-tuple-element.59.a0.a1, bf16[2048,4096]{1,0:T(8,128)(2,1)} %get-tuple-element.58.a2.a3.a0.a1, ...), custom_call_target="tpu_custom_call", output_to_operand_aliasing={{}: (9, {})} | custom-call | flops 68719476736 | bytes 176160768 | tf_op jit(solution)/shard_map/pallas_call | solution.py:58
  1246.8 45.8 %collective-permute-done.17.b2 = bf16[2048,1536]{1,0:T(8,128)(2,1)} collective-permute-done((bf16[2048,1536]{1,0:T(8,128)(2,1)}, bf16[2048,1536]{1,0:T(8,128)(2,1)}, u32[]{:S(2)}, u32[]{:S(2)}) %collective-permute-start.17) | collective-permute-done | bytes 6291488 | tf_op jit(solution)/shard_map/ppermute | solution.py:169
  1292.6 4.6 slice.45
  1297.2 1.7 collective-permute-start.16
  1298.9 4.2 collective-permute-done.20.b3
  1303.1 64.8 %shard_map.34.rest_0_ = bf16[2048,14336]{1,0:T(8,128)(2,1)} custom-call(s32[1]{0:T(128)} %bitcast.core_ref, bf16[2048,4096]{1,0:T(8,128)(2,1)} %get-tuple-element.59.a0.a1, bf16[2048,4096]{1,0:T(8,128)(2,1)} %get-tuple-element.59.a0.a1, bf16[2048,4096]{1,0:T(8,128)(2,1)} %get-tuple-element.58.a2.a3.a0.a1, ...), custom_call_target="tpu_custom_call", output_to_operand_aliasing={{}: (9, {})} | custom-call | flops 51539607552 | bytes 132120576 | tf_op jit(solution)/shard_map/pallas_call | solution.py:58
  1367.9 22.6 %collective-permute-done.16.b0 = bf16[2048,1024]{1,0:T(8,128)(2,1)} collective-permute-done((bf16[2048,1024]{1,0:T(8,128)(2,1)}, bf16[2048,1024]{1,0:T(8,128)(2,1)}, u32[]{:S(2)}, u32[]{:S(2)}) %collective-permute-start.16) | collective-permute-done | bytes 4194336 | tf_op jit(solution)/shard_map/ppermute | solution.py:169
  1390.5 3.0 slice.44
  1393.5 1.7 collective-permute-start.15
  1395.2 48.7 %near.1.s_ref = f32[2048,2048]{1,0:T(8,128)} custom-call(s32[1]{0:T(128)} %bitcast.core_ref, bf16[2048,4096]{1,0:T(8,128)(2,1)} %get-tuple-element.59.a0.a1, bf16[2048,4096]{1,0:T(8,128)(2,1)} %get-tuple-element.59.a0.a1, bf16[2048,14336]{1,0:T(8,128)(2,1)} %b0.15, bf16[2048,14336]{1,0:T(8,128)(2,1)} %collective-permute-done.1.b1), custom_call_target="tpu_custom_call" | custom-call | flops 34359738368 | bytes 92274688 | tf_op jit(solution)/shard_map/near/pallas_call | solution.py:84
  1443.9 5.8 copy-done
  1449.7 26.9 %shard_map.35.rest_0_ = bf16[2048,14336]{1,0:T(8,128)(2,1)} custom-call(s32[1]{0:T(128)} %bitcast.core_ref, bf16[2048,4096]{1,0:T(8,128)(2,1)S(1)} %copy-done, bf16[2048,4096]{1,0:T(8,128)(2,1)S(1)} %copy-done, bf16[2048,1024]{1,0:T(8,128)(2,1)} %collective-permute-done.16.b0, ...), custom_call_target="tpu_custom_call", output_to_operand_aliasing={{}: (6, {})} | custom-call | flops 17179869184 | bytes 46137344 | tf_op jit(solution)/shard_map/pallas_call | solution.py:135
  1478.4 2.5 collective-permute-done.22.b1
  1481.0 13.7 shard_map.36.rest_0_
  1494.7 8.8 collective-permute-done.14.b0
  1506.2 8.9 shard_map.37.rest_0_
  1515.0 4.1 collective-permute-done.13.b0
  1519.4 1.6 collective-permute-done.24.b1
  1521.0 6.5 shard_map.38.s_ref
  1527.6 5.9 collective-permute-done.12.b0
  1533.5 1.9 collective-permute-done.25.b1
  1535.4 5.2 shard_map.39
  (33 shorter events, 8.3 us)
Async XLA Ops:
  0.0 387.1 %collective-permute-start.1 = (bf16[2048,14336]{1,0:T(8,128)(2,1)}, bf16[2048,14336]{1,0:T(8,128)(2,1)}, u32[]{:S(2)}, u32[]{:S(2)}) collective-permute-start(bf16[2048,14336]{1,0:T(8,128)(2,1)} %b0.15), channel_id=1, source_target_pairs={{0,1},{1,0},{2,3},{3,2},{4,5},{5,4},{6,7},{7,6}} | collective-permute-start | bytes 176160768 | tf_op jit(solution)/shard_map/ppermute | solution.py:173
  0.8 363.7 %collective-permute-start = (bf16[2048,4096]{1,0:T(8,128)(2,1)}, bf16[2048,4096]{1,0:T(8,128)(2,1)}, u32[]{:S(2)}, u32[]{:S(2)}) collective-permute-start(bf16[2048,4096]{1,0:T(8,128)(2,1)} %param.2), channel_id=1, source_target_pairs={{0,4},{4,0},{1,5},{5,1},{2,6},{6,2},{3,7},{7,3}} | collective-permute-start | bytes 50331656 | tf_op jit(solution)/shard_map/ppermute | solution.py:172
  4.4 29.9 %collective-permute-start.6 = (bf16[2048,128]{1,0:T(8,128)(2,1)S(1)}, bf16[2048,128]{1,0:T(8,128)(2,1)S(1)}, u32[]{:S(2)}, u32[]{:S(2)}) collective-permute-start(bf16[2048,128]{1,0:T(8,128)(2,1)S(1)} %slice.40), channel_id=1, source_target_pairs={{0,2},{2,0},{1,3},{3,1},{4,6},{6,4},{5,7},{7,5}} | collective-permute-start | bytes 1572872 | tf_op jit(solution)/shard_map/ppermute | solution.py:169
  28.2 472.6 %collective-permute-start.4 = (bf16[2048,2560]{1,0:T(8,128)(2,1)}, bf16[2048,2560]{1,0:T(8,128)(2,1)}, u32[]{:S(2)}, u32[]{:S(2)}) collective-permute-start(bf16[2048,2560]{1,0:T(8,128)(2,1)} %get-tuple-element.55), channel_id=1, source_target_pairs={{0,2},{2,0},{1,3},{3,1},{4,6},{6,4},{5,7},{7,5}} | collective-permute-start | bytes 31457288 | tf_op jit(solution)/shard_map/ppermute | solution.py:169
  32.8 371.2 %collective-permute-start.5 = (bf16[2048,896]{1,0:T(8,128)(2,1)}, bf16[2048,896]{1,0:T(8,128)(2,1)}, u32[]{:S(2)}, u32[]{:S(2)}) collective-permute-start(bf16[2048,896]{1,0:T(8,128)(2,1)} %slice.39), channel_id=1, source_target_pairs={{0,2},{2,0},{1,3},{3,1},{4,6},{6,4},{5,7},{7,5}} | collective-permute-start | bytes 11010056 | tf_op jit(solution)/shard_map/ppermute | solution.py:169
  34.3 352.8 %copy-start.1 = (bf16[2048,128]{1,0:T(8,128)(2,1)}, bf16[2048,128]{1,0:T(8,128)(2,1)S(1)}, u32[]{:S(2)}) copy-start(bf16[2048,128]{1,0:T(8,128)(2,1)S(1)} %collective-permute-done.6.b2) | copy-start | bytes 1572868
  34.3 352.8 %collective-permute-start.7 = (bf16[2048,128]{1,0:T(8,128)(2,1)S(1)}, bf16[2048,128]{1,0:T(8,128)(2,1)S(1)}, u32[]{:S(2)}, u32[]{:S(2)}) collective-permute-start(bf16[2048,128]{1,0:T(8,128)(2,1)S(1)} %collective-permute-done.6.b2), channel_id=1, source_target_pairs={{0,1},{1,0},{2,3},{3,2},{4,5},{5,4},{6,7},{7,6}} | collective-permute-start | bytes 1572872 | tf_op jit(solution)/shard_map/ppermute | solution.py:184
  387.1 0.8 copy-start.2
  404.1 6.8 collective-permute-start.8
  500.8 16.5 %collective-permute-start.9 = (bf16[2048,2560]{1,0:T(8,128)(2,1)}, bf16[2048,2560]{1,0:T(8,128)(2,1)}, u32[]{:S(2)}, u32[]{:S(2)}) collective-permute-start(bf16[2048,2560]{1,0:T(8,128)(2,1)} %collective-permute-done.4.b2), channel_id=1, source_target_pairs={{0,1},{1,0},{2,3},{3,2},{4,5},{5,4},{6,7},{7,6}} | collective-permute-start | bytes 31457288 | tf_op jit(solution)/shard_map/ppermute | solution.py:184
  500.9 228.0 %collective-permute-start.3 = (bf16[2048,2560]{1,0:T(8,128)(2,1)}, bf16[2048,2560]{1,0:T(8,128)(2,1)}, u32[]{:S(2)}, u32[]{:S(2)}) collective-permute-start(bf16[2048,2560]{1,0:T(8,128)(2,1)} %get-tuple-element.56), channel_id=1, source_target_pairs={{0,2},{2,0},{1,3},{3,1},{4,6},{6,4},{5,7},{7,5}} | collective-permute-start | bytes 31457288 | tf_op jit(solution)/shard_map/ppermute | solution.py:169
  728.9 16.5 %collective-permute-start.10 = (bf16[2048,2560]{1,0:T(8,128)(2,1)}, bf16[2048,2560]{1,0:T(8,128)(2,1)}, u32[]{:S(2)}, u32[]{:S(2)}) collective-permute-start(bf16[2048,2560]{1,0:T(8,128)(2,1)} %collective-permute-done.3.b2), channel_id=1, source_target_pairs={{0,1},{1,0},{2,3},{3,2},{4,5},{5,4},{6,7},{7,6}} | collective-permute-start | bytes 31457288 | tf_op jit(solution)/shard_map/ppermute | solution.py:184
  728.9 228.1 %collective-permute-start.2 = (bf16[2048,2560]{1,0:T(8,128)(2,1)}, bf16[2048,2560]{1,0:T(8,128)(2,1)}, u32[]{:S(2)}, u32[]{:S(2)}) collective-permute-start(bf16[2048,2560]{1,0:T(8,128)(2,1)} %get-tuple-element.57), channel_id=1, source_target_pairs={{0,2},{2,0},{1,3},{3,1},{4,6},{6,4},{5,7},{7,5}} | collective-permute-start | bytes 31457288 | tf_op jit(solution)/shard_map/ppermute | solution.py:169
  957.1 16.5 %collective-permute-start.11 = (bf16[2048,2560]{1,0:T(8,128)(2,1)}, bf16[2048,2560]{1,0:T(8,128)(2,1)}, u32[]{:S(2)}, u32[]{:S(2)}) collective-permute-start(bf16[2048,2560]{1,0:T(8,128)(2,1)} %collective-permute-done.2.b2), channel_id=1, source_target_pairs={{0,1},{1,0},{2,3},{3,2},{4,5},{5,4},{6,7},{7,6}} | collective-permute-start | bytes 31457288 | tf_op jit(solution)/shard_map/ppermute | solution.py:184
  965.4 183.2 %collective-permute-start.18 = (bf16[2048,2048]{1,0:T(8,128)(2,1)}, bf16[2048,2048]{1,0:T(8,128)(2,1)}, u32[]{:S(2)}, u32[]{:S(2)}) collective-permute-start(bf16[2048,2048]{1,0:T(8,128)(2,1)} %slice.47), channel_id=1, source_target_pairs={{0,2},{2,0},{1,3},{3,1},{4,6},{6,4},{5,7},{7,5}} | collective-permute-start | bytes 25165832 | tf_op jit(solution)/shard_map/ppermute | solution.py:169
  1148.5 13.5 collective-permute-start.19
  1154.3 138.2 %collective-permute-start.17 = (bf16[2048,1536]{1,0:T(8,128)(2,1)}, bf16[2048,1536]{1,0:T(8,128)(2,1)}, u32[]{:S(2)}, u32[]{:S(2)}) collective-permute-start(bf16[2048,1536]{1,0:T(8,128)(2,1)} %slice.46), channel_id=1, source_target_pairs={{0,2},{2,0},{1,3},{3,1},{4,6},{6,4},{5,7},{7,5}} | collective-permute-start | bytes 18874376 | tf_op jit(solution)/shard_map/ppermute | solution.py:169
  1292.6 10.5 collective-permute-start.20
  1297.2 93.3 %collective-permute-start.16 = (bf16[2048,1024]{1,0:T(8,128)(2,1)}, bf16[2048,1024]{1,0:T(8,128)(2,1)}, u32[]{:S(2)}, u32[]{:S(2)}) collective-permute-start(bf16[2048,1024]{1,0:T(8,128)(2,1)} %slice.45), channel_id=1, source_target_pairs={{0,2},{2,0},{1,3},{3,1},{4,6},{6,4},{5,7},{7,5}} | collective-permute-start | bytes 12582920 | tf_op jit(solution)/shard_map/ppermute | solution.py:169
  1390.5 53.5 %collective-permute-start.21 = (bf16[2048,1024]{1,0:T(8,128)(2,1)}, bf16[2048,1024]{1,0:T(8,128)(2,1)}, u32[]{:S(2)}, u32[]{:S(2)}) collective-permute-start(bf16[2048,1024]{1,0:T(8,128)(2,1)} %collective-permute-done.16.b0), channel_id=1, source_target_pairs={{0,1},{1,0},{2,3},{3,2},{4,5},{5,4},{6,7},{7,6}} | collective-permute-start | bytes 12582920 | tf_op jit(solution)/shard_map/ppermute | solution.py:184
  1393.5 83.1 %collective-permute-start.15 = (bf16[2048,512]{1,0:T(8,128)(2,1)}, bf16[2048,512]{1,0:T(8,128)(2,1)}, u32[]{:S(2)}, u32[]{:S(2)}) collective-permute-start(bf16[2048,512]{1,0:T(8,128)(2,1)} %slice.44), channel_id=1, source_target_pairs={{0,2},{2,0},{1,3},{3,1},{4,6},{6,4},{5,7},{7,5}} | collective-permute-start | bytes 6291464 | tf_op jit(solution)/shard_map/ppermute | solution.py:169
  1443.9 5.8 copy-start
  1476.6 4.4 collective-permute-start.22
  1478.1 25.4 %collective-permute-start.14 = (bf16[2048,256]{1,0:T(8,128)(2,1)S(1)}, bf16[2048,256]{1,0:T(8,128)(2,1)S(1)}, u32[]{:S(2)}, u32[]{:S(2)}) collective-permute-start(bf16[2048,256]{1,0:T(8,128)(2,1)S(1)} %slice.43), channel_id=1, source_target_pairs={{0,2},{2,0},{1,3},{3,1},{4,6},{6,4},{5,7},{7,5}} | collective-permute-start | bytes 3145736 | tf_op jit(solution)/shard_map/ppermute | solution.py:169
  1503.5 2.7 collective-permute-start.23
  1504.8 14.4 collective-permute-start.13
  1519.1 1.9 collective-permute-start.24
  1519.1 14.3 collective-permute-start.12
  1533.5 1.9 collective-permute-start.25

commit v3 on v2

--- a/solution.py
+++ b/solution.py
@@ -1,3 +1,5 @@
+import functools
+
 import jax
 import jax.numpy as jnp
 from jax import lax
@@ -101,31 +103,32 @@
     )(core, a_near, a_near, b_own, b_pair)
 
 
-def far_body(core_ref, a0, a1, b0, b1, s_ref, *rest):
-    out_ref = rest[-1]
+def far_body(count, core_ref, *refs):
+    a_refs, b_refs = refs[:count], refs[count : 2 * count]
+    s_ref, out_ref = refs[2 * count], refs[-1]
     total = s_ref[...]
-    total += jnp.dot(a0[...], b0[...], preferred_element_type=jnp.float32)
-    total += jnp.dot(a1[...], b1[...], preferred_element_type=jnp.float32)
+    for a_ref, b_ref in zip(a_refs, b_refs):
+        total += jnp.dot(a_ref[...], b_ref[...], preferred_element_type=jnp.float32)
     out_ref[...] = total.astype(out_ref.dtype)
 
 
-def far_product(core, a_far, x_own, x_pair, sums, sums_start, part, parts, c_prev, start, tm=256):
+def far_product(core, a_far, x_own, x_pair, sums, sums_start, part, parts, c_prev, start, tm=1024):
     rows = a_far.shape[0]
-    depth, width = x_own.shape
-    tn = tile_of(start, width)
+    depth, width = (x_pair if x_own is None else x_own).shape
+    tn = min(256, tile_of(start, width))
     first = start // tn
     sums_first = sums_start // tn
     a_mine = pl.BlockSpec((tm, depth), lambda n, m, core: (m, core[0] * parts + part))
     a_other = pl.BlockSpec((tm, depth), lambda n, m, core: (m, (1 - core[0]) * parts + part))
     b_piece = pl.BlockSpec((depth, tn), lambda n, m, core: (0, n))
-    in_specs = [
-        a_mine, a_other, b_piece, b_piece, pl.BlockSpec((tm, tn), lambda n, m, core: (m, sums_first + n)),
-    ]
-    args = [a_far, a_far, x_own, x_pair, sums]
+    pairs = [(a, x) for a, x in ((a_mine, x_own), (a_other, x_pair)) if x is not None]
+    in_specs = [a for a, _ in pairs] + [b_piece] * len(pairs)
+    in_specs.append(pl.BlockSpec((tm, tn), lambda n, m, core: (m, sums_first + n)))
+    args = [a_far] * len(pairs) + [x for _, x in pairs] + [sums]
     if c_prev is None:
         out_specs = pl.BlockSpec((tm, tn), lambda n, m, core: (m, n))
         out_shape = jax.ShapeDtypeStruct((rows, width), jnp.float32)
-        aliases = {}
+        aliases = {len(args): 0} if sums.shape == (rows, width) else {}
     else:
         in_specs.append(pl.BlockSpec(memory_space=pl.ANY))
         aliases = {1 + len(args): 0}
@@ -133,7 +136,7 @@
         out_specs = pl.BlockSpec((tm, tn), lambda n, m, core: (m, first + n))
         out_shape = jax.ShapeDtypeStruct(c_prev.shape, c_prev.dtype)
     return pl.pallas_call(
-        far_body,
+        functools.partial(far_body, len(pairs)),
         grid_spec=pltpu.PrefetchScalarGridSpec(
             num_scalar_prefetch=1,
             grid=(width // tn, rows // tm),
@@ -142,7 +145,7 @@
         ),
         out_shape=out_shape,
         input_output_aliases=aliases,
-        cost_estimate=matmul_cost(rows, 2 * depth, width, width // tn),
+        cost_estimate=matmul_cost(rows, len(pairs) * depth, width, width // tn),
         compiler_params=pltpu.CompilerParams(vmem_limit_bytes=FAR_VMEM * MIB),
     )(core, *args)
 
@@ -187,7 +190,8 @@
             elif part < parts - 1:
                 half = far_product(core, a_far, x, x_pair, sums, starts[j] - starts[TAIL], part, parts, None, starts[j])
             elif half is not None:
-                c = far_product(core, a_far, x, x_pair, half, 0, part, parts, c, starts[j])
+                half = far_product(core, a_far, x, None, half, 0, part, parts, None, starts[j])
+                c = far_product(core, a_far, None, x_pair, half, 0, part, parts, c, starts[j])
                 half = None
             else:
                 c = far_product(core, a_far, x, x_pair, sums, starts[j] - starts[TAIL], part, parts, c, starts[j])

time: 1540 us -> 1540 us (level)
    pallas_call x5 -> x6, Pallas kernels: 61.2 us -> 54.8 us  [far_product(): pl.pallas_call(functools.partial(far_body, len(pairs)), grid_spec=pltpu.P...]
  transfers between devices with their start and end apart: 26 -> 26, of which waited for: 19 -> 18; matrix products, arithmetic and copies ran while one was open for 5% -> 5% of each run, Pallas kernels for 44% -> 44%
where the time goes in v3:
time: 1540 us
  waiting for transfers between devices  764 us (50%)
  Pallas kernels  673 us (44%)
  local copies, waits for them, and re-layouts  58.3 us (4%)
  other arithmetic  22.6 us (1%)
  starting transfers between devices  18.6 us (1%)
    pallas_call x7, Pallas kernels, whole_product(): pl.pallas_call(whole_body, grid_spec=pltpu.PrefetchScalarGridSpec(num_sca...  570 us
    ppermute x12, waiting for transfers between devices, local_product(): x_own.append(lax.ppermute(piece, 'row', across))  376 us
    ppermute x1, waiting for transfers between devices, local_product(): a_recv = lax.ppermute(a_blk, 'col', [(0, 1), (1, 0)])  330 us
    ppermute x12, waiting for transfers between devices, local_product(): x_pair = lax.ppermute(x, 'row', beside)  58 us
    pallas_call x6, Pallas kernels, far_product(): pl.pallas_call(functools.partial(far_body, len(pairs)), grid_spec=pltpu.P...  54.8 us
    slice x9, local copies, waits for them, and re-layouts, local_product(): lax.slice(b_blk, (part * rows, begin), ((part + 1) * rows, begin + width))  51.7 us
    pallas_call x1, Pallas kernels, near_sums(): pl.pallas_call(near_body, grid_spec=pltpu.PrefetchScalarGridSpec(num_scal...  48.7 us
  transfers between devices with their start and end apart: 26, of which 18 were waited for; matrix products, arithmetic and copies ran while one was open for 5% of the time, Pallas kernels for 44%

profile of v3, /device:TPU:0, one launch (start us, length us, event | category | flops | bytes accessed | tf_op | source)
XLA Modules:
  0.0 1536.6 jit_solution(13615048716311008194)
XLA Ops:
  0.8 2.5 collective-permute-start
  4.4 1.5 collective-permute-start.6
  5.9 22.2 %fusion.1 = (bf16[2048,2560]{1,0:T(8,128)(2,1)}, bf16[2048,2560]{1,0:T(8,128)(2,1)}, bf16[2048,2560]{1,0:T(8,128)(2,1)}) fusion(bf16[2048,14336]{1,0:T(8,128)(2,1)} %b0.15), kind=kLoop, calls=%fused_computation.3 | loop fusion | bytes 62914560 | tf_op jit(solution)/shard_map/slice | solution.py:171
  28.7 4.1 slice.39
  32.8 1.5 collective-permute-start.5
  34.4 330.2 %collective-permute-done = bf16[2048,4096]{1,0:T(8,128)(2,1)} collective-permute-done((bf16[2048,4096]{1,0:T(8,128)(2,1)}, bf16[2048,4096]{1,0:T(8,128)(2,1)}, u32[]{:S(2)}, u32[]{:S(2)}) %collective-permute-start) | collective-permute-done | bytes 16777248 | tf_op jit(solution)/shard_map/ppermute | solution.py:175
  364.5 22.6 %broadcast_select_fusion = (bf16[2048,4096]{1,0:T(8,128)(2,1)}, bf16[2048,4096]{1,0:T(8,128)(2,1)}) fusion(bf16[2048,4096]{1,0:T(8,128)(2,1)} %collective-permute-done, bf16[2048,4096]{1,0:T(8,128)(2,1)} %param.2, pred[]{:T(512)S(6)} %eq.3), kind=kLoop, calls=%fused_computation | loop fusion | flops 16777216 | bytes 67108864 | tf_op jit(solution)/shard_map/jit(_where)/select_n | solution.py:178
  388.0 16.1 %shard_map.28.rest_0_ = bf16[2048,14336]{1,0:T(8,128)(2,1)} custom-call(s32[1]{0:T(128)} %bitcast.core_ref, bf16[2048,4096]{1,0:T(8,128)(2,1)} %get-tuple-element.59.a0.a1, bf16[2048,4096]{1,0:T(8,128)(2,1)} %get-tuple-element.59.a0.a1, bf16[2048,4096]{1,0:T(8,128)(2,1)} %get-tuple-element.58.a2.a3.refs_0_.refs_1_, ...), custom_call_target="tpu_custom_call" | custom-call | flops 4294967296 | bytes 36175872 | tf_op jit(solution)/shard_map/pallas_call | solution.py:60
  404.1 6.7 collective-permute-done.8.b3
  410.8 90.0 %shard_map.29.rest_0_ = bf16[2048,14336]{1,0:T(8,128)(2,1)} custom-call(s32[1]{0:T(128)} %bitcast.core_ref, bf16[2048,4096]{1,0:T(8,128)(2,1)} %get-tuple-element.59.a0.a1, bf16[2048,4096]{1,0:T(8,128)(2,1)} %get-tuple-element.59.a0.a1, bf16[2048,4096]{1,0:T(8,128)(2,1)} %get-tuple-element.58.a2.a3.refs_0_.refs_1_, ...), custom_call_target="tpu_custom_call", output_to_operand_aliasing={{}: (9, {})} | custom-call | flops 30064771072 | bytes 253231104 | tf_op jit(solution)/shard_map/pallas_call | solution.py:60
  500.9 1.7 collective-permute-start.3
  502.7 14.7 collective-permute-done.9.b3
  517.3 104.7 %shard_map.30.rest_0_ = bf16[2048,14336]{1,0:T(8,128)(2,1)} custom-call(s32[1]{0:T(128)} %bitcast.core_ref, bf16[2048,4096]{1,0:T(8,128)(2,1)} %get-tuple-element.59.a0.a1, bf16[2048,4096]{1,0:T(8,128)(2,1)} %get-tuple-element.59.a0.a1, bf16[2048,4096]{1,0:T(8,128)(2,1)} %get-tuple-element.58.a2.a3.refs_0_.refs_1_, ...), custom_call_target="tpu_custom_call", output_to_operand_aliasing={{}: (9, {})} | custom-call | flops 85899345920 | bytes 220200960 | tf_op jit(solution)/shard_map/pallas_call | solution.py:60
  622.0 106.9 %collective-permute-done.3.b2 = bf16[2048,2560]{1,0:T(8,128)(2,1)} collective-permute-done((bf16[2048,2560]{1,0:T(8,128)(2,1)}, bf16[2048,2560]{1,0:T(8,128)(2,1)}, u32[]{:S(2)}, u32[]{:S(2)}) %collective-permute-start.3) | collective-permute-done | bytes 10485792 | tf_op jit(solution)/shard_map/ppermute | solution.py:172
  728.9 1.7 collective-permute-start.2
  730.7 14.8 collective-permute-done.10.b3
  745.4 104.7 %shard_map.31.rest_0_ = bf16[2048,14336]{1,0:T(8,128)(2,1)} custom-call(s32[1]{0:T(128)} %bitcast.core_ref, bf16[2048,4096]{1,0:T(8,128)(2,1)} %get-tuple-element.59.a0.a1, bf16[2048,4096]{1,0:T(8,128)(2,1)} %get-tuple-element.59.a0.a1, bf16[2048,4096]{1,0:T(8,128)(2,1)} %get-tuple-element.58.a2.a3.refs_0_.refs_1_, ...), custom_call_target="tpu_custom_call", output_to_operand_aliasing={{}: (9, {})} | custom-call | flops 85899345920 | bytes 220200960 | tf_op jit(solution)/shard_map/pallas_call | solution.py:60
  850.2 106.9 %collective-permute-done.2.b2 = bf16[2048,2560]{1,0:T(8,128)(2,1)} collective-permute-done((bf16[2048,2560]{1,0:T(8,128)(2,1)}, bf16[2048,2560]{1,0:T(8,128)(2,1)}, u32[]{:S(2)}, u32[]{:S(2)}) %collective-permute-start.2) | collective-permute-done | bytes 10485792 | tf_op jit(solution)/shard_map/ppermute | solution.py:172
  957.1 8.3 slice.47
  965.4 1.7 collective-permute-start.18
  967.1 6.5 collective-permute-done.11.b3
  973.6 104.7 %shard_map.32.rest_0_ = bf16[2048,14336]{1,0:T(8,128)(2,1)} custom-call(s32[1]{0:T(128)} %bitcast.core_ref, bf16[2048,4096]{1,0:T(8,128)(2,1)} %get-tuple-element.59.a0.a1, bf16[2048,4096]{1,0:T(8,128)(2,1)} %get-tuple-element.59.a0.a1, bf16[2048,4096]{1,0:T(8,128)(2,1)} %get-tuple-element.58.a2.a3.refs_0_.refs_1_, ...), custom_call_target="tpu_custom_call", output_to_operand_aliasing={{}: (9, {})} | custom-call | flops 85899345920 | bytes 220200960 | tf_op jit(solution)/shard_map/pallas_call | solution.py:60
  1078.3 70.3 %collective-permute-done.18.b2 = bf16[2048,2048]{1,0:T(8,128)(2,1)} collective-permute-done((bf16[2048,2048]{1,0:T(8,128)(2,1)}, bf16[2048,2048]{1,0:T(8,128)(2,1)}, u32[]{:S(2)}, u32[]{:S(2)}) %collective-permute-start.18) | collective-permute-done | bytes 8388640 | tf_op jit(solution)/shard_map/ppermute | solution.py:172
  1148.5 5.8 slice.46
  1154.3 1.7 collective-permute-start.17
  1156.0 6.0 collective-permute-done.19.b3
  1162.0 84.7 %shard_map.33.rest_0_ = bf16[2048,14336]{1,0:T(8,128)(2,1)} custom-call(s32[1]{0:T(128)} %bitcast.core_ref, bf16[2048,4096]{1,0:T(8,128)(2,1)} %get-tuple-element.59.a0.a1, bf16[2048,4096]{1,0:T(8,128)(2,1)} %get-tuple-element.59.a0.a1, bf16[2048,4096]{1,0:T(8,128)(2,1)} %get-tuple-element.58.a2.a3.refs_0_.refs_1_, ...), custom_call_target="tpu_custom_call", output_to_operand_aliasing={{}: (9, {})} | custom-call | flops 68719476736 | bytes 176160768 | tf_op jit(solution)/shard_map/pallas_call | solution.py:60
  1246.8 45.8 %collective-permute-done.17.b2 = bf16[2048,1536]{1,0:T(8,128)(2,1)} collective-permute-done((bf16[2048,1536]{1,0:T(8,128)(2,1)}, bf16[2048,1536]{1,0:T(8,128)(2,1)}, u32[]{:S(2)}, u32[]{:S(2)}) %collective-permute-start.17) | collective-permute-done | bytes 6291488 | tf_op jit(solution)/shard_map/ppermute | solution.py:172
  1292.6 4.6 slice.45
  1297.2 1.7 collective-permute-start.16
  1298.9 4.2 collective-permute-done.20.b3
  1303.1 64.8 %shard_map.34.refs_5_ = bf16[2048,14336]{1,0:T(8,128)(2,1)} custom-call(s32[1]{0:T(128)} %bitcast.core_ref, bf16[2048,4096]{1,0:T(8,128)(2,1)} %get-tuple-element.59.a0.a1, bf16[2048,4096]{1,0:T(8,128)(2,1)} %get-tuple-element.59.a0.a1, bf16[2048,4096]{1,0:T(8,128)(2,1)} %get-tuple-element.58.a2.a3.refs_0_.refs_1_, ...), custom_call_target="tpu_custom_call", output_to_operand_aliasing={{}: (9, {})} | custom-call | flops 51539607552 | bytes 132120576 | tf_op jit(solution)/shard_map/pallas_call | solution.py:60
  1367.9 22.6 %collective-permute-done.16.refs_2_ = bf16[2048,1024]{1,0:T(8,128)(2,1)} collective-permute-done((bf16[2048,1024]{1,0:T(8,128)(2,1)}, bf16[2048,1024]{1,0:T(8,128)(2,1)}, u32[]{:S(2)}, u32[]{:S(2)}) %collective-permute-start.16) | collective-permute-done | bytes 4194336 | tf_op jit(solution)/shard_map/ppermute | solution.py:172
  1390.5 3.0 slice.44
  1393.5 1.7 collective-permute-start.15
  1395.2 48.7 %near.1.refs_4_ = f32[2048,2048]{1,0:T(8,128)} custom-call(s32[1]{0:T(128)} %bitcast.core_ref, bf16[2048,4096]{1,0:T(8,128)(2,1)} %get-tuple-element.59.a0.a1, bf16[2048,4096]{1,0:T(8,128)(2,1)} %get-tuple-element.59.a0.a1, bf16[2048,14336]{1,0:T(8,128)(2,1)} %b0.15, bf16[2048,14336]{1,0:T(8,128)(2,1)} %collective-permute-done.1.b1), custom_call_target="tpu_custom_call" | custom-call | flops 34359738368 | bytes 92274688 | tf_op jit(solution)/shard_map/near/pallas_call | solution.py:86
  1443.9 5.8 copy-done
  1449.7 25.5 %shard_map.35.refs_5_ = bf16[2048,14336]{1,0:T(8,128)(2,1)} custom-call(s32[1]{0:T(128)} %bitcast.core_ref, bf16[2048,4096]{1,0:T(8,128)(2,1)S(1)} %copy-done, bf16[2048,4096]{1,0:T(8,128)(2,1)S(1)} %copy-done, bf16[2048,1024]{1,0:T(8,128)(2,1)} %collective-permute-done.16.refs_2_, ...), custom_call_target="tpu_custom_call", output_to_operand_aliasing={{}: (6, {})} | custom-call | flops 17179869184 | bytes 79691776 | tf_op jit(solution)/shard_map/pallas_call | solution.py:138
  1477.1 2.5 collective-permute-done.22.refs_3_
  1479.6 13.5 shard_map.36.refs_5_
  1493.1 9.0 collective-permute-done.14.refs_2_
  1504.8 7.2 shard_map.37.refs_3_
  1512.0 5.7 collective-permute-done.13.refs_2_
  1518.1 1.6 collective-permute-done.24.refs_3_
  1519.7 4.0 shard_map.38.refs_2_
  1523.7 8.4 collective-permute-done.12.refs_1_
  1532.1 1.9 shard_map.39.refs_2_
  1534.0 2.5 shard_map.40
  (34 shorter events, 8.3 us)
Async XLA Ops:
  0.0 387.1 %collective-permute-start.1 = (bf16[2048,14336]{1,0:T(8,128)(2,1)}, bf16[2048,14336]{1,0:T(8,128)(2,1)}, u32[]{:S(2)}, u32[]{:S(2)}) collective-permute-start(bf16[2048,14336]{1,0:T(8,128)(2,1)} %b0.15), channel_id=1, source_target_pairs={{0,1},{1,0},{2,3},{3,2},{4,5},{5,4},{6,7},{7,6}} | collective-permute-start | bytes 176160768 | tf_op jit(solution)/shard_map/ppermute | solution.py:176
  0.8 363.7 %collective-permute-start = (bf16[2048,4096]{1,0:T(8,128)(2,1)}, bf16[2048,4096]{1,0:T(8,128)(2,1)}, u32[]{:S(2)}, u32[]{:S(2)}) collective-permute-start(bf16[2048,4096]{1,0:T(8,128)(2,1)} %param.2), channel_id=1, source_target_pairs={{0,4},{4,0},{1,5},{5,1},{2,6},{6,2},{3,7},{7,3}} | collective-permute-start | bytes 50331656 | tf_op jit(solution)/shard_map/ppermute | solution.py:175
  4.4 29.9 %collective-permute-start.6 = (bf16[2048,128]{1,0:T(8,128)(2,1)S(1)}, bf16[2048,128]{1,0:T(8,128)(2,1)S(1)}, u32[]{:S(2)}, u32[]{:S(2)}) collective-permute-start(bf16[2048,128]{1,0:T(8,128)(2,1)S(1)} %slice.40), channel_id=1, source_target_pairs={{0,2},{2,0},{1,3},{3,1},{4,6},{6,4},{5,7},{7,5}} | collective-permute-start | bytes 1572872 | tf_op jit(solution)/shard_map/ppermute | solution.py:172
  28.2 472.6 %collective-permute-start.4 = (bf16[2048,2560]{1,0:T(8,128)(2,1)}, bf16[2048,2560]{1,0:T(8,128)(2,1)}, u32[]{:S(2)}, u32[]{:S(2)}) collective-permute-start(bf16[2048,2560]{1,0:T(8,128)(2,1)} %get-tuple-element.55), channel_id=1, source_target_pairs={{0,2},{2,0},{1,3},{3,1},{4,6},{6,4},{5,7},{7,5}} | collective-permute-start | bytes 31457288 | tf_op jit(solution)/shard_map/ppermute | solution.py:172
  32.8 371.2 %collective-permute-start.5 = (bf16[2048,896]{1,0:T(8,128)(2,1)}, bf16[2048,896]{1,0:T(8,128)(2,1)}, u32[]{:S(2)}, u32[]{:S(2)}) collective-permute-start(bf16[2048,896]{1,0:T(8,128)(2,1)} %slice.39), channel_id=1, source_target_pairs={{0,2},{2,0},{1,3},{3,1},{4,6},{6,4},{5,7},{7,5}} | collective-permute-start | bytes 11010056 | tf_op jit(solution)/shard_map/ppermute | solution.py:172
  34.3 352.8 %copy-start.1 = (bf16[2048,128]{1,0:T(8,128)(2,1)}, bf16[2048,128]{1,0:T(8,128)(2,1)S(1)}, u32[]{:S(2)}) copy-start(bf16[2048,128]{1,0:T(8,128)(2,1)S(1)} %collective-permute-done.6.b2) | copy-start | bytes 1572868
  34.3 352.8 %collective-permute-start.7 = (bf16[2048,128]{1,0:T(8,128)(2,1)S(1)}, bf16[2048,128]{1,0:T(8,128)(2,1)S(1)}, u32[]{:S(2)}, u32[]{:S(2)}) collective-permute-start(bf16[2048,128]{1,0:T(8,128)(2,1)S(1)} %collective-permute-done.6.b2), channel_id=1, source_target_pairs={{0,1},{1,0},{2,3},{3,2},{4,5},{5,4},{6,7},{7,6}} | collective-permute-start | bytes 1572872 | tf_op jit(solution)/shard_map/ppermute | solution.py:187
  387.1 0.8 copy-start.2
  404.1 6.8 collective-permute-start.8
  500.8 16.5 %collective-permute-start.9 = (bf16[2048,2560]{1,0:T(8,128)(2,1)}, bf16[2048,2560]{1,0:T(8,128)(2,1)}, u32[]{:S(2)}, u32[]{:S(2)}) collective-permute-start(bf16[2048,2560]{1,0:T(8,128)(2,1)} %collective-permute-done.4.b2), channel_id=1, source_target_pairs={{0,1},{1,0},{2,3},{3,2},{4,5},{5,4},{6,7},{7,6}} | collective-permute-start | bytes 31457288 | tf_op jit(solution)/shard_map/ppermute | solution.py:187
  500.9 228.0 %collective-permute-start.3 = (bf16[2048,2560]{1,0:T(8,128)(2,1)}, bf16[2048,2560]{1,0:T(8,128)(2,1)}, u32[]{:S(2)}, u32[]{:S(2)}) collective-permute-start(bf16[2048,2560]{1,0:T(8,128)(2,1)} %get-tuple-element.56), channel_id=1, source_target_pairs={{0,2},{2,0},{1,3},{3,1},{4,6},{6,4},{5,7},{7,5}} | collective-permute-start | bytes 31457288 | tf_op jit(solution)/shard_map/ppermute | solution.py:172
  728.9 16.5 %collective-permute-start.10 = (bf16[2048,2560]{1,0:T(8,128)(2,1)}, bf16[2048,2560]{1,0:T(8,128)(2,1)}, u32[]{:S(2)}, u32[]{:S(2)}) collective-permute-start(bf16[2048,2560]{1,0:T(8,128)(2,1)} %collective-permute-done.3.b2), channel_id=1, source_target_pairs={{0,1},{1,0},{2,3},{3,2},{4,5},{5,4},{6,7},{7,6}} | collective-permute-start | bytes 31457288 | tf_op jit(solution)/shard_map/ppermute | solution.py:187
  728.9 228.1 %collective-permute-start.2 = (bf16[2048,2560]{1,0:T(8,128)(2,1)}, bf16[2048,2560]{1,0:T(8,128)(2,1)}, u32[]{:S(2)}, u32[]{:S(2)}) collective-permute-start(bf16[2048,2560]{1,0:T(8,128)(2,1)} %get-tuple-element.57), channel_id=1, source_target_pairs={{0,2},{2,0},{1,3},{3,1},{4,6},{6,4},{5,7},{7,5}} | collective-permute-start | bytes 31457288 | tf_op jit(solution)/shard_map/ppermute | solution.py:172
  957.1 16.5 %collective-permute-start.11 = (bf16[2048,2560]{1,0:T(8,128)(2,1)}, bf16[2048,2560]{1,0:T(8,128)(2,1)}, u32[]{:S(2)}, u32[]{:S(2)}) collective-permute-start(bf16[2048,2560]{1,0:T(8,128)(2,1)} %collective-permute-done.2.b2), channel_id=1, source_target_pairs={{0,1},{1,0},{2,3},{3,2},{4,5},{5,4},{6,7},{7,6}} | collective-permute-start | bytes 31457288 | tf_op jit(solution)/shard_map/ppermute | solution.py:187
  965.4 183.2 %collective-permute-start.18 = (bf16[2048,2048]{1,0:T(8,128)(2,1)}, bf16[2048,2048]{1,0:T(8,128)(2,1)}, u32[]{:S(2)}, u32[]{:S(2)}) collective-permute-start(bf16[2048,2048]{1,0:T(8,128)(2,1)} %slice.47), channel_id=1, source_target_pairs={{0,2},{2,0},{1,3},{3,1},{4,6},{6,4},{5,7},{7,5}} | collective-permute-start | bytes 25165832 | tf_op jit(solution)/shard_map/ppermute | solution.py:172
  1148.5 13.5 collective-permute-start.19
  1154.3 138.2 %collective-permute-start.17 = (bf16[2048,1536]{1,0:T(8,128)(2,1)}, bf16[2048,1536]{1,0:T(8,128)(2,1)}, u32[]{:S(2)}, u32[]{:S(2)}) collective-permute-start(bf16[2048,1536]{1,0:T(8,128)(2,1)} %slice.46), channel_id=1, source_target_pairs={{0,2},{2,0},{1,3},{3,1},{4,6},{6,4},{5,7},{7,5}} | collective-permute-start | bytes 18874376 | tf_op jit(solution)/shard_map/ppermute | solution.py:172
  1292.6 10.5 collective-permute-start.20
  1297.2 93.3 %collective-permute-start.16 = (bf16[2048,1024]{1,0:T(8,128)(2,1)}, bf16[2048,1024]{1,0:T(8,128)(2,1)}, u32[]{:S(2)}, u32[]{:S(2)}) collective-permute-start(bf16[2048,1024]{1,0:T(8,128)(2,1)} %slice.45), channel_id=1, source_target_pairs={{0,2},{2,0},{1,3},{3,1},{4,6},{6,4},{5,7},{7,5}} | collective-permute-start | bytes 12582920 | tf_op jit(solution)/shard_map/ppermute | solution.py:172
  1390.5 53.5 %collective-permute-start.21 = (bf16[2048,1024]{1,0:T(8,128)(2,1)}, bf16[2048,1024]{1,0:T(8,128)(2,1)}, u32[]{:S(2)}, u32[]{:S(2)}) collective-permute-start(bf16[2048,1024]{1,0:T(8,128)(2,1)} %collective-permute-done.16.refs_2_), channel_id=1, source_target_pairs={{0,1},{1,0},{2,3},{3,2},{4,5},{5,4},{6,7},{7,6}} | collective-permute-start | bytes 12582920 | tf_op jit(solution)/shard_map/ppermute | solution.py:187
  1393.5 81.8 %collective-permute-start.15 = (bf16[2048,512]{1,0:T(8,128)(2,1)}, bf16[2048,512]{1,0:T(8,128)(2,1)}, u32[]{:S(2)}, u32[]{:S(2)}) collective-permute-start(bf16[2048,512]{1,0:T(8,128)(2,1)} %slice.44), channel_id=1, source_target_pairs={{0,2},{2,0},{1,3},{3,1},{4,6},{6,4},{5,7},{7,5}} | collective-permute-start | bytes 6291464 | tf_op jit(solution)/shard_map/ppermute | solution.py:172
  1443.9 5.8 copy-start
  1475.2 4.4 collective-permute-start.22
  1476.8 25.4 %collective-permute-start.14 = (bf16[2048,256]{1,0:T(8,128)(2,1)S(1)}, bf16[2048,256]{1,0:T(8,128)(2,1)S(1)}, u32[]{:S(2)}, u32[]{:S(2)}) collective-permute-start(bf16[2048,256]{1,0:T(8,128)(2,1)S(1)} %slice.43), channel_id=1, source_target_pairs={{0,2},{2,0},{1,3},{3,1},{4,6},{6,4},{5,7},{7,5}} | collective-permute-start | bytes 3145736 | tf_op jit(solution)/shard_map/ppermute | solution.py:172
  1502.1 2.7 collective-permute-start.23
  1503.4 14.4 collective-permute-start.13
  1517.8 1.9 collective-permute-start.24
  1517.8 14.3 collective-permute-start.12
  1532.1 1.9 collective-permute-start.25

commit v4 on v3

v4 whole, which is shorter than its diff:
```python
import functools

import jax
import jax.numpy as jnp
from jax import lax
from jax.experimental import pallas as pl
from jax.experimental.pallas import tpu as pltpu
from jax.sharding import PartitionSpec as P


PIECES = (
    (128, 0, 1, 1), (896, 0, 1, 1), (2560, 0, 1, 1), (2560, 0, 1, 1), (2560, 0, 1, 1), (2048, 0, 1, 1),
    (1536, 0, 1, 1), (1024, 0, 1, 1), (512, 0, 1, 1), (256, 0, 1, 1), (256, 0, 2, 4), (256, 2, 3, 4), (256, 3, 4, 4),
)
TAIL = 7
LATE = 9
NEAR_AFTER = 4
MIB = 1024 * 1024


def matmul_cost(rows, depth, width, tiles):
    return pl.CostEstimate(
        flops=2 * rows * depth * width,
        bytes_accessed=2 * (rows * depth * tiles + depth * width + rows * width),
        transcendentals=0,
    )


def tile_of(start, width, most=512):
    for tn in (512, 256, 128):
        if tn <= most and start % tn == 0 and width % tn == 0:
            return tn


def whole_body(a0, a1, a2, a3, b0, b1, b2, b3, *rest):
    c_ref = rest[-1]
    total = jnp.dot(a0[...], b0[...], preferred_element_type=jnp.float32)
    total += jnp.dot(a1[...], b1[...], preferred_element_type=jnp.float32)
    total += jnp.dot(a2[...], b2[...], preferred_element_type=jnp.float32)
    total += jnp.dot(a3[...], b3[...], preferred_element_type=jnp.float32)
    c_ref[...] = total.astype(c_ref.dtype)


def whole_product(a_parts, b_own, b_pair, x_own, x_pair, c_prev, start, tm=512):
    rows, depth = a_parts[0].shape
    columns = b_own.shape[1]
    width = x_own.shape[1]
    tn = tile_of(start, width)
    first = start // tn
    b_whole = pl.BlockSpec((depth, tn), lambda n, m: (0, first + n))
    b_piece = pl.BlockSpec((depth, tn), lambda n, m: (0, n))
    in_specs = [pl.BlockSpec((tm, depth), lambda n, m: (m, 0))] * 4 + [b_whole, b_whole, b_piece, b_piece]
    args = [*a_parts, b_own, b_pair, x_own, x_pair]
    aliases = {}
    if c_prev is not None:
        in_specs.append(pl.BlockSpec(memory_space=pl.ANY))
        aliases = {len(args): 0}
        args.append(c_prev)
    return pl.pallas_call(
        whole_body,
        grid=(width // tn, rows // tm),
        in_specs=in_specs,
        out_specs=pl.BlockSpec((tm, tn), lambda n, m: (m, first + n)),
        out_shape=jax.ShapeDtypeStruct((rows, columns), jnp.bfloat16),
        input_output_aliases=aliases,
        cost_estimate=matmul_cost(rows, 4 * depth, width, width // tn),
        compiler_params=pltpu.CompilerParams(vmem_limit_bytes=62 * MIB),
    )(*args)


def near_body(a0, a1, b0, b1, s_ref):
    s_ref[...] = jnp.dot(a0[...], b0[...], preferred_element_type=jnp.float32)
    s_ref[...] += jnp.dot(a1[...], b1[...], preferred_element_type=jnp.float32)


def near_sums(a_parts, b_own, b_pair, start, tm=512, tn=512):
    rows, depth = a_parts[0].shape
    width = b_own.shape[1] - start
    first = start // tn
    b_whole = pl.BlockSpec((depth, tn), lambda n, m: (0, first + n))
    return pl.pallas_call(
        near_body,
        grid=(width // tn, rows // tm),
        in_specs=[pl.BlockSpec((tm, depth), lambda n, m: (m, 0))] * 2 + [b_whole, b_whole],
        out_specs=pl.BlockSpec((tm, tn), lambda n, m: (m, n)),
        out_shape=jax.ShapeDtypeStruct((rows, width), jnp.float32),
        cost_estimate=matmul_cost(rows, 2 * depth, width, width // tn),
        compiler_params=pltpu.CompilerParams(vmem_limit_bytes=62 * MIB),
        name="near",
    )(*a_parts, b_own, b_pair)


def far_body(count, *refs):
    a_refs, b_refs = refs[:count], refs[count : 2 * count]
    s_ref, out_ref = refs[2 * count], refs[-1]
    total = s_ref[...]
    for a_ref, b_ref in zip(a_refs, b_refs):
        total += jnp.dot(a_ref[...], b_ref[...], preferred_element_type=jnp.float32)
    out_ref[...] = total.astype(out_ref.dtype)


def far_product(pairs, first_row, sums, sums_start, c_prev, start, tm=1024):
    rows = pairs[0][0].shape[0]
    depth, width = pairs[0][1].shape
    tn = tile_of(start, width, 256)
    first = start // tn
    sums_first = sums_start // tn
    a_column = first_row // depth
    in_specs = [pl.BlockSpec((tm, depth), lambda n, m: (m, a_column))] * len(pairs)
    in_specs += [pl.BlockSpec((depth, tn), lambda n, m: (0, n))] * len(pairs)
    in_specs.append(pl.BlockSpec((tm, tn), lambda n, m: (m, sums_first + n)))
    args = [a for a, _ in pairs] + [x for _, x in pairs] + [sums]
    if c_prev is None:
        out_specs = pl.BlockSpec((tm, tn), lambda n, m: (m, n))
        out_shape = jax.ShapeDtypeStruct((rows, width), jnp.float32)
        aliases = {len(args) - 1: 0} if sums.shape == (rows, width) else {}
    else:
        in_specs.append(pl.BlockSpec(memory_space=pl.ANY))
        aliases = {len(args): 0}
        args.append(c_prev)
        out_specs = pl.BlockSpec((tm, tn), lambda n, m: (m, first + n))
        out_shape = jax.ShapeDtypeStruct(c_prev.shape, c_prev.dtype)
    return pl.pallas_call(
        functools.partial(far_body, len(pairs)),
        grid=(width // tn, rows // tm),
        in_specs=in_specs,
        out_specs=out_specs,
        out_shape=out_shape,
        input_output_aliases=aliases,
        cost_estimate=matmul_cost(rows, len(pairs) * depth, width, width // tn),
        compiler_params=pltpu.CompilerParams(vmem_limit_bytes=FAR_VMEM * MIB),
    )(*args)


FAR_VMEM = 28


def solution(mesh):
    across = [(0, 2), (2, 0), (1, 3), (3, 1)]
    beside = [(0, 1), (1, 0), (2, 3), (3, 2)]
    count = len(PIECES)

    def local_product(a_blk, b_blk):
        depth = b_blk.shape[0]
        row_id = lax.axis_index("row")
        first_core = lax.rem(row_id, 2) == 0
        aligned = lax.div(row_id, 2) == lax.axis_index("col")

        starts = []
        begin = 0
        for width, _, end, parts in PIECES:
            starts.append(begin)
            if end == parts:
                begin += width

        def send(j, block):
            width, lo, hi, parts = PIECES[j]
            rows = depth // parts
            piece = lax.slice(block, (lo * rows, starts[j]), (hi * rows, starts[j] + width))
            return lax.ppermute(piece, "row", across)

        x_own = [send(j, b_blk) for j in range(LATE)]
        a_recv = lax.ppermute(a_blk, "col", [(0, 1), (1, 0)])
        b_pair = lax.ppermute(b_blk, "row", beside)
        a_near = []
        a_far = []
        for side in (True, False):
            mine = first_core == side
            halves = [jnp.where(mine, a[:, :depth], a[:, depth:]) for a in (a_blk, a_recv)]
            a_near.append(jnp.where(aligned, halves[0], halves[1]))
            a_far.append(jnp.where(aligned, halves[1], halves[0]))
        c = None
        sums = None
        for j, (width, lo, hi, parts) in enumerate(PIECES):
            if j == LATE - 2:
                b_late, c = lax.optimization_barrier((b_blk, c))
                x_own += [send(i, b_late) for i in range(LATE, count)]
            x = x_own[j]
            if j >= TAIL and lo > 0:
                x, half = lax.optimization_barrier((x, half))
            elif j:
                x, c = lax.optimization_barrier((x, c))
            x_pair = lax.ppermute(x, "row", beside)
            if j < TAIL:
                c = whole_product(a_near + a_far, b_blk, b_pair, x, x_pair, c, starts[j])
            else:
                row = lo * (depth // parts)
                if lo == 0:
                    half, offset = sums, starts[j] - starts[TAIL]
                pairs = [(a_far[0], x), (a_far[1], x_pair)]
                if j == count - 1:
                    half = far_product(pairs[:1], row, half, offset, None, starts[j])
                    pairs = pairs[1:]
                if hi == parts:
                    c = far_product(pairs, row, half, offset, c, starts[j])
                else:
                    half = far_product(pairs, row, half, offset, None, starts[j])
                    offset = 0
            if j == NEAR_AFTER:
                a_near[0], c = lax.optimization_barrier((a_near[0], c))
                sums = near_sums(a_near, b_blk, b_pair, starts[TAIL])
        return c

    return jax.shard_map(
        local_product,
        mesh=mesh,
        in_specs=(P(("dp", "row"), "col"), P("row", "col")),
        out_specs=P(("dp", "row"), "col"),
        check_vma=False,
    )
```

time: 1540 us -> 1540 us (level)
    ppermute x12 -> x13, waiting for transfers between devices: 376 us -> 689 us  [send(): return lax.ppermute(piece, 'row', across)]
    ppermute x1, waiting for transfers between devices: 330 us -> 21.3 us  [local_product(): a_recv = lax.ppermute(a_blk, 'col', [(0, 1), (1, 0)])]
    pallas_call x14 -> x15, Pallas kernels: 673 us -> 666 us  [the longest x7 568 us: whole_product(): pl.pallas_call(whole_body, grid=(width // tn, rows // tm), in_specs=in_sp...]
    slice x9 -> x10, local copies, waits for them, and re-layouts: 51.7 us -> 52.8 us  [send(): lax.slice(block, (lo * rows, starts[j]), (hi * rows, starts[j] + width))]
    ppermute x12 -> x13, waiting for transfers between devices: 58 us -> 58.5 us  [local_product(): x_pair = lax.ppermute(x, 'row', beside)]
  transfers between devices with their start and end apart: 26 -> 28, of which waited for: 18 -> 22; matrix products, arithmetic and copies ran while one was open for 5% -> 5% of each run, Pallas kernels for 44% -> 43%
where the time goes in v4:
time: 1540 us
  waiting for transfers between devices  769 us (50%)
  Pallas kernels  666 us (43%)
  local copies, waits for them, and re-layouts  60.3 us (4%)
  other arithmetic  21.4 us (1%)
  starting transfers between devices  18.9 us (1%)
    ppermute x13, waiting for transfers between devices, send(): return lax.ppermute(piece, 'row', across)  689 us
    pallas_call x7, Pallas kernels, whole_product(): pl.pallas_call(whole_body, grid=(width // tn, rows // tm), in_specs=in_sp...  568 us
    ppermute x13, waiting for transfers between devices, local_product(): x_pair = lax.ppermute(x, 'row', beside)  58.5 us
    slice x10, local copies, waits for them, and re-layouts, send(): lax.slice(block, (lo * rows, starts[j]), (hi * rows, starts[j] + width))  52.8 us
    pallas_call x7, Pallas kernels, far_product(): pl.pallas_call(functools.partial(far_body, len(pairs)), grid=(width // tn...  49.3 us
    pallas_call x1, Pallas kernels, near_sums(): pl.pallas_call(near_body, grid=(width // tn, rows // tm), in_specs=[pl.Bl...  48.8 us
  transfers between devices with their start and end apart: 28, of which 22 were waited for; matrix products, arithmetic and copies ran while one was open for 5% of the time, Pallas kernels for 43%

profile of v4, /device:TPU:0, one launch (start us, length us, event | category | flops | bytes accessed | tf_op | source)
XLA Modules:
  0.0 1535.7 jit_solution(8911817701789212021)
XLA Ops:
  0.8 2.5 collective-permute-start
  3.3 22.3 %fusion.1 = (bf16[2048,2560]{1,0:T(8,128)(2,1)}, bf16[2048,2560]{1,0:T(8,128)(2,1)}, bf16[2048,2560]{1,0:T(8,128)(2,1)}) fusion(bf16[2048,14336]{1,0:T(8,128)(2,1)} %b0.15), kind=kLoop, calls=%fused_computation.9 | loop fusion | bytes 62914560 | tf_op jit(solution)/shard_map/slice | solution.py:159
  27.1 4.1 slice.62
  34.3 308.9 %collective-permute-done.6.b2 = bf16[2048,128]{1,0:T(8,128)(2,1)S(1)} collective-permute-done((bf16[2048,128]{1,0:T(8,128)(2,1)S(1)}, bf16[2048,128]{1,0:T(8,128)(2,1)S(1)}, u32[]{:S(2)}, u32[]{:S(2)}) %collective-permute-start.6) | collective-permute-done | bytes 524320 | tf_op jit(solution)/shard_map/ppermute | solution.py:160
  343.2 21.3 %collective-permute-done = bf16[2048,4096]{1,0:T(8,128)(2,1)} collective-permute-done((bf16[2048,4096]{1,0:T(8,128)(2,1)}, bf16[2048,4096]{1,0:T(8,128)(2,1)}, u32[]{:S(2)}, u32[]{:S(2)}) %collective-permute-start) | collective-permute-done | bytes 16777248 | tf_op jit(solution)/shard_map/ppermute | solution.py:163
  364.5 21.4 %broadcast_select_fusion.4 = (bf16[2048,2048]{1,0:T(8,128)(2,1)}, bf16[2048,2048]{1,0:T(8,128)(2,1)}, bf16[2048,2048]{1,0:T(8,128)(2,1)}, bf16[2048,2048]{1,0:T(8,128)(2,1)}) fusion(pred[]{:T(512)S(6)} %eq.9, bf16[2048,4096]{1,0:T(8,128)(2,1)} %param.2, pred[]{:T(512)S(6)} %eq.10, bf16[2048,4096]{1,0:T(8,128)(2,1)} %collective-permute-done, pred[]{:T(512)S(6)} %eq.11), kind=kLoop, calls=%fused_computation.4 | loop fusion | flops 33554432 | bytes 67108864 | tf_op jit(solution)/shard_map/jit(_where)/select_n | solution.py:171
  386.7 16.1 %shard_map.28.rest_0_ = bf16[2048,14336]{1,0:T(8,128)(2,1)} custom-call(bf16[2048,2048]{1,0:T(8,128)(2,1)} %get-tuple-element.41.a0, bf16[2048,2048]{1,0:T(8,128)(2,1)} %get-tuple-element.68.a1, bf16[2048,2048]{1,0:T(8,128)(2,1)} %get-tuple-element.66.a2.refs_0_, bf16[2048,2048]{1,0:T(8,128)(2,1)} %get-tuple-element.69.a3.refs_1_.refs_0_, ...), custom_call_target="tpu_custom_call" | custom-call | flops 4294967296 | bytes 36175872 | tf_op jit(solution)/shard_map/pallas_call | solution.py:59
  402.9 6.7 collective-permute-done.8.b3
  409.6 90.0 %shard_map.29.rest_0_ = bf16[2048,14336]{1,0:T(8,128)(2,1)} custom-call(bf16[2048,2048]{1,0:T(8,128)(2,1)} %get-tuple-element.41.a0, bf16[2048,2048]{1,0:T(8,128)(2,1)} %get-tuple-element.68.a1, bf16[2048,2048]{1,0:T(8,128)(2,1)} %get-tuple-element.66.a2.refs_0_, ...), custom_call_target="tpu_custom_call", output_to_operand_aliasing={{}: (8, {})} | custom-call | flops 30064771072 | bytes 253231104 | tf_op jit(solution)/shard_map/pallas_call | solution.py:59
  499.8 1.7 collective-permute-start.3
  501.5 14.7 collective-permute-done.9.b3
  516.2 104.3 %shard_map.30.rest_0_ = bf16[2048,14336]{1,0:T(8,128)(2,1)} custom-call(bf16[2048,2048]{1,0:T(8,128)(2,1)} %get-tuple-element.41.a0, bf16[2048,2048]{1,0:T(8,128)(2,1)} %get-tuple-element.68.a1, bf16[2048,2048]{1,0:T(8,128)(2,1)} %get-tuple-element.66.a2.refs_0_, ...), custom_call_target="tpu_custom_call", output_to_operand_aliasing={{}: (8, {})} | custom-call | flops 85899345920 | bytes 220200960 | tf_op jit(solution)/shard_map/pallas_call | solution.py:59
  620.4 107.4 %collective-permute-done.3.b2 = bf16[2048,2560]{1,0:T(8,128)(2,1)} collective-permute-done((bf16[2048,2560]{1,0:T(8,128)(2,1)}, bf16[2048,2560]{1,0:T(8,128)(2,1)}, u32[]{:S(2)}, u32[]{:S(2)}) %collective-permute-start.3) | collective-permute-done | bytes 10485792 | tf_op jit(solution)/shard_map/ppermute | solution.py:160
  727.8 1.7 collective-permute-start.2
  729.5 14.8 collective-permute-done.10.b3
  744.3 104.3 %shard_map.31.rest_0_ = bf16[2048,14336]{1,0:T(8,128)(2,1)} custom-call(bf16[2048,2048]{1,0:T(8,128)(2,1)} %get-tuple-element.41.a0, bf16[2048,2048]{1,0:T(8,128)(2,1)} %get-tuple-element.68.a1, bf16[2048,2048]{1,0:T(8,128)(2,1)} %get-tuple-element.66.a2.refs_0_, ...), custom_call_target="tpu_custom_call", output_to_operand_aliasing={{}: (8, {})} | custom-call | flops 85899345920 | bytes 220200960 | tf_op jit(solution)/shard_map/pallas_call | solution.py:59
  848.5 107.4 %collective-permute-done.2.b2 = bf16[2048,2560]{1,0:T(8,128)(2,1)} collective-permute-done((bf16[2048,2560]{1,0:T(8,128)(2,1)}, bf16[2048,2560]{1,0:T(8,128)(2,1)}, u32[]{:S(2)}, u32[]{:S(2)}) %collective-permute-start.2) | collective-permute-done | bytes 10485792 | tf_op jit(solution)/shard_map/ppermute | solution.py:160
  955.9 8.3 slice.65
  964.2 1.7 collective-permute-start.13
  966.0 6.5 collective-permute-done.11.b3
  972.4 104.3 %shard_map.32.rest_0_ = bf16[2048,14336]{1,0:T(8,128)(2,1)} custom-call(bf16[2048,2048]{1,0:T(8,128)(2,1)} %get-tuple-element.41.a0, bf16[2048,2048]{1,0:T(8,128)(2,1)} %get-tuple-element.68.a1, bf16[2048,2048]{1,0:T(8,128)(2,1)} %get-tuple-element.66.a2.refs_0_, ...), custom_call_target="tpu_custom_call", output_to_operand_aliasing={{}: (8, {})} | custom-call | flops 85899345920 | bytes 220200960 | tf_op jit(solution)/shard_map/pallas_call | solution.py:59
  1076.8 70.7 %collective-permute-done.13.b2 = bf16[2048,2048]{1,0:T(8,128)(2,1)} collective-permute-done((bf16[2048,2048]{1,0:T(8,128)(2,1)}, bf16[2048,2048]{1,0:T(8,128)(2,1)}, u32[]{:S(2)}, u32[]{:S(2)}) %collective-permute-start.13) | collective-permute-done | bytes 8388640 | tf_op jit(solution)/shard_map/ppermute | solution.py:160
  1147.4 5.9 slice.64
  1153.3 1.7 collective-permute-start.12
  1155.0 5.9 collective-permute-done.14.b3
  1160.9 84.4 %shard_map.33.rest_0_ = bf16[2048,14336]{1,0:T(8,128)(2,1)} custom-call(bf16[2048,2048]{1,0:T(8,128)(2,1)} %get-tuple-element.41.a0, bf16[2048,2048]{1,0:T(8,128)(2,1)} %get-tuple-element.68.a1, bf16[2048,2048]{1,0:T(8,128)(2,1)} %get-tuple-element.66.a2.refs_0_, ...), custom_call_target="tpu_custom_call", output_to_operand_aliasing={{}: (8, {})} | custom-call | flops 68719476736 | bytes 176160768 | tf_op jit(solution)/shard_map/pallas_call | solution.py:59
  1245.3 46.2 %collective-permute-done.12.b2 = bf16[2048,1536]{1,0:T(8,128)(2,1)} collective-permute-done((bf16[2048,1536]{1,0:T(8,128)(2,1)}, bf16[2048,1536]{1,0:T(8,128)(2,1)}, u32[]{:S(2)}, u32[]{:S(2)}) %collective-permute-start.12) | collective-permute-done | bytes 6291488 | tf_op jit(solution)/shard_map/ppermute | solution.py:160
  1291.5 4.6 slice.71
  1296.1 1.7 collective-permute-start.21
  1297.9 4.2 collective-permute-done.15.b3
  1302.0 64.5 %shard_map.34.refs_5_ = bf16[2048,14336]{1,0:T(8,128)(2,1)} custom-call(bf16[2048,2048]{1,0:T(8,128)(2,1)} %get-tuple-element.41.a0, bf16[2048,2048]{1,0:T(8,128)(2,1)} %get-tuple-element.68.a1, bf16[2048,2048]{1,0:T(8,128)(2,1)} %get-tuple-element.66.a2.refs_0_, ...), custom_call_target="tpu_custom_call", output_to_operand_aliasing={{}: (8, {})} | custom-call | flops 51539607552 | bytes 132120576 | tf_op jit(solution)/shard_map/pallas_call | solution.py:59
  1366.6 22.9 %collective-permute-done.21.refs_2_ = bf16[2048,1024]{1,0:T(8,128)(2,1)} collective-permute-done((bf16[2048,1024]{1,0:T(8,128)(2,1)}, bf16[2048,1024]{1,0:T(8,128)(2,1)}, u32[]{:S(2)}, u32[]{:S(2)}) %collective-permute-start.21) | collective-permute-done | bytes 4194336 | tf_op jit(solution)/shard_map/ppermute | solution.py:160
  1389.4 3.1 slice.70
  1392.5 1.7 collective-permute-start.20
  1394.3 48.8 %near.1.refs_4_ = f32[2048,2048]{1,0:T(8,128)} custom-call(bf16[2048,2048]{1,0:T(8,128)(2,1)} %get-tuple-element.41.a0, bf16[2048,2048]{1,0:T(8,128)(2,1)} %get-tuple-element.68.a1, bf16[2048,14336]{1,0:T(8,128)(2,1)} %b0.15, bf16[2048,14336]{1,0:T(8,128)(2,1)} %collective-permute-done.1.b1), custom_call_target="tpu_custom_call" | custom-call | flops 34359738368 | bytes 92274688 | tf_op jit(solution)/shard_map/near/pallas_call | solution.py:81
  1443.0 3.4 copy-done
  1446.4 3.4 copy-done.1
  1449.8 21.6 %shard_map.35.refs_5_ = bf16[2048,14336]{1,0:T(8,128)(2,1)} custom-call(bf16[2048,2048]{1,0:T(8,128)(2,1)S(1)} %copy-done, bf16[2048,2048]{1,0:T(8,128)(2,1)S(1)} %copy-done.1, bf16[2048,1024]{1,0:T(8,128)(2,1)} %collective-permute-done.21.refs_2_, bf16[2048,1024]{1,0:T(8,128)(2,1)} %collective-permute-done.22.refs_3_, ...), custom_call_target="tpu_custom_call", output_to_operand_aliasing={{}: (5, {})} | custom-call | flops 17179869184 | bytes 79691776 | tf_op jit(solution)/shard_map/pallas_call | solution.py:123
  1473.2 2.5 collective-permute-done.23.refs_3_
  1475.8 12.0 shard_map.36.refs_5_
  1487.7 10.5 collective-permute-done.19.refs_2_
  1500.9 6.7 shard_map.37.refs_3_
  1507.6 6.1 collective-permute-done.18.refs_2_
  1515.6 4.0 shard_map.38.refs_4_
  1519.7 3.9 collective-permute-done.17.refs_2_
  1525.1 1.9 shard_map.39.refs_2_
  1527.0 5.3 collective-permute-done.16.refs_1_
  1533.8 1.9 shard_map.41
  (47 shorter events, 15.9 us)
Async XLA Ops:
  0.0 385.9 %collective-permute-start.1 = (bf16[2048,14336]{1,0:T(8,128)(2,1)}, bf16[2048,14336]{1,0:T(8,128)(2,1)}, u32[]{:S(2)}, u32[]{:S(2)}) collective-permute-start(bf16[2048,14336]{1,0:T(8,128)(2,1)} %b0.15), channel_id=1, source_target_pairs={{0,1},{1,0},{2,3},{3,2},{4,5},{5,4},{6,7},{7,6}} | collective-permute-start | bytes 176160768 | tf_op jit(solution)/shard_map/ppermute | solution.py:164
  0.8 363.7 %collective-permute-start = (bf16[2048,4096]{1,0:T(8,128)(2,1)}, bf16[2048,4096]{1,0:T(8,128)(2,1)}, u32[]{:S(2)}, u32[]{:S(2)}) collective-permute-start(bf16[2048,4096]{1,0:T(8,128)(2,1)} %param.2), channel_id=1, source_target_pairs={{0,4},{4,0},{1,5},{5,1},{2,6},{6,2},{3,7},{7,3}} | collective-permute-start | bytes 50331656 | tf_op jit(solution)/shard_map/ppermute | solution.py:163
  25.6 474.0 %collective-permute-start.4 = (bf16[2048,2560]{1,0:T(8,128)(2,1)}, bf16[2048,2560]{1,0:T(8,128)(2,1)}, u32[]{:S(2)}, u32[]{:S(2)}) collective-permute-start(bf16[2048,2560]{1,0:T(8,128)(2,1)} %get-tuple-element.63), channel_id=1, source_target_pairs={{0,2},{2,0},{1,3},{3,1},{4,6},{6,4},{5,7},{7,5}} | collective-permute-start | bytes 31457288 | tf_op jit(solution)/shard_map/ppermute | solution.py:160
  31.2 371.6 %collective-permute-start.5 = (bf16[2048,896]{1,0:T(8,128)(2,1)}, bf16[2048,896]{1,0:T(8,128)(2,1)}, u32[]{:S(2)}, u32[]{:S(2)}) collective-permute-start(bf16[2048,896]{1,0:T(8,128)(2,1)} %slice.62), channel_id=1, source_target_pairs={{0,2},{2,0},{1,3},{3,1},{4,6},{6,4},{5,7},{7,5}} | collective-permute-start | bytes 11010056 | tf_op jit(solution)/shard_map/ppermute | solution.py:160
  32.8 310.4 %collective-permute-start.6 = (bf16[2048,128]{1,0:T(8,128)(2,1)S(1)}, bf16[2048,128]{1,0:T(8,128)(2,1)S(1)}, u32[]{:S(2)}, u32[]{:S(2)}) collective-permute-start(bf16[2048,128]{1,0:T(8,128)(2,1)S(1)} %slice.63), channel_id=1, source_target_pairs={{0,2},{2,0},{1,3},{3,1},{4,6},{6,4},{5,7},{7,5}} | collective-permute-start | bytes 1572872 | tf_op jit(solution)/shard_map/ppermute | solution.py:160
  343.2 42.7 %copy-start.2 = (bf16[2048,128]{1,0:T(8,128)(2,1)}, bf16[2048,128]{1,0:T(8,128)(2,1)S(1)}, u32[]{:S(2)}) copy-start(bf16[2048,128]{1,0:T(8,128)(2,1)S(1)} %collective-permute-done.6.b2) | copy-start | bytes 1572868
  343.2 42.7 %collective-permute-start.7 = (bf16[2048,128]{1,0:T(8,128)(2,1)S(1)}, bf16[2048,128]{1,0:T(8,128)(2,1)S(1)}, u32[]{:S(2)}, u32[]{:S(2)}) collective-permute-start(bf16[2048,128]{1,0:T(8,128)(2,1)S(1)} %collective-permute-done.6.b2), channel_id=1, source_target_pairs={{0,1},{1,0},{2,3},{3,2},{4,5},{5,4},{6,7},{7,6}} | collective-permute-start | bytes 1572872 | tf_op jit(solution)/shard_map/ppermute | solution.py:183
  385.9 0.8 copy-start.3
  402.8 6.8 collective-permute-start.8
  499.6 16.5 %collective-permute-start.9 = (bf16[2048,2560]{1,0:T(8,128)(2,1)}, bf16[2048,2560]{1,0:T(8,128)(2,1)}, u32[]{:S(2)}, u32[]{:S(2)}) collective-permute-start(bf16[2048,2560]{1,0:T(8,128)(2,1)} %collective-permute-done.4.b2), channel_id=1, source_target_pairs={{0,1},{1,0},{2,3},{3,2},{4,5},{5,4},{6,7},{7,6}} | collective-permute-start | bytes 31457288 | tf_op jit(solution)/shard_map/ppermute | solution.py:183
  499.8 228.0 %collective-permute-start.3 = (bf16[2048,2560]{1,0:T(8,128)(2,1)}, bf16[2048,2560]{1,0:T(8,128)(2,1)}, u32[]{:S(2)}, u32[]{:S(2)}) collective-permute-start(bf16[2048,2560]{1,0:T(8,128)(2,1)} %get-tuple-element.64), channel_id=1, source_target_pairs={{0,2},{2,0},{1,3},{3,1},{4,6},{6,4},{5,7},{7,5}} | collective-permute-start | bytes 31457288 | tf_op jit(solution)/shard_map/ppermute | solution.py:160
  727.8 16.5 %collective-permute-start.10 = (bf16[2048,2560]{1,0:T(8,128)(2,1)}, bf16[2048,2560]{1,0:T(8,128)(2,1)}, u32[]{:S(2)}, u32[]{:S(2)}) collective-permute-start(bf16[2048,2560]{1,0:T(8,128)(2,1)} %collective-permute-done.3.b2), channel_id=1, source_target_pairs={{0,1},{1,0},{2,3},{3,2},{4,5},{5,4},{6,7},{7,6}} | collective-permute-start | bytes 31457288 | tf_op jit(solution)/shard_map/ppermute | solution.py:183
  727.8 228.1 %collective-permute-start.2 = (bf16[2048,2560]{1,0:T(8,128)(2,1)}, bf16[2048,2560]{1,0:T(8,128)(2,1)}, u32[]{:S(2)}, u32[]{:S(2)}) collective-permute-start(bf16[2048,2560]{1,0:T(8,128)(2,1)} %get-tuple-element.65), channel_id=1, source_target_pairs={{0,2},{2,0},{1,3},{3,1},{4,6},{6,4},{5,7},{7,5}} | collective-permute-start | bytes 31457288 | tf_op jit(solution)/shard_map/ppermute | solution.py:160
  955.9 16.5 %collective-permute-start.11 = (bf16[2048,2560]{1,0:T(8,128)(2,1)}, bf16[2048,2560]{1,0:T(8,128)(2,1)}, u32[]{:S(2)}, u32[]{:S(2)}) collective-permute-start(bf16[2048,2560]{1,0:T(8,128)(2,1)} %collective-permute-done.2.b2), channel_id=1, source_target_pairs={{0,1},{1,0},{2,3},{3,2},{4,5},{5,4},{6,7},{7,6}} | collective-permute-start | bytes 31457288 | tf_op jit(solution)/shard_map/ppermute | solution.py:183
  964.2 183.2 %collective-permute-start.13 = (bf16[2048,2048]{1,0:T(8,128)(2,1)}, bf16[2048,2048]{1,0:T(8,128)(2,1)}, u32[]{:S(2)}, u32[]{:S(2)}) collective-permute-start(bf16[2048,2048]{1,0:T(8,128)(2,1)} %slice.65), channel_id=1, source_target_pairs={{0,2},{2,0},{1,3},{3,1},{4,6},{6,4},{5,7},{7,5}} | collective-permute-start | bytes 25165832 | tf_op jit(solution)/shard_map/ppermute | solution.py:160
  1147.4 13.5 collective-permute-start.14
  1153.3 138.2 %collective-permute-start.12 = (bf16[2048,1536]{1,0:T(8,128)(2,1)}, bf16[2048,1536]{1,0:T(8,128)(2,1)}, u32[]{:S(2)}, u32[]{:S(2)}) collective-permute-start(bf16[2048,1536]{1,0:T(8,128)(2,1)} %slice.64), channel_id=1, source_target_pairs={{0,2},{2,0},{1,3},{3,1},{4,6},{6,4},{5,7},{7,5}} | collective-permute-start | bytes 18874376 | tf_op jit(solution)/shard_map/ppermute | solution.py:160
  1291.5 10.5 collective-permute-start.15
  1296.1 93.3 %collective-permute-start.21 = (bf16[2048,1024]{1,0:T(8,128)(2,1)}, bf16[2048,1024]{1,0:T(8,128)(2,1)}, u32[]{:S(2)}, u32[]{:S(2)}) collective-permute-start(bf16[2048,1024]{1,0:T(8,128)(2,1)} %slice.71), channel_id=1, source_target_pairs={{0,2},{2,0},{1,3},{3,1},{4,6},{6,4},{5,7},{7,5}} | collective-permute-start | bytes 12582920 | tf_op jit(solution)/shard_map/ppermute | solution.py:160
  1389.4 53.6 %collective-permute-start.22 = (bf16[2048,1024]{1,0:T(8,128)(2,1)}, bf16[2048,1024]{1,0:T(8,128)(2,1)}, u32[]{:S(2)}, u32[]{:S(2)}) collective-permute-start(bf16[2048,1024]{1,0:T(8,128)(2,1)} %collective-permute-done.21.refs_2_), channel_id=1, source_target_pairs={{0,1},{1,0},{2,3},{3,2},{4,5},{5,4},{6,7},{7,6}} | collective-permute-start | bytes 12582920 | tf_op jit(solution)/shard_map/ppermute | solution.py:183
  1392.5 78.9 %collective-permute-start.20 = (bf16[2048,512]{1,0:T(8,128)(2,1)}, bf16[2048,512]{1,0:T(8,128)(2,1)}, u32[]{:S(2)}, u32[]{:S(2)}) collective-permute-start(bf16[2048,512]{1,0:T(8,128)(2,1)} %slice.70), channel_id=1, source_target_pairs={{0,2},{2,0},{1,3},{3,1},{4,6},{6,4},{5,7},{7,5}} | collective-permute-start | bytes 6291464 | tf_op jit(solution)/shard_map/ppermute | solution.py:160
  1443.0 3.4 copy-start
  1446.4 3.4 copy-start.1
  1471.4 4.4 collective-permute-start.23
  1472.9 25.4 %collective-permute-start.19 = (bf16[2048,256]{1,0:T(8,128)(2,1)S(1)}, bf16[2048,256]{1,0:T(8,128)(2,1)S(1)}, u32[]{:S(2)}, u32[]{:S(2)}) collective-permute-start(bf16[2048,256]{1,0:T(8,128)(2,1)S(1)} %slice.69), channel_id=1, source_target_pairs={{0,2},{2,0},{1,3},{3,1},{4,6},{6,4},{5,7},{7,5}} | collective-permute-start | bytes 3145736 | tf_op jit(solution)/shard_map/ppermute | solution.py:160
  1475.8 58.0 %slice-start = ((s8[8388608]{0:T(1024)(128)(4,1)}), s8[4194304]{0:T(1024)(128)(4,1)S(1)}, s32[]{:S(2)}) async-start(s8[8388608]{0:T(1024)(128)(4,1)} %bitcast), calls=%async_computation | async-start | bytes 8388608
  1498.3 2.7 collective-permute-start.24
  1499.4 34.4 %slice-start.1 = ((s8[8388608]{0:T(1024)(128)(4,1)}), s8[4194304]{0:T(1024)(128)(4,1)S(1)}, s32[]{:S(2)}) async-start(s8[8388608]{0:T(1024)(128)(4,1)} %bitcast), calls=%async_computation.1 | async-start | bytes 8388608
  1499.4 14.4 collective-permute-start.18
  1513.7 1.9 collective-permute-start.25
  1514.8 8.7 collective-permute-start.17
  1523.5 1.5 collective-permute-start.26
  1523.6 8.7 collective-permute-start.16
  1532.3 1.5 collective-permute-start.27

commit v5 on v4

--- a/solution.py
+++ b/solution.py
@@ -9,12 +9,16 @@
 
 
 PIECES = (
-    (128, 0, 1, 1), (896, 0, 1, 1), (2560, 0, 1, 1), (2560, 0, 1, 1), (2560, 0, 1, 1), (2048, 0, 1, 1),
-    (1536, 0, 1, 1), (1024, 0, 1, 1), (512, 0, 1, 1), (256, 0, 1, 1), (256, 0, 2, 4), (256, 2, 3, 4), (256, 3, 4, 4),
+    (14080, 256, 0, 2, 8),
+    (0, 256, 0, 1, 1), (256, 768, 0, 1, 1), (1024, 2560, 0, 1, 1), (3584, 2560, 0, 1, 1), (6144, 2560, 0, 1, 1),
+    (8704, 2048, 0, 1, 1), (10752, 1536, 0, 1, 1),
+    (12288, 1024, 0, 1, 1), (13312, 512, 0, 1, 1), (13824, 256, 0, 1, 1),
+    (14080, 256, 2, 4, 8), (14080, 256, 4, 6, 8), (14080, 256, 6, 7, 8), (14080, 256, 7, 8, 8),
 )
-TAIL = 7
-LATE = 9
-NEAR_AFTER = 4
+TAIL = 8
+LATE = 10
+LATEST = 13
+NEAR_AFTER = 5
 MIB = 1024 * 1024
 
 
@@ -99,17 +103,19 @@
     out_ref[...] = total.astype(out_ref.dtype)
 
 
-def far_product(pairs, first_row, sums, sums_start, c_prev, start, tm=1024):
-    rows = pairs[0][0].shape[0]
-    depth, width = pairs[0][1].shape
+def far_product(terms, sums, sums_start, c_prev, start, tm=1024):
+    rows = terms[0][0].shape[0]
+    width = terms[0][1].shape[1]
     tn = tile_of(start, width, 256)
     first = start // tn
     sums_first = sums_start // tn
-    a_column = first_row // depth
-    in_specs = [pl.BlockSpec((tm, depth), lambda n, m: (m, a_column))] * len(pairs)
-    in_specs += [pl.BlockSpec((depth, tn), lambda n, m: (0, n))] * len(pairs)
+    in_specs = [
+        pl.BlockSpec((tm, x.shape[0]), functools.partial(lambda n, m, k: (m, k), k=row // x.shape[0]))
+        for _, x, row in terms
+    ]
+    in_specs += [pl.BlockSpec((x.shape[0], tn), lambda n, m: (0, n)) for _, x, _ in terms]
     in_specs.append(pl.BlockSpec((tm, tn), lambda n, m: (m, sums_first + n)))
-    args = [a for a, _ in pairs] + [x for _, x in pairs] + [sums]
+    args = [a for a, _, _ in terms] + [x for _, x, _ in terms] + [sums]
     if c_prev is None:
         out_specs = pl.BlockSpec((tm, tn), lambda n, m: (m, n))
         out_shape = jax.ShapeDtypeStruct((rows, width), jnp.float32)
@@ -121,22 +127,58 @@
         out_specs = pl.BlockSpec((tm, tn), lambda n, m: (m, first + n))
         out_shape = jax.ShapeDtypeStruct(c_prev.shape, c_prev.dtype)
     return pl.pallas_call(
-        functools.partial(far_body, len(pairs)),
+        functools.partial(far_body, len(terms)),
         grid=(width // tn, rows // tm),
         in_specs=in_specs,
         out_specs=out_specs,
         out_shape=out_shape,
         input_output_aliases=aliases,
-        cost_estimate=matmul_cost(rows, len(pairs) * depth, width, width // tn),
+        cost_estimate=matmul_cost(rows, sum(x.shape[0] for _, x, _ in terms), width, width // tn),
         compiler_params=pltpu.CompilerParams(vmem_limit_bytes=FAR_VMEM * MIB),
     )(*args)
 
 
+def last_body(start, block, a_ref, x_ref, s_ref, c_prev, c_ref, held, sems):
+    rows, width = held.shape
+    copies = []
+    for i in range(rows // block):
+        part = pl.ds(i * block, block)
+        total = s_ref[part, :] + jnp.dot(a_ref[part, :], x_ref[...], preferred_element_type=jnp.float32)
+        held[part, :] = total.astype(held.dtype)
+        copy = pltpu.make_async_copy(held.at[part, :], c_ref.at[part, pl.ds(start, width)], sems.at[i])
+        copy.start()
+        copies.append(copy)
+    for copy in copies:
+        copy.wait()
+
+
+def last_product(a, x, row, sums, c_prev, start, block=512):
+    rows = a.shape[0]
+    depth, width = x.shape
+    return pl.pallas_call(
+        functools.partial(last_body, start, block),
+        grid=(1,),
+        in_specs=[
+            pl.BlockSpec((rows, depth), lambda n: (0, row // depth)),
+            pl.BlockSpec((depth, width), lambda n: (0, 0)),
+            pl.BlockSpec((rows, width), lambda n: (0, 0)),
+            pl.BlockSpec(memory_space=pl.ANY),
+        ],
+        out_specs=pl.BlockSpec(memory_space=pl.ANY),
+        out_shape=jax.ShapeDtypeStruct(c_prev.shape, c_prev.dtype),
+        scratch_shapes=[pltpu.VMEM((rows, width), c_prev.dtype), pltpu.SemaphoreType.DMA((rows // block,))],
+        input_output_aliases={3: 0},
+        cost_estimate=matmul_cost(rows, depth, width, 1),
+        compiler_params=pltpu.CompilerParams(vmem_limit_bytes=FAR_VMEM * MIB),
+        name="last",
+    )(a, x, sums, c_prev)
+
+
 FAR_VMEM = 28
 
 
 def solution(mesh):
-    across = [(0, 2), (2, 0), (1, 3), (3, 1)]
+    across = [(0, 3), (3, 0), (1, 2), (2, 1)]
     beside = [(0, 1), (1, 0), (2, 3), (3, 2)]
     count = len(PIECES)
 
@@ -145,21 +187,19 @@
         row_id = lax.axis_index("row")
         first_core = lax.rem(row_id, 2) == 0
         aligned = lax.div(row_id, 2) == lax.axis_index("col")
-
-        starts = []
-        begin = 0
-        for width, _, end, parts in PIECES:
-            starts.append(begin)
-            if end == parts:
-                begin += width
+        row_of = [lo * depth // parts for _, _, lo, _, parts in PIECES]
 
         def send(j, block):
-            width, lo, hi, parts = PIECES[j]
+            start, width, lo, hi, parts = PIECES[j]
             rows = depth // parts
-            piece = lax.slice(block, (lo * rows, starts[j]), (hi * rows, starts[j] + width))
+            piece = lax.slice(block, (lo * rows, start), (hi * rows, start + width))
             return lax.ppermute(piece, "row", across)
 
+        def pass_on(j):
+            return lax.ppermute(x_own[j], "row", beside)
+
         x_own = [send(j, b_blk) for j in range(LATE)]
+        x_pair = [None] * count
         a_recv = lax.ppermute(a_blk, "col", [(0, 1), (1, 0)])
         b_pair = lax.ppermute(b_blk, "row", beside)
         a_near = []
@@ -168,37 +208,51 @@
             mine = first_core == side
             halves = [jnp.where(mine, a[:, :depth], a[:, depth:]) for a in (a_blk, a_recv)]
             a_near.append(jnp.where(aligned, halves[0], halves[1]))
-            a_far.append(jnp.where(aligned, halves[1], halves[0]))
+            a_far.insert(0, jnp.where(aligned, halves[1], halves[0]))
         c = None
-        sums = None
-        for j, (width, lo, hi, parts) in enumerate(PIECES):
+        for j in range(1, LATE + 1):
+            start = PIECES[j][0]
             if j == LATE - 2:
                 b_late, c = lax.optimization_barrier((b_blk, c))
-                x_own += [send(i, b_late) for i in range(LATE, count)]
-            x = x_own[j]
-            if j >= TAIL and lo > 0:
-                x, half = lax.optimization_barrier((x, half))
-            elif j:
-                x, c = lax.optimization_barrier((x, c))
-            x_pair = lax.ppermute(x, "row", beside)
+                x_own += [send(i, b_late) for i in range(LATE, LATEST)]
+            if j == LATE:
+                b_late, c = lax.optimization_barrier((b_blk, c))
+                x_own += [send(i, b_late) for i in range(LATEST, count)]
+            if j > 1:
+                x_own[j], c = lax.optimization_barrier((x_own[j], c))
+            x_pair[j] = pass_on(j)
             if j < TAIL:
-                c = whole_product(a_near + a_far, b_blk, b_pair, x, x_pair, c, starts[j])
+                c = whole_product(a_near + a_far, b_blk, b_pair, x_own[j], x_pair[j], c, start)
             else:
-                row = lo * (depth // parts)
-                if lo == 0:
-                    half, offset = sums, starts[j] - starts[TAIL]
-                pairs = [(a_far[0], x), (a_far[1], x_pair)]
-                if j == count - 1:
-                    half = far_product(pairs[:1], row, half, offset, None, starts[j])
-                    pairs = pairs[1:]
-                if hi == parts:
-                    c = far_product(pairs, row, half, offset, c, starts[j])
-                else:
-                    half = far_product(pairs, row, half, offset, None, starts[j])
-                    offset = 0
+                terms = [(a_far[0], x_own[j], 0), (a_far[1], x_pair[j], 0)]
+                c = far_product(terms, sums, start - PIECES[TAIL][0], c, start)
+            if j == 2:
+                x_own[0], a_last, c = lax.optimization_barrier((x_own[0], a_far[1], c))
+                x_pair[0] = pass_on(0)
+                a_last = a_last[:, row_of[-1] :]
+                a_last, c = lax.optimization_barrier((a_last, c))
             if j == NEAR_AFTER:
                 a_near[0], c = lax.optimization_barrier((a_near[0], c))
-                sums = near_sums(a_near, b_blk, b_pair, starts[TAIL])
+                sums = near_sums(a_near, b_blk, b_pair, PIECES[TAIL][0])
+
+        start = PIECES[-1][0]
+        both = lambda j: [(a_far[0], x_own[j], row_of[j]), (a_far[1], x_pair[j], row_of[j])]
+        j = LATE + 1
+        x_own[j], c = lax.optimization_barrier((x_own[j], c))
+        x_pair[j] = pass_on(j)
+        half = far_product(both(0) + both(j), sums, start - PIECES[TAIL][0], None, start)
+        j += 1
+        x_own[j], half = lax.optimization_barrier((x_own[j], half))
+        x_pair[j] = pass_on(j)
+        half = far_product(both(j), half, 0, None, start)
+        j += 1
+        x_own[j], half = lax.optimization_barrier((x_own[j], half))
+        x_pair[j] = pass_on(j)
+        j += 1
+        x_own[j], x_pair[j - 1] = lax.optimization_barrier((x_own[j], x_pair[j - 1]))
+        x_pair[j] = pass_on(j)
+        half = far_product(both(j - 1) + both(j)[:1], half, 0, None, start)
+        c = last_product(a_last, x_pair[j], 0, half, c, start)
         return c
 
     return jax.shard_map(

time: 1540 us -> 1480 us (0.961)
  Pallas kernels: 666 us -> 619 us
    ppermute x13 -> x15, waiting for transfers between devices: 689 us -> 612 us  [send(): return lax.ppermute(piece, 'row', across)]
    ppermute x1, waiting for transfers between devices: 21.3 us -> 88.1 us  [local_product(): a_recv = lax.ppermute(a_blk, 'col', [(0, 1), (1, 0)])]
    pallas_call x7, Pallas kernels: 568 us -> 521 us  [whole_product(): pl.pallas_call(whole_body, grid=(width // tn, rows // tm), in_specs=in_sp...]
    ppermute x13 -> x15, waiting for transfers between devices: 58.5 us -> 53.5 us  [pass_on(): return lax.ppermute(x_own[j], 'row', beside)]
    slice x10 -> x12, local copies, waits for them, and re-layouts: 52.8 us -> 54.7 us  [the longest x11 53.4 us: send(): piece = lax.slice(block, (lo * rows, start), (hi * rows, start + width))]
  transfers between devices with their start and end apart: 28 -> 32, of which waited for: 22 -> 21; matrix products, arithmetic and copies ran while one was open for 5% -> 5% of each run, Pallas kernels for 43% -> 42%
where the time goes in v5:
time: 1480 us
  waiting for transfers between devices  754 us (51%)
  Pallas kernels  619 us (42%)
  local copies, waits for them, and re-layouts  62.5 us (4%)
  starting transfers between devices  24.8 us (2%)
  other arithmetic  21.3 us (1%)
    ppermute x15, waiting for transfers between devices, send(): return lax.ppermute(piece, 'row', across)  612 us
    pallas_call x7, Pallas kernels, whole_product(): pl.pallas_call(whole_body, grid=(width // tn, rows // tm), in_specs=in_sp...  521 us
    ppermute x1, waiting for transfers between devices, local_product(): a_recv = lax.ppermute(a_blk, 'col', [(0, 1), (1, 0)])  88.1 us
    ppermute x15, waiting for transfers between devices, pass_on(): return lax.ppermute(x_own[j], 'row', beside)  53.5 us
    slice x11, local copies, waits for them, and re-layouts, send(): piece = lax.slice(block, (lo * rows, start), (hi * rows, start + width))  53.4 us
    pallas_call x1, Pallas kernels, near_sums(): pl.pallas_call(near_body, grid=(width // tn, rows // tm), in_specs=[pl.Bl...  48.7 us
    pallas_call x6, Pallas kernels, far_product(): pl.pallas_call(functools.partial(far_body, len(terms)), grid=(width // tn...  47.9 us
  transfers between devices with their start and end apart: 32, of which 21 were waited for; matrix products, arithmetic and copies ran while one was open for 5% of the time, Pallas kernels for 42%

profile of v5, /device:TPU:0, one launch (start us, length us, event | category | flops | bytes accessed | tf_op | source)
XLA Modules:
  0.0 1481.8 jit_solution(5052386703922036853)
XLA Ops:
  0.8 2.5 collective-permute-start.1
  3.3 22.1 %fusion.2 = (bf16[2048,2560]{1,0:T(8,128)(2,1)}, bf16[2048,2560]{1,0:T(8,128)(2,1)}, bf16[2048,2560]{1,0:T(8,128)(2,1)}) fusion(bf16[2048,14336]{1,0:T(8,128)(2,1)} %b0.15), kind=kLoop, calls=%fused_computation.10 | loop fusion | bytes 62914560 | tf_op jit(solution)/shard_map/slice | solution.py:195
  28.6 3.8 slice.69
  33.7 241.8 %collective-permute-done.4.b2 = bf16[2048,256]{1,0:T(8,128)(2,1)S(1)} collective-permute-done((bf16[2048,256]{1,0:T(8,128)(2,1)S(1)}, bf16[2048,256]{1,0:T(8,128)(2,1)S(1)}, u32[]{:S(2)}, u32[]{:S(2)}) %collective-permute-start.4) | collective-permute-done | bytes 1048608 | tf_op jit(solution)/shard_map/ppermute | solution.py:196
  276.5 88.1 %collective-permute-done.1 = bf16[2048,4096]{1,0:T(8,128)(2,1)} collective-permute-done((bf16[2048,4096]{1,0:T(8,128)(2,1)}, bf16[2048,4096]{1,0:T(8,128)(2,1)}, u32[]{:S(2)}, u32[]{:S(2)}) %collective-permute-start.1) | collective-permute-done | bytes 16777248 | tf_op jit(solution)/shard_map/ppermute | solution.py:203
  364.5 21.3 %broadcast_select_fusion.4 = (bf16[2048,2048]{1,0:T(8,128)(2,1)}, bf16[2048,2048]{1,0:T(8,128)(2,1)}, bf16[2048,2048]{1,0:T(8,128)(2,1)}, bf16[2048,2048]{1,0:T(8,128)(2,1)}) fusion(pred[]{:T(512)S(6)} %eq.9, bf16[2048,4096]{1,0:T(8,128)(2,1)} %param.2, pred[]{:T(512)S(6)} %eq.11, bf16[2048,4096]{1,0:T(8,128)(2,1)} %collective-permute-done.1, pred[]{:T(512)S(6)} %eq.10), kind=kLoop, calls=%fused_computation.4 | loop fusion | flops 33554432 | bytes 67108864 | tf_op jit(solution)/shard_map/jit(_where)/select_n | solution.py:211
  386.8 16.9 %shard_map.28.rest_0_ = bf16[2048,14336]{1,0:T(8,128)(2,1)} custom-call(bf16[2048,2048]{1,0:T(8,128)(2,1)} %get-tuple-element.54.a0, bf16[2048,2048]{1,0:T(8,128)(2,1)} %get-tuple-element.88.a1, bf16[2048,2048]{1,0:T(8,128)(2,1)} %get-tuple-element.86.a2.refs_0_.refs_2_, bf16[2048,2048]{1,0:T(8,128)(2,1)} %get-tuple-element.44.a3.refs_1_.refs_3_, ...), custom_call_target="tpu_custom_call" | custom-call | flops 8589934592 | bytes 38797312 | tf_op jit(solution)/shard_map/pallas_call | solution.py:63
  404.7 1.8 collective-permute-start
  406.6 3.2 collective-permute-done.6.b3
  409.7 42.7 %shard_map.29.rest_0_ = bf16[2048,14336]{1,0:T(8,128)(2,1)} custom-call(bf16[2048,2048]{1,0:T(8,128)(2,1)} %get-tuple-element.54.a0, bf16[2048,2048]{1,0:T(8,128)(2,1)} %get-tuple-element.88.a1, bf16[2048,2048]{1,0:T(8,128)(2,1)} %get-tuple-element.86.a2.refs_0_.refs_2_, ...), custom_call_target="tpu_custom_call", output_to_operand_aliasing={{}: (8, {})} | custom-call | flops 25769803776 | bytes 116391936 | tf_op jit(solution)/shard_map/pallas_call | solution.py:63
  453.9 1.7 collective-permute-start.10
  455.6 14.7 collective-permute-done.12.b3
  470.2 104.3 %shard_map.30.rest_0_ = bf16[2048,14336]{1,0:T(8,128)(2,1)} custom-call(bf16[2048,2048]{1,0:T(8,128)(2,1)} %get-tuple-element.54.a0, bf16[2048,2048]{1,0:T(8,128)(2,1)} %get-tuple-element.88.a1, bf16[2048,2048]{1,0:T(8,128)(2,1)} %get-tuple-element.86.a2.refs_0_.refs_2_, ...), custom_call_target="tpu_custom_call", output_to_operand_aliasing={{}: (8, {})} | custom-call | flops 85899345920 | bytes 220200960 | tf_op jit(solution)/shard_map/pallas_call | solution.py:63
  574.6 106.8 %collective-permute-done.10.b2 = bf16[2048,2560]{1,0:T(8,128)(2,1)} collective-permute-done((bf16[2048,2560]{1,0:T(8,128)(2,1)}, bf16[2048,2560]{1,0:T(8,128)(2,1)}, u32[]{:S(2)}, u32[]{:S(2)}) %collective-permute-start.10) | collective-permute-done | bytes 10485792 | tf_op jit(solution)/shard_map/ppermute | solution.py:196
  683.2 14.7 collective-permute-done.13.b3
  697.8 104.3 %shard_map.31.rest_0_ = bf16[2048,14336]{1,0:T(8,128)(2,1)} custom-call(bf16[2048,2048]{1,0:T(8,128)(2,1)} %get-tuple-element.54.a0, bf16[2048,2048]{1,0:T(8,128)(2,1)} %get-tuple-element.88.a1, bf16[2048,2048]{1,0:T(8,128)(2,1)} %get-tuple-element.86.a2.refs_0_.refs_2_, ...), custom_call_target="tpu_custom_call", output_to_operand_aliasing={{}: (8, {})} | custom-call | flops 85899345920 | bytes 220200960 | tf_op jit(solution)/shard_map/pallas_call | solution.py:63
  802.1 107.3 %collective-permute-done.9.b2 = bf16[2048,2560]{1,0:T(8,128)(2,1)} collective-permute-done((bf16[2048,2560]{1,0:T(8,128)(2,1)}, bf16[2048,2560]{1,0:T(8,128)(2,1)}, u32[]{:S(2)}, u32[]{:S(2)}) %collective-permute-start.9) | collective-permute-done | bytes 10485792 | tf_op jit(solution)/shard_map/ppermute | solution.py:196
  909.5 8.3 slice.78
  917.9 1.7 collective-permute-start.16
  919.6 6.3 collective-permute-done.14.b3
  925.9 104.3 %shard_map.32.rest_0_ = bf16[2048,14336]{1,0:T(8,128)(2,1)} custom-call(bf16[2048,2048]{1,0:T(8,128)(2,1)} %get-tuple-element.54.a0, bf16[2048,2048]{1,0:T(8,128)(2,1)} %get-tuple-element.88.a1, bf16[2048,2048]{1,0:T(8,128)(2,1)} %get-tuple-element.86.a2.refs_0_.refs_2_, ...), custom_call_target="tpu_custom_call", output_to_operand_aliasing={{}: (8, {})} | custom-call | flops 85899345920 | bytes 220200960 | tf_op jit(solution)/shard_map/pallas_call | solution.py:63
  1030.2 70.2 %collective-permute-done.16.b2 = bf16[2048,2048]{1,0:T(8,128)(2,1)} collective-permute-done((bf16[2048,2048]{1,0:T(8,128)(2,1)}, bf16[2048,2048]{1,0:T(8,128)(2,1)}, u32[]{:S(2)}, u32[]{:S(2)}) %collective-permute-start.16) | collective-permute-done | bytes 8388640 | tf_op jit(solution)/shard_map/ppermute | solution.py:196
  1100.8 5.8 slice.77
  1108.1 5.8 collective-permute-done.17.b3
  1113.9 84.4 %shard_map.33.rest_0_ = bf16[2048,14336]{1,0:T(8,128)(2,1)} custom-call(bf16[2048,2048]{1,0:T(8,128)(2,1)} %get-tuple-element.54.a0, bf16[2048,2048]{1,0:T(8,128)(2,1)} %get-tuple-element.88.a1, bf16[2048,2048]{1,0:T(8,128)(2,1)} %get-tuple-element.86.a2.refs_0_.refs_2_, ...), custom_call_target="tpu_custom_call", output_to_operand_aliasing={{}: (8, {})} | custom-call | flops 68719476736 | bytes 176160768 | tf_op jit(solution)/shard_map/pallas_call | solution.py:63
  1198.3 46.1 %collective-permute-done.15.b2 = bf16[2048,1536]{1,0:T(8,128)(2,1)} collective-permute-done((bf16[2048,1536]{1,0:T(8,128)(2,1)}, bf16[2048,1536]{1,0:T(8,128)(2,1)}, u32[]{:S(2)}, u32[]{:S(2)}) %collective-permute-start.15) | collective-permute-done | bytes 6291488 | tf_op jit(solution)/shard_map/ppermute | solution.py:196
  1244.6 4.6 slice.73
  1249.2 1.7 collective-permute-start.8
  1250.9 4.1 collective-permute-done.18.b3
  1254.9 64.5 %shard_map.34.refs_5_ = bf16[2048,14336]{1,0:T(8,128)(2,1)} custom-call(bf16[2048,2048]{1,0:T(8,128)(2,1)} %get-tuple-element.54.a0, bf16[2048,2048]{1,0:T(8,128)(2,1)} %get-tuple-element.88.a1, bf16[2048,2048]{1,0:T(8,128)(2,1)} %get-tuple-element.86.a2.refs_0_.refs_2_, ...), custom_call_target="tpu_custom_call", output_to_operand_aliasing={{}: (8, {})} | custom-call | flops 51539607552 | bytes 132120576 | tf_op jit(solution)/shard_map/pallas_call | solution.py:63
  1319.5 22.3 %collective-permute-done.8.refs_2_ = bf16[2048,1024]{1,0:T(8,128)(2,1)} collective-permute-done((bf16[2048,1024]{1,0:T(8,128)(2,1)}, bf16[2048,1024]{1,0:T(8,128)(2,1)}, u32[]{:S(2)}, u32[]{:S(2)}) %collective-permute-start.8) | collective-permute-done | bytes 4194336 | tf_op jit(solution)/shard_map/ppermute | solution.py:196
  1342.2 3.1 slice.72
  1345.3 1.5 collective-permute-start.7
  1346.7 48.7 %near.1.refs_4_.refs_8_ = f32[2048,2048]{1,0:T(8,128)} custom-call(bf16[2048,2048]{1,0:T(8,128)(2,1)} %get-tuple-element.54.a0, bf16[2048,2048]{1,0:T(8,128)(2,1)} %get-tuple-element.88.a1, bf16[2048,14336]{1,0:T(8,128)(2,1)} %b0.15, bf16[2048,14336]{1,0:T(8,128)(2,1)} %collective-permute-done.2.b1), custom_call_target="tpu_custom_call" | custom-call | flops 34359738368 | bytes 92274688 | tf_op jit(solution)/shard_map/near/pallas_call | solution.py:85
  1395.5 3.4 copy-done
  1398.8 3.4 copy-done.1
  1402.2 21.6 %shard_map.35.refs_5_ = bf16[2048,14336]{1,0:T(8,128)(2,1)} custom-call(bf16[2048,2048]{1,0:T(8,128)(2,1)S(1)} %copy-done, bf16[2048,2048]{1,0:T(8,128)(2,1)S(1)} %copy-done.1, bf16[2048,1024]{1,0:T(8,128)(2,1)} %collective-permute-done.8.refs_2_, bf16[2048,1024]{1,0:T(8,128)(2,1)} %collective-permute-done.19.refs_3_, ...), custom_call_target="tpu_custom_call", output_to_operand_aliasing={{}: (5, {})} | custom-call | flops 17179869184 | bytes 79691776 | tf_op jit(solution)/shard_map/pallas_call | solution.py:129
  1425.6 2.6 collective-permute-done.20.refs_3_
  1428.2 11.8 shard_map.36.refs_5_
  1440.0 10.6 collective-permute-done.26.refs_2_
  1453.3 6.7 shard_map.37.c_prev
  1462.1 4.1 shard_map.38.refs_4_
  1466.2 2.5 collective-permute-done.23.refs_2_
  1470.4 1.5 collective-permute-start.21
  1471.9 1.9 shard_map.39.refs_6_
  1473.8 1.8 collective-permute-done.22.refs_3_
  1476.3 2.1 collective-permute-done.21.refs_5_
  1478.5 1.7 shard_map.40.s_ref
  (52 shorter events, 24.3 us)
Async XLA Ops:
  0.0 386.8 %collective-permute-start.2 = (bf16[2048,14336]{1,0:T(8,128)(2,1)}, bf16[2048,14336]{1,0:T(8,128)(2,1)}, u32[]{:S(2)}, u32[]{:S(2)}) collective-permute-start(bf16[2048,14336]{1,0:T(8,128)(2,1)} %b0.15), channel_id=1, source_target_pairs={{0,1},{1,0},{2,3},{3,2},{4,5},{5,4},{6,7},{7,6}} | collective-permute-start | bytes 176160768 | tf_op jit(solution)/shard_map/ppermute | solution.py:204
  0.8 363.7 %collective-permute-start.1 = (bf16[2048,4096]{1,0:T(8,128)(2,1)}, bf16[2048,4096]{1,0:T(8,128)(2,1)}, u32[]{:S(2)}, u32[]{:S(2)}) collective-permute-start(bf16[2048,4096]{1,0:T(8,128)(2,1)} %param.2), channel_id=1, source_target_pairs={{0,4},{4,0},{1,5},{5,1},{2,6},{6,2},{3,7},{7,3}} | collective-permute-start | bytes 50331656 | tf_op jit(solution)/shard_map/ppermute | solution.py:203
  25.5 428.2 %collective-permute-start.11 = (bf16[2048,2560]{1,0:T(8,128)(2,1)}, bf16[2048,2560]{1,0:T(8,128)(2,1)}, u32[]{:S(2)}, u32[]{:S(2)}) collective-permute-start(bf16[2048,2560]{1,0:T(8,128)(2,1)} %get-tuple-element.83), channel_id=1, source_target_pairs={{0,3},{3,0},{1,2},{2,1},{4,7},{7,4},{5,6},{6,5}} | collective-permute-start | bytes 31457288 | tf_op jit(solution)/shard_map/ppermute | solution.py:196
  28.1 247.3 %collective-permute-start.4 = (bf16[2048,256]{1,0:T(8,128)(2,1)S(1)}, bf16[2048,256]{1,0:T(8,128)(2,1)S(1)}, u32[]{:S(2)}, u32[]{:S(2)}) collective-permute-start(bf16[2048,256]{1,0:T(8,128)(2,1)S(1)} %slice.70), channel_id=1, source_target_pairs={{0,3},{3,0},{1,2},{2,1},{4,7},{7,4},{5,6},{6,5}} | collective-permute-start | bytes 3145736 | tf_op jit(solution)/shard_map/ppermute | solution.py:196
  32.3 371.4 %collective-permute-start.3 = (bf16[2048,768]{1,0:T(8,128)(2,1)}, bf16[2048,768]{1,0:T(8,128)(2,1)}, u32[]{:S(2)}, u32[]{:S(2)}) collective-permute-start(bf16[2048,768]{1,0:T(8,128)(2,1)} %slice.69), channel_id=1, source_target_pairs={{0,3},{3,0},{1,2},{2,1},{4,7},{7,4},{5,6},{6,5}} | collective-permute-start | bytes 9437192 | tf_op jit(solution)/shard_map/ppermute | solution.py:196
  275.5 110.4 %copy-start.2 = (bf16[2048,256]{1,0:T(8,128)(2,1)}, bf16[2048,256]{1,0:T(8,128)(2,1)S(1)}, u32[]{:S(2)}) copy-start(bf16[2048,256]{1,0:T(8,128)(2,1)S(1)} %collective-permute-done.4.b2) | copy-start | bytes 3145732
  275.5 110.4 %collective-permute-start.5 = (bf16[2048,256]{1,0:T(8,128)(2,1)S(1)}, bf16[2048,256]{1,0:T(8,128)(2,1)S(1)}, u32[]{:S(2)}, u32[]{:S(2)}) collective-permute-start(bf16[2048,256]{1,0:T(8,128)(2,1)S(1)} %collective-permute-done.4.b2), channel_id=1, source_target_pairs={{0,1},{1,0},{2,3},{3,2},{4,5},{5,4},{6,7},{7,6}} | collective-permute-start | bytes 3145736 | tf_op jit(solution)/shard_map/ppermute | solution.py:199
  385.9 1.0 copy-start.3
  403.7 6.0 collective-permute-start.6
  404.7 47.7 %collective-permute-start = (bf16[512,256]{1,0:T(8,128)(2,1)S(1)}, bf16[512,256]{1,0:T(8,128)(2,1)}, u32[]{:S(2)}, u32[]{:S(2)}) collective-permute-start(bf16[512,256]{1,0:T(8,128)(2,1)S(1)} %slice.64), channel_id=1, source_target_pairs={{0,3},{3,0},{1,2},{2,1},{4,7},{7,4},{5,6},{6,5}} | collective-permute-start | bytes 786440 | tf_op jit(solution)/shard_map/ppermute | solution.py:196
  453.7 16.5 %collective-permute-start.12 = (bf16[2048,2560]{1,0:T(8,128)(2,1)}, bf16[2048,2560]{1,0:T(8,128)(2,1)}, u32[]{:S(2)}, u32[]{:S(2)}) collective-permute-start(bf16[2048,2560]{1,0:T(8,128)(2,1)} %collective-permute-done.11.b2), channel_id=1, source_target_pairs={{0,1},{1,0},{2,3},{3,2},{4,5},{5,4},{6,7},{7,6}} | collective-permute-start | bytes 31457288 | tf_op jit(solution)/shard_map/ppermute | solution.py:199
  453.9 227.5 %collective-permute-start.10 = (bf16[2048,2560]{1,0:T(8,128)(2,1)}, bf16[2048,2560]{1,0:T(8,128)(2,1)}, u32[]{:S(2)}, u32[]{:S(2)}) collective-permute-start(bf16[2048,2560]{1,0:T(8,128)(2,1)} %get-tuple-element.84), channel_id=1, source_target_pairs={{0,3},{3,0},{1,2},{2,1},{4,7},{7,4},{5,6},{6,5}} | collective-permute-start | bytes 31457288 | tf_op jit(solution)/shard_map/ppermute | solution.py:196
  681.3 16.5 %collective-permute-start.13 = (bf16[2048,2560]{1,0:T(8,128)(2,1)}, bf16[2048,2560]{1,0:T(8,128)(2,1)}, u32[]{:S(2)}, u32[]{:S(2)}) collective-permute-start(bf16[2048,2560]{1,0:T(8,128)(2,1)} %collective-permute-done.10.b2), channel_id=1, source_target_pairs={{0,1},{1,0},{2,3},{3,2},{4,5},{5,4},{6,7},{7,6}} | collective-permute-start | bytes 31457288 | tf_op jit(solution)/shard_map/ppermute | solution.py:199
  681.7 227.7 %collective-permute-start.9 = (bf16[2048,2560]{1,0:T(8,128)(2,1)}, bf16[2048,2560]{1,0:T(8,128)(2,1)}, u32[]{:S(2)}, u32[]{:S(2)}) collective-permute-start(bf16[2048,2560]{1,0:T(8,128)(2,1)} %get-tuple-element.85), channel_id=1, source_target_pairs={{0,3},{3,0},{1,2},{2,1},{4,7},{7,4},{5,6},{6,5}} | collective-permute-start | bytes 31457288 | tf_op jit(solution)/shard_map/ppermute | solution.py:196
  909.4 16.5 %collective-permute-start.14 = (bf16[2048,2560]{1,0:T(8,128)(2,1)}, bf16[2048,2560]{1,0:T(8,128)(2,1)}, u32[]{:S(2)}, u32[]{:S(2)}) collective-permute-start(bf16[2048,2560]{1,0:T(8,128)(2,1)} %collective-permute-done.9.b2), channel_id=1, source_target_pairs={{0,1},{1,0},{2,3},{3,2},{4,5},{5,4},{6,7},{7,6}} | collective-permute-start | bytes 31457288 | tf_op jit(solution)/shard_map/ppermute | solution.py:199
  917.9 182.5 %collective-permute-start.16 = (bf16[2048,2048]{1,0:T(8,128)(2,1)}, bf16[2048,2048]{1,0:T(8,128)(2,1)}, u32[]{:S(2)}, u32[]{:S(2)}) collective-permute-start(bf16[2048,2048]{1,0:T(8,128)(2,1)} %slice.78), channel_id=1, source_target_pairs={{0,3},{3,0},{1,2},{2,1},{4,7},{7,4},{5,6},{6,5}} | collective-permute-start | bytes 25165832 | tf_op jit(solution)/shard_map/ppermute | solution.py:196
  1100.4 13.5 collective-permute-start.17
  1106.6 137.8 %collective-permute-start.15 = (bf16[2048,1536]{1,0:T(8,128)(2,1)}, bf16[2048,1536]{1,0:T(8,128)(2,1)}, u32[]{:S(2)}, u32[]{:S(2)}) collective-permute-start(bf16[2048,1536]{1,0:T(8,128)(2,1)} %slice.77), channel_id=1, source_target_pairs={{0,3},{3,0},{1,2},{2,1},{4,7},{7,4},{5,6},{6,5}} | collective-permute-start | bytes 18874376 | tf_op jit(solution)/shard_map/ppermute | solution.py:196
  1244.4 10.5 collective-permute-start.18
  1249.2 92.6 %collective-permute-start.8 = (bf16[2048,1024]{1,0:T(8,128)(2,1)}, bf16[2048,1024]{1,0:T(8,128)(2,1)}, u32[]{:S(2)}, u32[]{:S(2)}) collective-permute-start(bf16[2048,1024]{1,0:T(8,128)(2,1)} %slice.73), channel_id=1, source_target_pairs={{0,3},{3,0},{1,2},{2,1},{4,7},{7,4},{5,6},{6,5}} | collective-permute-start | bytes 12582920 | tf_op jit(solution)/shard_map/ppermute | solution.py:196
  1341.8 53.7 %collective-permute-start.19 = (bf16[2048,1024]{1,0:T(8,128)(2,1)}, bf16[2048,1024]{1,0:T(8,128)(2,1)}, u32[]{:S(2)}, u32[]{:S(2)}) collective-permute-start(bf16[2048,1024]{1,0:T(8,128)(2,1)} %collective-permute-done.8.refs_2_), channel_id=1, source_target_pairs={{0,1},{1,0},{2,3},{3,2},{4,5},{5,4},{6,7},{7,6}} | collective-permute-start | bytes 12582920 | tf_op jit(solution)/shard_map/ppermute | solution.py:199
  1345.3 78.5 %collective-permute-start.7 = (bf16[2048,512]{1,0:T(8,128)(2,1)}, bf16[2048,512]{1,0:T(8,128)(2,1)}, u32[]{:S(2)}, u32[]{:S(2)}) collective-permute-start(bf16[2048,512]{1,0:T(8,128)(2,1)} %slice.72), channel_id=1, source_target_pairs={{0,3},{3,0},{1,2},{2,1},{4,7},{7,4},{5,6},{6,5}} | collective-permute-start | bytes 6291464 | tf_op jit(solution)/shard_map/ppermute | solution.py:196
  1395.5 3.4 copy-start
  1398.8 3.4 copy-start.1
  1423.8 4.4 collective-permute-start.20
  1425.5 25.2 %collective-permute-start.26 = (bf16[2048,256]{1,0:T(8,128)(2,1)S(1)}, bf16[2048,256]{1,0:T(8,128)(2,1)S(1)}, u32[]{:S(2)}, u32[]{:S(2)}) collective-permute-start(bf16[2048,256]{1,0:T(8,128)(2,1)S(1)} %slice.83), channel_id=1, source_target_pairs={{0,3},{3,0},{1,2},{2,1},{4,7},{7,4},{5,6},{6,5}} | collective-permute-start | bytes 3145736 | tf_op jit(solution)/shard_map/ppermute | solution.py:196
  1450.6 2.7 collective-permute-start.27
  1450.8 10.2 collective-permute-start.24
  1452.2 8.3 collective-permute-start.25
  1460.5 1.5 collective-permute-start.28
  1460.7 8.1 collective-permute-start.23
  1468.7 3.1 collective-permute-start.29
  1470.1 5.5 collective-permute-start.22
  1470.4 8.0 collective-permute-start.21
  1475.6 2.8 collective-permute-start.30
  1478.4 1.9 collective-permute-start.31

commit v6 on v5

v6 whole, which is shorter than its diff:
```python
import functools

import jax
import jax.numpy as jnp
from jax import lax
from jax.experimental import pallas as pl
from jax.experimental.pallas import tpu as pltpu
from jax.sharding import PartitionSpec as P


PIECES = (
    (14080, 256, 0, 4),
    (0, 256, 0, 16), (256, 768, 0, 16), (1024, 2560, 0, 16), (3584, 2560, 0, 16), (6144, 2560, 0, 16),
    (8704, 2048, 0, 16), (10752, 1536, 0, 16),
    (12288, 1024, 0, 16), (13312, 512, 0, 16), (13824, 256, 0, 16),
    (14080, 256, 4, 5), (14080, 256, 9, 4), (14080, 256, 13, 3),
)
TAIL = 8
LATE = 10
LATEST = 12
NEAR_AFTER = 5
FAR_VMEM = 24
MIB = 1024 * 1024


def matmul_cost(rows, depth, width, tiles):
    return pl.CostEstimate(
        flops=2 * rows * depth * width,
        bytes_accessed=2 * (rows * depth * tiles + depth * width + rows * width),
        transcendentals=0,
    )


def tile_of(start, width, most=512):
    for tn in (512, 256, 128):
        if tn <= most and start % tn == 0 and width % tn == 0:
            return tn


def whole_body(a0, a1, a2, a3, b0, b1, b2, b3, *rest):
    c_ref = rest[-1]
    total = jnp.dot(a0[...], b0[...], preferred_element_type=jnp.float32)
    total += jnp.dot(a1[...], b1[...], preferred_element_type=jnp.float32)
    total += jnp.dot(a2[...], b2[...], preferred_element_type=jnp.float32)
    total += jnp.dot(a3[...], b3[...], preferred_element_type=jnp.float32)
    c_ref[...] = total.astype(c_ref.dtype)


def whole_product(a_parts, b_own, b_pair, x_own, x_pair, c_prev, start, tm=512):
    rows, depth = a_parts[0].shape
    columns = b_own.shape[1]
    width = x_own.shape[1]
    tn = tile_of(start, width)
    first = start // tn
    b_whole = pl.BlockSpec((depth, tn), lambda n, m: (0, first + n))
    b_piece = pl.BlockSpec((depth, tn), lambda n, m: (0, n))
    in_specs = [pl.BlockSpec((tm, depth), lambda n, m: (m, 0))] * 4 + [b_whole, b_whole, b_piece, b_piece]
    args = [*a_parts, b_own, b_pair, x_own, x_pair]
    aliases = {}
    if c_prev is not None:
        in_specs.append(pl.BlockSpec(memory_space=pl.ANY))
        aliases = {len(args): 0}
        args.append(c_prev)
    return pl.pallas_call(
        whole_body,
        grid=(width // tn, rows // tm),
        in_specs=in_specs,
        out_specs=pl.BlockSpec((tm, tn), lambda n, m: (m, first + n)),
        out_shape=jax.ShapeDtypeStruct((rows, columns), jnp.bfloat16),
        input_output_aliases=aliases,
        cost_estimate=matmul_cost(rows, 4 * depth, width, width // tn),
        compiler_params=pltpu.CompilerParams(vmem_limit_bytes=62 * MIB),
    )(*args)


def near_body(a0, a1, b0, b1, *rest):
    s_ref = rest[-1]
    total = jnp.dot(a0[...], b0[...], preferred_element_type=jnp.float32)
    total += jnp.dot(a1[...], b1[...], preferred_element_type=jnp.float32)
    if len(rest) > 1:
        total += rest[0][...]
    s_ref[...] = total


def near_sums(a_parts, b_own, b_pair, more, start, width, tm=512, tn=256):
    rows, depth = a_parts[0].shape
    first = start // tn
    b_whole = pl.BlockSpec((depth, tn), lambda n, m: (0, first + n))
    in_specs = [pl.BlockSpec((tm, depth), lambda n, m: (m, 0))] * 2 + [b_whole, b_whole]
    args = [*a_parts, b_own, b_pair]
    if more is not None:
        in_specs.append(pl.BlockSpec((tm, tn), lambda n, m: (m, n)))
        args.append(more)
    return pl.pallas_call(
        near_body,
        grid=(width // tn, rows // tm),
        in_specs=in_specs,
        out_specs=pl.BlockSpec((tm, tn), lambda n, m: (m, n)),
        out_shape=jax.ShapeDtypeStruct((rows, width), jnp.float32),
        cost_estimate=matmul_cost(rows, 2 * depth, width, width // tn),
        compiler_params=pltpu.CompilerParams(vmem_limit_bytes=62 * MIB),
    )(*args)


def far_body(a_of, columns, summed, *refs):
    count = len(a_of)
    x_refs = refs[max(a_of) + 1 :]
    total = x_refs[count][...] if summed else None
    for which, column, x_ref in zip(a_of, columns, x_refs):
        depth = x_ref.shape[0]
        product = jnp.dot(
            refs[which][:, column : column + depth], x_ref[...], preferred_element_type=jnp.float32
        )
        total = product if total is None else total + product
    refs[-1][...] = total.astype(refs[-1].dtype)


def far_product(a_far, terms, sums, sums_start, c_prev, start, tm=1024):
    rows, depth = a_far[0].shape
    width = terms[0][1].shape[1]
    tn = tile_of(start, width, 256)
    first = start // tn
    sums_first = sums_start // tn
    used = sorted({i for i, _, _ in terms})
    args = [a_far[i] for i in used] + [x for _, x, _ in terms]
    in_specs = [pl.BlockSpec((tm, depth), lambda n, m: (m, 0)) for _ in used]
    in_specs += [pl.BlockSpec((x.shape[0], tn), lambda n, m: (0, n)) for _, x, _ in terms]
    aliases = {}
    if sums is not None:
        in_specs.append(pl.BlockSpec((tm, tn), lambda n, m: (m, sums_first + n)))
        args.append(sums)
    if c_prev is None:
        out_specs = pl.BlockSpec((tm, tn), lambda n, m: (m, n))
        out_shape = jax.ShapeDtypeStruct((rows, width), jnp.float32)
        if sums is not None and sums.shape == (rows, width):
            aliases = {len(args) - 1: 0}
    else:
        in_specs.append(pl.BlockSpec(memory_space=pl.ANY))
        aliases = {len(args): 0}
        args.append(c_prev)
        out_specs = pl.BlockSpec((tm, tn), lambda n, m: (m, first + n))
        out_shape = jax.ShapeDtypeStruct(c_prev.shape, c_prev.dtype)
    return pl.pallas_call(
        functools.partial(
            far_body, [used.index(i) for i, _, _ in terms], [row for _, _, row in terms], sums is not None
        ),
        grid=(width // tn, rows // tm),
        in_specs=in_specs,
        out_specs=out_specs,
        out_shape=out_shape,
        input_output_aliases=aliases,
        cost_estimate=matmul_cost(rows, sum(x.shape[0] for _, x, _ in terms), width, width // tn),
        compiler_params=pltpu.CompilerParams(vmem_limit_bytes=FAR_VMEM * MIB),
    )(*args)


def last_body(start, block, a_ref, x_ref, s_ref, c_prev, c_ref, held, sems):
    rows, width = held.shape
    copies = []
    for i in range(rows // block):
        part = pl.ds(i * block, block)
        total = s_ref[part, :] + jnp.dot(a_ref[part, :], x_ref[...], preferred_element_type=jnp.float32)
        held[part, :] = total.astype(held.dtype)
        copy = pltpu.make_async_copy(held.at[part, :], c_ref.at[part, pl.ds(start, width)], sems.at[i])
        copy.start()
        copies.append(copy)
    for copy in copies:
        copy.wait()


def last_product(a, x, sums, c_prev, start, block=512):
    rows = a.shape[0]
    depth, width = x.shape
    return pl.pallas_call(
        functools.partial(last_body, start, block),
        grid=(1,),
        in_specs=[
            pl.BlockSpec((rows, depth), lambda n: (0, 0)),
            pl.BlockSpec((depth, width), lambda n: (0, 0)),
            pl.BlockSpec((rows, width), lambda n: (0, 0)),
            pl.BlockSpec(memory_space=pl.ANY),
        ],
        out_specs=pl.BlockSpec(memory_space=pl.ANY),
        out_shape=jax.ShapeDtypeStruct(c_prev.shape, c_prev.dtype),
        scratch_shapes=[pltpu.VMEM((rows, width), c_prev.dtype), pltpu.SemaphoreType.DMA((rows // block,))],
        input_output_aliases={3: 0},
        cost_estimate=matmul_cost(rows, depth, width, 1),
        compiler_params=pltpu.CompilerParams(vmem_limit_bytes=FAR_VMEM * MIB),
        name="last",
    )(a, x, sums, c_prev)


def solution(mesh):
    across = [(0, 3), (3, 0), (1, 2), (2, 1)]
    beside = [(0, 1), (1, 0), (2, 3), (3, 2)]
    count = len(PIECES)
    last = count - 1

    def local_product(a_blk, b_blk):
        depth = b_blk.shape[0]
        row_id = lax.axis_index("row")
        first_core = lax.rem(row_id, 2) == 0
        aligned = lax.div(row_id, 2) == lax.axis_index("col")
        row_of = [row * depth // 16 for _, _, row, _ in PIECES]
        x_own = [None] * count
        x_pair = [None] * count

        def send(j, block):
            start, width, _, rows = PIECES[j]
            piece = lax.slice(block, (row_of[j], start), (row_of[j] + rows * depth // 16, start + width))
            x_own[j] = lax.ppermute(piece, "row", across)

        def pass_on(j, after):
            x_own[j], after = lax.optimization_barrier((x_own[j], after))
            x_pair[j] = lax.ppermute(x_own[j], "row", beside)
            return after

        def both(j):
            return [(0, x_own[j], row_of[j]), (1, x_pair[j], row_of[j])]

        for j in range(LATE):
            send(j, b_blk)
        a_recv = lax.ppermute(a_blk, "col", [(0, 1), (1, 0)])
        b_pair = lax.ppermute(b_blk, "row", beside)
        x_pair[0] = lax.ppermute(x_own[0], "row", beside)
        a_near = []
        a_far = []
        for side in (True, False):
            mine = first_core == side
            halves = [jnp.where(mine, a[:, :depth], a[:, depth:]) for a in (a_blk, a_recv)]
            a_near.append(jnp.where(aligned, halves[0], halves[1]))
            a_far.insert(0, jnp.where(aligned, halves[1], halves[0]))
        tail = PIECES[TAIL][0]
        end = PIECES[last][0]
        half = far_product(a_far, both(0), None, 0, None, end)
        c = None
        for j in range(1, LATE + 1):
            start = PIECES[j][0]
            if j == LATE - 2:
                b_late, c = lax.optimization_barrier((b_blk, c))
                for i in range(LATE, LATEST):
                    send(i, b_late)
            if j == LATE:
                b_late, c = lax.optimization_barrier((b_blk, c))
                for i in range(LATEST, count):
                    send(i, b_late)
            if j == 1:
                half = pass_on(j, half)
            else:
                c = pass_on(j, c)
            if j < TAIL:
                c = whole_product(a_near + a_far, b_blk, b_pair, x_own[j], x_pair[j], c, start)
            else:
                c = far_product(a_far, both(j), sums, start - tail, c, start)
            if j == 2:
                a_last, c = lax.optimization_barrier((a_far[1], c))
                a_last = a_last[:, row_of[last] :]
                a_last, c = lax.optimization_barrier((a_last, c))
            if j == NEAR_AFTER:
                a_near[0], c = lax.optimization_barrier((a_near[0], c))
                sums = near_sums(a_near, b_blk, b_pair, None, tail, end - tail)
                half = near_sums(a_near, b_blk, b_pair, half, end, b_blk.shape[1] - end)

        for j in range(LATE + 1, last):
            c = pass_on(j, c)
            half = far_product(a_far, both(j), half, 0, None, end)
            half, c = lax.optimization_barrier((half, c))
        half = pass_on(last, half)
        half = far_product(a_far, both(last)[:1], half, 0, None, end)
        c = last_product(a_last, x_pair[last], half, c, end)
        return c

    return jax.shard_map(
        local_product,
        mesh=mesh,
        in_specs=(P(("dp", "row"), "col"), P("row", "col")),
        out_specs=P(("dp", "row"), "col"),
        check_vma=False,
    )
```

time: 1480 us -> 1510 us (1.020)
  Pallas kernels: 619 us -> 642 us
  local copies, waits for them, and re-layouts: 62.5 us -> 78.2 us
    pallas_call x7 -> x9, Pallas kernels: 96.6 us -> 119 us  [the longest x2 70.8 us: near_sums(): pl.pallas_call(near_body, grid=(width // tn, rows // tm), in_specs=in_spe...]
    ppermute x30 -> x28, waiting for transfers between devices: 666 us -> 647 us  [the longest x14 590 us: send(): x_own[j] = lax.ppermute(piece, 'row', across)]
    ppermute x1, waiting for transfers between devices: 88.1 us -> 104 us  [local_product(): a_recv = lax.ppermute(a_blk, 'col', [(0, 1), (1, 0)])]
    slice x12 -> x13, local copies, waits for them, and re-layouts: 54.7 us -> 56.5 us  [the longest x12 54.9 us: send(): lax.slice(block, (row_of[j], start), (row_of[j] + rows * depth // 16, sta...]
  transfers between devices with their start and end apart: 32 -> 30, of which waited for: 21 -> 19; matrix products, arithmetic and copies ran while one was open for 5% -> 5% of each run, Pallas kernels for 42% -> 42%
where the time goes in v6:
time: 1510 us
  waiting for transfers between devices  751 us (50%)
  Pallas kernels  642 us (43%)
  local copies, waits for them, and re-layouts  78.2 us (5%)
  starting transfers between devices  24.4 us (2%)
  other arithmetic  17.8 us (1%)
    ppermute x14, waiting for transfers between devices, send(): x_own[j] = lax.ppermute(piece, 'row', across)  590 us
    pallas_call x7, Pallas kernels, whole_product(): pl.pallas_call(whole_body, grid=(width // tn, rows // tm), in_specs=in_sp...  521 us
    ppermute x1, waiting for transfers between devices, local_product(): a_recv = lax.ppermute(a_blk, 'col', [(0, 1), (1, 0)])  104 us
    pallas_call x2, Pallas kernels, near_sums(): pl.pallas_call(near_body, grid=(width // tn, rows // tm), in_specs=in_spe...  70.8 us
    ppermute x13, waiting for transfers between devices, pass_on(): x_pair[j] = lax.ppermute(x_own[j], 'row', beside)  56.7 us
    slice x12, local copies, waits for them, and re-layouts, send(): lax.slice(block, (row_of[j], start), (row_of[j] + rows * depth // 16, sta...  54.9 us
    pallas_call x7, Pallas kernels, far_product(): pl.pallas_call(functools.partial(far_body, [used.index(i) for i, _, _ in...  48 us
  transfers between devices with their start and end apart: 30, of which 19 were waited for; matrix products, arithmetic and copies ran while one was open for 5% of the time, Pallas kernels for 42%

profile of v6, /device:TPU:0, one launch (start us, length us, event | category | flops | bytes accessed | tf_op | source)
XLA Modules:
  0.0 1513.5 jit_solution(15321830093113916906)
XLA Ops:
  0.8 2.5 collective-permute-start
  3.3 22.2 %fusion = (bf16[2048,2560]{1,0:T(8,128)(2,1)}, bf16[2048,2560]{1,0:T(8,128)(2,1)}, bf16[2048,2560]{1,0:T(8,128)(2,1)}) fusion(bf16[2048,14336]{1,0:T(8,128)(2,1)} %b0.17), kind=kLoop, calls=%fused_computation.8 | loop fusion | bytes 62914560 | tf_op jit(solution)/shard_map/slice | solution.py:210
  30.9 3.8 slice.65
  34.7 223.9 %collective-permute-done.4.refs_2_ = bf16[512,256]{1,0:T(8,128)(2,1)S(1)} collective-permute-done((bf16[512,256]{1,0:T(8,128)(2,1)S(1)}, bf16[512,256]{1,0:T(8,128)(2,1)S(1)}, u32[]{:S(2)}, u32[]{:S(2)}) %collective-permute-start.4) | collective-permute-done | bytes 262176 | tf_op jit(solution)/shard_map/ppermute | solution.py:211
  258.7 2.1 collective-permute-start.2
  260.8 103.7 %collective-permute-done = bf16[2048,4096]{1,0:T(8,128)(2,1)} collective-permute-done((bf16[2048,4096]{1,0:T(8,128)(2,1)}, bf16[2048,4096]{1,0:T(8,128)(2,1)}, u32[]{:S(2)}, u32[]{:S(2)}) %collective-permute-start) | collective-permute-done | bytes 16777248 | tf_op jit(solution)/shard_map/ppermute | solution.py:223
  364.5 17.8 %broadcast_select_fusion.4 = (bf16[2048,2048]{1,0:T(8,128)(2,1)S(1)}, bf16[2048,2048]{1,0:T(8,128)(2,1)}, bf16[2048,2048]{1,0:T(8,128)(2,1)}, bf16[2048,2048]{1,0:T(8,128)(2,1)S(1)}) fusion(pred[]{:T(512)S(6)} %eq.9, bf16[2048,4096]{1,0:T(8,128)(2,1)} %param.2, pred[]{:T(512)S(6)} %eq.11, bf16[2048,4096]{1,0:T(8,128)(2,1)} %collective-permute-done, pred[]{:T(512)S(6)} %eq.10), kind=kLoop, calls=%fused_computation.4 | loop fusion | flops 33554432 | bytes 67108864 | tf_op jit(solution)/shard_map/jit(_where)/select_n | solution.py:232
  383.8 1.8 copy-done
  385.6 2.6 copy-done.3
  390.0 2.3 collective-permute-done.6.b3
  393.3 17.0 %shard_map.29.rest_0_ = bf16[2048,14336]{1,0:T(8,128)(2,1)} custom-call(bf16[2048,2048]{1,0:T(8,128)(2,1)} %get-tuple-element.58.a0, bf16[2048,2048]{1,0:T(8,128)(2,1)} %get-tuple-element.90.a1, bf16[2048,2048]{1,0:T(8,128)(2,1)} %copy-done, bf16[2048,2048]{1,0:T(8,128)(2,1)} %copy-done.3, bf16[2048,14336]{1,0:T(8,128)(2,1)} %b0.17, ...), custom_call_target="tpu_custom_call" | custom-call | flops 8589934592 | bytes 38797312 | tf_op jit(solution)/shard_map/pallas_call | solution.py:64
  410.7 5.6 collective-permute-done.7.b3
  416.3 42.7 %shard_map.30.rest_0_ = bf16[2048,14336]{1,0:T(8,128)(2,1)} custom-call(bf16[2048,2048]{1,0:T(8,128)(2,1)} %get-tuple-element.58.a0, bf16[2048,2048]{1,0:T(8,128)(2,1)} %get-tuple-element.90.a1, bf16[2048,2048]{1,0:T(8,128)(2,1)} %copy-done, bf16[2048,2048]{1,0:T(8,128)(2,1)} %copy-done.3, bf16[2048,14336]{1,0:T(8,128)(2,1)} %b0.17, ...), custom_call_target="tpu_custom_call", output_to_operand_aliasing={{}: (8, {})} | custom-call | flops 25769803776 | bytes 116391936 | tf_op jit(solution)/shard_map/pallas_call | solution.py:64
  462.4 14.7 collective-permute-done.13.b3
  477.1 104.3 %shard_map.31.rest_0_ = bf16[2048,14336]{1,0:T(8,128)(2,1)} custom-call(bf16[2048,2048]{1,0:T(8,128)(2,1)} %get-tuple-element.58.a0, bf16[2048,2048]{1,0:T(8,128)(2,1)} %get-tuple-element.90.a1, bf16[2048,2048]{1,0:T(8,128)(2,1)} %copy-done, bf16[2048,2048]{1,0:T(8,128)(2,1)} %copy-done.3, bf16[2048,14336]{1,0:T(8,128)(2,1)} %b0.17, ...), custom_call_target="tpu_custom_call", output_to_operand_aliasing={{}: (8, {})} | custom-call | flops 85899345920 | bytes 220200960 | tf_op jit(solution)/shard_map/pallas_call | solution.py:64
  581.3 107.3 %collective-permute-done.11.b2 = bf16[2048,2560]{1,0:T(8,128)(2,1)} collective-permute-done((bf16[2048,2560]{1,0:T(8,128)(2,1)}, bf16[2048,2560]{1,0:T(8,128)(2,1)}, u32[]{:S(2)}, u32[]{:S(2)}) %collective-permute-start.11) | collective-permute-done | bytes 10485792 | tf_op jit(solution)/shard_map/ppermute | solution.py:211
  688.7 1.7 collective-permute-start.10
  690.4 14.7 collective-permute-done.14.b3
  705.1 104.3 %shard_map.32.rest_0_ = bf16[2048,14336]{1,0:T(8,128)(2,1)} custom-call(bf16[2048,2048]{1,0:T(8,128)(2,1)} %get-tuple-element.58.a0, bf16[2048,2048]{1,0:T(8,128)(2,1)} %get-tuple-element.90.a1, bf16[2048,2048]{1,0:T(8,128)(2,1)} %copy-done, bf16[2048,2048]{1,0:T(8,128)(2,1)} %copy-done.3, bf16[2048,14336]{1,0:T(8,128)(2,1)} %b0.17, ...), custom_call_target="tpu_custom_call", output_to_operand_aliasing={{}: (8, {})} | custom-call | flops 85899345920 | bytes 220200960 | tf_op jit(solution)/shard_map/pallas_call | solution.py:64
  809.4 106.9 %collective-permute-done.10.b2 = bf16[2048,2560]{1,0:T(8,128)(2,1)} collective-permute-done((bf16[2048,2560]{1,0:T(8,128)(2,1)}, bf16[2048,2560]{1,0:T(8,128)(2,1)}, u32[]{:S(2)}, u32[]{:S(2)}) %collective-permute-start.10) | collective-permute-done | bytes 10485792 | tf_op jit(solution)/shard_map/ppermute | solution.py:211
  916.6 8.3 slice.75
  926.3 6.4 collective-permute-done.15.b3
  932.7 104.4 %shard_map.33.rest_0_ = bf16[2048,14336]{1,0:T(8,128)(2,1)} custom-call(bf16[2048,2048]{1,0:T(8,128)(2,1)} %get-tuple-element.58.a0, bf16[2048,2048]{1,0:T(8,128)(2,1)} %get-tuple-element.90.a1, bf16[2048,2048]{1,0:T(8,128)(2,1)} %copy-done, bf16[2048,2048]{1,0:T(8,128)(2,1)} %copy-done.3, bf16[2048,14336]{1,0:T(8,128)(2,1)} %b0.17, ...), custom_call_target="tpu_custom_call", output_to_operand_aliasing={{}: (8, {})} | custom-call | flops 85899345920 | bytes 220200960 | tf_op jit(solution)/shard_map/pallas_call | solution.py:64
  1037.1 70.5 %collective-permute-done.17.b2 = bf16[2048,2048]{1,0:T(8,128)(2,1)} collective-permute-done((bf16[2048,2048]{1,0:T(8,128)(2,1)}, bf16[2048,2048]{1,0:T(8,128)(2,1)}, u32[]{:S(2)}, u32[]{:S(2)}) %collective-permute-start.17) | collective-permute-done | bytes 8388640 | tf_op jit(solution)/shard_map/ppermute | solution.py:211
  1107.7 5.8 slice.74
  1113.5 1.7 collective-permute-start.16
  1115.2 5.9 collective-permute-done.18.b3
  1121.1 84.4 %shard_map.34.rest_0_ = bf16[2048,14336]{1,0:T(8,128)(2,1)} custom-call(bf16[2048,2048]{1,0:T(8,128)(2,1)} %get-tuple-element.58.a0, bf16[2048,2048]{1,0:T(8,128)(2,1)} %get-tuple-element.90.a1, bf16[2048,2048]{1,0:T(8,128)(2,1)} %copy-done, bf16[2048,2048]{1,0:T(8,128)(2,1)} %copy-done.3, bf16[2048,14336]{1,0:T(8,128)(2,1)} %b0.17, ...), custom_call_target="tpu_custom_call", output_to_operand_aliasing={{}: (8, {})} | custom-call | flops 68719476736 | bytes 176160768 | tf_op jit(solution)/shard_map/pallas_call | solution.py:64
  1205.5 45.6 %collective-permute-done.16.b2 = bf16[2048,1536]{1,0:T(8,128)(2,1)} collective-permute-done((bf16[2048,1536]{1,0:T(8,128)(2,1)}, bf16[2048,1536]{1,0:T(8,128)(2,1)}, u32[]{:S(2)}, u32[]{:S(2)}) %collective-permute-start.16) | collective-permute-done | bytes 6291488 | tf_op jit(solution)/shard_map/ppermute | solution.py:211
  1251.5 4.6 slice.70
  1257.6 4.1 collective-permute-done.19.b3
  1261.6 64.5 %shard_map.35.refs_5_ = bf16[2048,14336]{1,0:T(8,128)(2,1)} custom-call(bf16[2048,2048]{1,0:T(8,128)(2,1)} %get-tuple-element.58.a0, bf16[2048,2048]{1,0:T(8,128)(2,1)} %get-tuple-element.90.a1, bf16[2048,2048]{1,0:T(8,128)(2,1)} %copy-done, bf16[2048,2048]{1,0:T(8,128)(2,1)} %copy-done.3, bf16[2048,14336]{1,0:T(8,128)(2,1)} %b0.17, ...), custom_call_target="tpu_custom_call", output_to_operand_aliasing={{}: (8, {})} | custom-call | flops 51539607552 | bytes 132120576 | tf_op jit(solution)/shard_map/pallas_call | solution.py:64
  1326.1 22.8 %collective-permute-done.9.refs_2_ = bf16[2048,1024]{1,0:T(8,128)(2,1)} collective-permute-done((bf16[2048,1024]{1,0:T(8,128)(2,1)}, bf16[2048,1024]{1,0:T(8,128)(2,1)}, u32[]{:S(2)}, u32[]{:S(2)}) %collective-permute-start.9) | collective-permute-done | bytes 4194336 | tf_op jit(solution)/shard_map/ppermute | solution.py:211
  1349.1 3.0 slice.69
  1353.8 59.7 %shard_map.36.refs_4_ = f32[2048,1792]{1,0:T(8,128)} custom-call(bf16[2048,2048]{1,0:T(8,128)(2,1)} %get-tuple-element.58.a0, bf16[2048,2048]{1,0:T(8,128)(2,1)} %get-tuple-element.90.a1, bf16[2048,14336]{1,0:T(8,128)(2,1)} %b0.17, bf16[2048,14336]{1,0:T(8,128)(2,1)} %collective-permute-done.1.b1), custom_call_target="tpu_custom_call" | custom-call | flops 30064771072 | bytes 139460608 | tf_op jit(solution)/shard_map/pallas_call | solution.py:94
  1413.6 3.4 copy-done.1
  1416.9 3.4 copy-done.4
  1420.3 21.6 %shard_map.37.refs_5_ = bf16[2048,14336]{1,0:T(8,128)(2,1)} custom-call(bf16[2048,2048]{1,0:T(8,128)(2,1)S(1)} %copy-done.1, bf16[2048,2048]{1,0:T(8,128)(2,1)S(1)} %copy-done.4, bf16[2048,1024]{1,0:T(8,128)(2,1)} %collective-permute-done.9.refs_2_, bf16[2048,1024]{1,0:T(8,128)(2,1)} %collective-permute-done.20.refs_3_, ...), custom_call_target="tpu_custom_call", output_to_operand_aliasing={{}: (5, {})} | custom-call | flops 17179869184 | bytes 79691776 | tf_op jit(solution)/shard_map/pallas_call | solution.py:143
  1443.7 2.6 collective-permute-done.21.refs_3_
  1446.3 11.8 shard_map.38.refs_5_
  1458.1 10.2 collective-permute-done.25.refs_2_
  1473.1 6.7 shard_map.39.c_prev
  1480.2 11.1 shard_map.40.refs_4_
  1491.3 3.4 copy-done.2
  1494.7 3.4 copy-done.5
  1499.7 2.9 shard_map.41.refs_4_
  1504.4 2.5 shard_map.42.refs_2_
  1506.9 3.3 collective-permute-done.22.refs_1_
  (63 shorter events, 33.5 us)
Async XLA Ops:
  0.0 393.3 %collective-permute-start.1 = (bf16[2048,14336]{1,0:T(8,128)(2,1)}, bf16[2048,14336]{1,0:T(8,128)(2,1)}, u32[]{:S(2)}, u32[]{:S(2)}) collective-permute-start(bf16[2048,14336]{1,0:T(8,128)(2,1)} %b0.17), channel_id=1, source_target_pairs={{0,1},{1,0},{2,3},{3,2},{4,5},{5,4},{6,7},{7,6}} | collective-permute-start | bytes 176160768 | tf_op jit(solution)/shard_map/ppermute | solution.py:224
  0.8 363.7 %collective-permute-start = (bf16[2048,4096]{1,0:T(8,128)(2,1)}, bf16[2048,4096]{1,0:T(8,128)(2,1)}, u32[]{:S(2)}, u32[]{:S(2)}) collective-permute-start(bf16[2048,4096]{1,0:T(8,128)(2,1)} %param.2), channel_id=1, source_target_pairs={{0,4},{4,0},{1,5},{5,1},{2,6},{6,2},{3,7},{7,3}} | collective-permute-start | bytes 50331656 | tf_op jit(solution)/shard_map/ppermute | solution.py:223
  25.6 435.0 %collective-permute-start.12 = (bf16[2048,2560]{1,0:T(8,128)(2,1)}, bf16[2048,2560]{1,0:T(8,128)(2,1)}, u32[]{:S(2)}, u32[]{:S(2)}) collective-permute-start(bf16[2048,2560]{1,0:T(8,128)(2,1)} %get-tuple-element.85), channel_id=1, source_target_pairs={{0,3},{3,0},{1,2},{2,1},{4,7},{7,4},{5,6},{6,5}} | collective-permute-start | bytes 31457288 | tf_op jit(solution)/shard_map/ppermute | solution.py:211
  27.9 230.8 %collective-permute-start.4 = (bf16[512,256]{1,0:T(8,128)(2,1)S(1)}, bf16[512,256]{1,0:T(8,128)(2,1)S(1)}, u32[]{:S(2)}, u32[]{:S(2)}) collective-permute-start(bf16[512,256]{1,0:T(8,128)(2,1)S(1)} %slice.67), channel_id=1, source_target_pairs={{0,3},{3,0},{1,2},{2,1},{4,7},{7,4},{5,6},{6,5}} | collective-permute-start | bytes 786440 | tf_op jit(solution)/shard_map/ppermute | solution.py:211
  29.6 359.9 %collective-permute-start.3 = (bf16[2048,256]{1,0:T(8,128)(2,1)S(1)}, bf16[2048,256]{1,0:T(8,128)(2,1)S(1)}, u32[]{:S(2)}, u32[]{:S(2)}) collective-permute-start(bf16[2048,256]{1,0:T(8,128)(2,1)S(1)} %slice.66), channel_id=1, source_target_pairs={{0,3},{3,0},{1,2},{2,1},{4,7},{7,4},{5,6},{6,5}} | collective-permute-start | bytes 3145736 | tf_op jit(solution)/shard_map/ppermute | solution.py:211
  258.7 151.6 %collective-permute-start.2 = (bf16[2048,768]{1,0:T(8,128)(2,1)}, bf16[2048,768]{1,0:T(8,128)(2,1)}, u32[]{:S(2)}, u32[]{:S(2)}) collective-permute-start(bf16[2048,768]{1,0:T(8,128)(2,1)} %slice.65), channel_id=1, source_target_pairs={{0,3},{3,0},{1,2},{2,1},{4,7},{7,4},{5,6},{6,5}} | collective-permute-start | bytes 9437192 | tf_op jit(solution)/shard_map/ppermute | solution.py:211
  364.5 17.8 %collective-permute-start.5 = (bf16[512,256]{1,0:T(8,128)(2,1)S(1)}, bf16[512,256]{1,0:T(8,128)(2,1)S(1)}, u32[]{:S(2)}, u32[]{:S(2)}) collective-permute-start(bf16[512,256]{1,0:T(8,128)(2,1)S(1)} %collective-permute-done.4.refs_2_), channel_id=1, source_target_pairs={{0,1},{1,0},{2,3},{3,2},{4,5},{5,4},{6,7},{7,6}} | collective-permute-start | bytes 786440 | tf_op jit(solution)/shard_map/ppermute | solution.py:225
  382.3 3.3 copy-start
  382.3 5.8 copy-start.3
  388.2 1.3 copy-start.7
  389.5 3.8 copy-start.8
  389.5 2.8 collective-permute-start.6
  392.3 1.0 copy-start.9
  410.3 6.0 collective-permute-start.7
  460.5 16.5 %collective-permute-start.13 = (bf16[2048,2560]{1,0:T(8,128)(2,1)}, bf16[2048,2560]{1,0:T(8,128)(2,1)}, u32[]{:S(2)}, u32[]{:S(2)}) collective-permute-start(bf16[2048,2560]{1,0:T(8,128)(2,1)} %collective-permute-done.12.b2), channel_id=1, source_target_pairs={{0,1},{1,0},{2,3},{3,2},{4,5},{5,4},{6,7},{7,6}} | collective-permute-start | bytes 31457288 | tf_op jit(solution)/shard_map/ppermute | solution.py:215
  460.9 227.7 %collective-permute-start.11 = (bf16[2048,2560]{1,0:T(8,128)(2,1)}, bf16[2048,2560]{1,0:T(8,128)(2,1)}, u32[]{:S(2)}, u32[]{:S(2)}) collective-permute-start(bf16[2048,2560]{1,0:T(8,128)(2,1)} %get-tuple-element.86), channel_id=1, source_target_pairs={{0,3},{3,0},{1,2},{2,1},{4,7},{7,4},{5,6},{6,5}} | collective-permute-start | bytes 31457288 | tf_op jit(solution)/shard_map/ppermute | solution.py:211
  688.6 16.5 %collective-permute-start.14 = (bf16[2048,2560]{1,0:T(8,128)(2,1)}, bf16[2048,2560]{1,0:T(8,128)(2,1)}, u32[]{:S(2)}, u32[]{:S(2)}) collective-permute-start(bf16[2048,2560]{1,0:T(8,128)(2,1)} %collective-permute-done.11.b2), channel_id=1, source_target_pairs={{0,1},{1,0},{2,3},{3,2},{4,5},{5,4},{6,7},{7,6}} | collective-permute-start | bytes 31457288 | tf_op jit(solution)/shard_map/ppermute | solution.py:215
  688.7 227.5 %collective-permute-start.10 = (bf16[2048,2560]{1,0:T(8,128)(2,1)}, bf16[2048,2560]{1,0:T(8,128)(2,1)}, u32[]{:S(2)}, u32[]{:S(2)}) collective-permute-start(bf16[2048,2560]{1,0:T(8,128)(2,1)} %get-tuple-element.87), channel_id=1, source_target_pairs={{0,3},{3,0},{1,2},{2,1},{4,7},{7,4},{5,6},{6,5}} | collective-permute-start | bytes 31457288 | tf_op jit(solution)/shard_map/ppermute | solution.py:211
  916.2 16.5 %collective-permute-start.15 = (bf16[2048,2560]{1,0:T(8,128)(2,1)}, bf16[2048,2560]{1,0:T(8,128)(2,1)}, u32[]{:S(2)}, u32[]{:S(2)}) collective-permute-start(bf16[2048,2560]{1,0:T(8,128)(2,1)} %collective-permute-done.10.b2), channel_id=1, source_target_pairs={{0,1},{1,0},{2,3},{3,2},{4,5},{5,4},{6,7},{7,6}} | collective-permute-start | bytes 31457288 | tf_op jit(solution)/shard_map/ppermute | solution.py:215
  924.8 182.7 %collective-permute-start.17 = (bf16[2048,2048]{1,0:T(8,128)(2,1)}, bf16[2048,2048]{1,0:T(8,128)(2,1)}, u32[]{:S(2)}, u32[]{:S(2)}) collective-permute-start(bf16[2048,2048]{1,0:T(8,128)(2,1)} %slice.75), channel_id=1, source_target_pairs={{0,3},{3,0},{1,2},{2,1},{4,7},{7,4},{5,6},{6,5}} | collective-permute-start | bytes 25165832 | tf_op jit(solution)/shard_map/ppermute | solution.py:211
  1107.6 13.5 collective-permute-start.18
  1113.5 137.6 %collective-permute-start.16 = (bf16[2048,1536]{1,0:T(8,128)(2,1)}, bf16[2048,1536]{1,0:T(8,128)(2,1)}, u32[]{:S(2)}, u32[]{:S(2)}) collective-permute-start(bf16[2048,1536]{1,0:T(8,128)(2,1)} %slice.74), channel_id=1, source_target_pairs={{0,3},{3,0},{1,2},{2,1},{4,7},{7,4},{5,6},{6,5}} | collective-permute-start | bytes 18874376 | tf_op jit(solution)/shard_map/ppermute | solution.py:211
  1251.1 10.5 collective-permute-start.19
  1256.1 92.9 %collective-permute-start.9 = (bf16[2048,1024]{1,0:T(8,128)(2,1)}, bf16[2048,1024]{1,0:T(8,128)(2,1)}, u32[]{:S(2)}, u32[]{:S(2)}) collective-permute-start(bf16[2048,1024]{1,0:T(8,128)(2,1)} %slice.70), channel_id=1, source_target_pairs={{0,3},{3,0},{1,2},{2,1},{4,7},{7,4},{5,6},{6,5}} | collective-permute-start | bytes 12582920 | tf_op jit(solution)/shard_map/ppermute | solution.py:211
  1348.9 64.6 %collective-permute-start.20 = (bf16[2048,1024]{1,0:T(8,128)(2,1)}, bf16[2048,1024]{1,0:T(8,128)(2,1)}, u32[]{:S(2)}, u32[]{:S(2)}) collective-permute-start(bf16[2048,1024]{1,0:T(8,128)(2,1)} %collective-permute-done.9.refs_2_), channel_id=1, source_target_pairs={{0,1},{1,0},{2,3},{3,2},{4,5},{5,4},{6,7},{7,6}} | collective-permute-start | bytes 12582920 | tf_op jit(solution)/shard_map/ppermute | solution.py:215
  1352.1 89.8 %collective-permute-start.8 = (bf16[2048,512]{1,0:T(8,128)(2,1)}, bf16[2048,512]{1,0:T(8,128)(2,1)}, u32[]{:S(2)}, u32[]{:S(2)}) collective-permute-start(bf16[2048,512]{1,0:T(8,128)(2,1)} %slice.69), channel_id=1, source_target_pairs={{0,3},{3,0},{1,2},{2,1},{4,7},{7,4},{5,6},{6,5}} | collective-permute-start | bytes 6291464 | tf_op jit(solution)/shard_map/ppermute | solution.py:211
  1413.6 3.4 copy-start.1
  1416.9 3.4 copy-start.4
  1441.9 4.4 collective-permute-start.21
  1443.4 24.9 %collective-permute-start.25 = (bf16[2048,256]{1,0:T(8,128)(2,1)S(1)}, bf16[2048,256]{1,0:T(8,128)(2,1)S(1)}, u32[]{:S(2)}, u32[]{:S(2)}) collective-permute-start(bf16[2048,256]{1,0:T(8,128)(2,1)S(1)} %slice.79), channel_id=1, source_target_pairs={{0,3},{3,0},{1,2},{2,1},{4,7},{7,4},{5,6},{6,5}} | collective-permute-start | bytes 3145736 | tf_op jit(solution)/shard_map/ppermute | solution.py:211
  1468.3 4.8 collective-permute-start.26
  1469.7 10.1 collective-permute-start.24
  1471.4 31.2 %collective-permute-start.23 = (bf16[512,256]{1,0:T(8,128)(2,1)}, bf16[512,256]{1,0:T(8,128)(2,1)}, u32[]{:S(2)}, u32[]{:S(2)}) collective-permute-start(bf16[512,256]{1,0:T(8,128)(2,1)} %slice.77), channel_id=1, source_target_pairs={{0,3},{3,0},{1,2},{2,1},{4,7},{7,4},{5,6},{6,5}} | collective-permute-start | bytes 786440 | tf_op jit(solution)/shard_map/ppermute | solution.py:211
  1479.8 11.5 collective-permute-start.27
  1491.3 3.4 copy-start.2
  1494.7 3.4 copy-start.5
  1498.1 1.6 copy-start.6
  1502.6 1.8 collective-permute-start.28
  1503.6 6.6 collective-permute-start.22
  1510.3 1.5 collective-permute-start.29

commit v7 on v6

--- a/solution.py
+++ b/solution.py
@@ -9,11 +9,11 @@
 
 
 PIECES = (
-    (14080, 256, 0, 4),
+    (14080, 256, 0, 3),
     (0, 256, 0, 16), (256, 768, 0, 16), (1024, 2560, 0, 16), (3584, 2560, 0, 16), (6144, 2560, 0, 16),
     (8704, 2048, 0, 16), (10752, 1536, 0, 16),
     (12288, 1024, 0, 16), (13312, 512, 0, 16), (13824, 256, 0, 16),
-    (14080, 256, 4, 5), (14080, 256, 9, 4), (14080, 256, 13, 3),
+    (14080, 256, 3, 6), (14080, 256, 9, 4), (14080, 256, 13, 3),
 )
 TAIL = 8
 LATE = 10
@@ -231,6 +231,7 @@
             a_near.append(jnp.where(aligned, halves[0], halves[1]))
             a_far.insert(0, jnp.where(aligned, halves[1], halves[0]))
         tail = PIECES[TAIL][0]
+        before = PIECES[LATE][0]
         end = PIECES[last][0]
         half = far_product(a_far, both(0), None, 0, None, end)
         c = None
@@ -251,14 +252,16 @@
             if j < TAIL:
                 c = whole_product(a_near + a_far, b_blk, b_pair, x_own[j], x_pair[j], c, start)
             else:
-                c = far_product(a_far, both(j), sums, start - tail, c, start)
+                near, near_start = (sums_before, before) if j == LATE else (sums, tail)
+                c = far_product(a_far, both(j), near, start - near_start, c, start)
             if j == 2:
                 a_last, c = lax.optimization_barrier((a_far[1], c))
                 a_last = a_last[:, row_of[last] :]
                 a_last, c = lax.optimization_barrier((a_last, c))
             if j == NEAR_AFTER:
                 a_near[0], c = lax.optimization_barrier((a_near[0], c))
-                sums = near_sums(a_near, b_blk, b_pair, None, tail, end - tail)
+                sums = near_sums(a_near, b_blk, b_pair, None, tail, before - tail)
+                sums_before = near_sums(a_near, b_blk, b_pair, None, before, end - before)
                 half = near_sums(a_near, b_blk, b_pair, half, end, b_blk.shape[1] - end)
 
         for j in range(LATE + 1, last):

time: 1510 us -> 1530 us (1.013)
    pallas_call x2 -> x3, Pallas kernels: 70.8 us -> 72.8 us  [near_sums(): pl.pallas_call(near_body, grid=(width // tn, rows // tm), in_specs=in_spe...]
where the time goes in v7:
time: 1530 us; the launch traced here: 1520 us
  waiting for transfers between devices  752 us (49%)
  Pallas kernels  644 us (42%)
  local copies, waits for them, and re-layouts  86.5 us (6%)
  starting transfers between devices  23.8 us (2%)
  other arithmetic  17.8 us (1%)
    ppermute x14, waiting for transfers between devices, send(): x_own[j] = lax.ppermute(piece, 'row', across)  590 us
    pallas_call x7, Pallas kernels, whole_product(): pl.pallas_call(whole_body, grid=(width // tn, rows // tm), in_specs=in_sp...  521 us
    ppermute x1, waiting for transfers between devices, local_product(): a_recv = lax.ppermute(a_blk, 'col', [(0, 1), (1, 0)])  105 us
    pallas_call x3, Pallas kernels, near_sums(): pl.pallas_call(near_body, grid=(width // tn, rows // tm), in_specs=in_spe...  72.8 us
    ppermute x13, waiting for transfers between devices, pass_on(): x_pair[j] = lax.ppermute(x_own[j], 'row', beside)  56.9 us
    slice x12, local copies, waits for them, and re-layouts, send(): lax.slice(block, (row_of[j], start), (row_of[j] + rows * depth // 16, sta...  54.9 us
    pallas_call x7, Pallas kernels, far_product(): pl.pallas_call(functools.partial(far_body, [used.index(i) for i, _, _ in...  48.5 us
  transfers between devices with their start and end apart: 30, of which 19 were waited for; matrix products, arithmetic and copies ran while one was open for 5% of the time, Pallas kernels for 42%

profile of v7, /device:TPU:0, one launch (start us, length us, event | category | flops | bytes accessed | tf_op | source)
XLA Modules:
  0.0 1524.6 jit_solution(8357636014594487662)
XLA Ops:
  0.8 2.5 collective-permute-start
  3.3 22.2 %fusion = (bf16[2048,2560]{1,0:T(8,128)(2,1)}, bf16[2048,2560]{1,0:T(8,128)(2,1)}, bf16[2048,2560]{1,0:T(8,128)(2,1)}) fusion(bf16[2048,14336]{1,0:T(8,128)(2,1)} %b0.19), kind=kLoop, calls=%fused_computation.8 | loop fusion | bytes 62914560 | tf_op jit(solution)/shard_map/slice | solution.py:210
  30.9 3.8 slice.65
  34.7 222.6 %collective-permute-done.4.refs_2_ = bf16[384,256]{1,0:T(8,128)(2,1)S(1)} collective-permute-done((bf16[384,256]{1,0:T(8,128)(2,1)S(1)}, bf16[384,256]{1,0:T(8,128)(2,1)S(1)}, u32[]{:S(2)}, u32[]{:S(2)}) %collective-permute-start.4) | collective-permute-done | bytes 196640 | tf_op jit(solution)/shard_map/ppermute | solution.py:211
  257.3 2.1 collective-permute-start.2
  259.4 105.1 %collective-permute-done = bf16[2048,4096]{1,0:T(8,128)(2,1)} collective-permute-done((bf16[2048,4096]{1,0:T(8,128)(2,1)}, bf16[2048,4096]{1,0:T(8,128)(2,1)}, u32[]{:S(2)}, u32[]{:S(2)}) %collective-permute-start) | collective-permute-done | bytes 16777248 | tf_op jit(solution)/shard_map/ppermute | solution.py:223
  364.5 17.8 %broadcast_select_fusion.4 = (bf16[2048,2048]{1,0:T(8,128)(2,1)S(1)}, bf16[2048,2048]{1,0:T(8,128)(2,1)}, bf16[2048,2048]{1,0:T(8,128)(2,1)}, bf16[2048,2048]{1,0:T(8,128)(2,1)S(1)}) fusion(pred[]{:T(512)S(6)} %eq.9, bf16[2048,4096]{1,0:T(8,128)(2,1)} %param.2, pred[]{:T(512)S(6)} %eq.11, bf16[2048,4096]{1,0:T(8,128)(2,1)} %collective-permute-done, pred[]{:T(512)S(6)} %eq.10), kind=kLoop, calls=%fused_computation.4 | loop fusion | flops 33554432 | bytes 67108864 | tf_op jit(solution)/shard_map/jit(_where)/select_n | solution.py:232
  385.6 2.5 copy-done.4
  390.0 2.3 collective-permute-done.6.b3
  393.2 16.9 %shard_map.29.rest_0_ = bf16[2048,14336]{1,0:T(8,128)(2,1)} custom-call(bf16[2048,2048]{1,0:T(8,128)(2,1)} %get-tuple-element.58.a0, bf16[2048,2048]{1,0:T(8,128)(2,1)} %get-tuple-element.90.a1, bf16[2048,2048]{1,0:T(8,128)(2,1)} %copy-done, bf16[2048,2048]{1,0:T(8,128)(2,1)} %copy-done.4, bf16[2048,14336]{1,0:T(8,128)(2,1)} %b0.19, ...), custom_call_target="tpu_custom_call" | custom-call | flops 8589934592 | bytes 38797312 | tf_op jit(solution)/shard_map/pallas_call | solution.py:64
  410.5 5.6 collective-permute-done.7.b3
  416.2 42.7 %shard_map.30.rest_0_ = bf16[2048,14336]{1,0:T(8,128)(2,1)} custom-call(bf16[2048,2048]{1,0:T(8,128)(2,1)} %get-tuple-element.58.a0, bf16[2048,2048]{1,0:T(8,128)(2,1)} %get-tuple-element.90.a1, bf16[2048,2048]{1,0:T(8,128)(2,1)} %copy-done, bf16[2048,2048]{1,0:T(8,128)(2,1)} %copy-done.4, bf16[2048,14336]{1,0:T(8,128)(2,1)} %b0.19, ...), custom_call_target="tpu_custom_call", output_to_operand_aliasing={{}: (8, {})} | custom-call | flops 25769803776 | bytes 116391936 | tf_op jit(solution)/shard_map/pallas_call | solution.py:64
  462.3 14.7 collective-permute-done.13.b3
  477.0 104.3 %shard_map.31.rest_0_ = bf16[2048,14336]{1,0:T(8,128)(2,1)} custom-call(bf16[2048,2048]{1,0:T(8,128)(2,1)} %get-tuple-element.58.a0, bf16[2048,2048]{1,0:T(8,128)(2,1)} %get-tuple-element.90.a1, bf16[2048,2048]{1,0:T(8,128)(2,1)} %copy-done, bf16[2048,2048]{1,0:T(8,128)(2,1)} %copy-done.4, bf16[2048,14336]{1,0:T(8,128)(2,1)} %b0.19, ...), custom_call_target="tpu_custom_call", output_to_operand_aliasing={{}: (8, {})} | custom-call | flops 85899345920 | bytes 220200960 | tf_op jit(solution)/shard_map/pallas_call | solution.py:64
  581.2 107.3 %collective-permute-done.11.b2 = bf16[2048,2560]{1,0:T(8,128)(2,1)} collective-permute-done((bf16[2048,2560]{1,0:T(8,128)(2,1)}, bf16[2048,2560]{1,0:T(8,128)(2,1)}, u32[]{:S(2)}, u32[]{:S(2)}) %collective-permute-start.11) | collective-permute-done | bytes 10485792 | tf_op jit(solution)/shard_map/ppermute | solution.py:211
  690.4 14.7 collective-permute-done.14.b3
  705.0 104.3 %shard_map.32.rest_0_ = bf16[2048,14336]{1,0:T(8,128)(2,1)} custom-call(bf16[2048,2048]{1,0:T(8,128)(2,1)} %get-tuple-element.58.a0, bf16[2048,2048]{1,0:T(8,128)(2,1)} %get-tuple-element.90.a1, bf16[2048,2048]{1,0:T(8,128)(2,1)} %copy-done, bf16[2048,2048]{1,0:T(8,128)(2,1)} %copy-done.4, bf16[2048,14336]{1,0:T(8,128)(2,1)} %b0.19, ...), custom_call_target="tpu_custom_call", output_to_operand_aliasing={{}: (8, {})} | custom-call | flops 85899345920 | bytes 220200960 | tf_op jit(solution)/shard_map/pallas_call | solution.py:64
  809.3 106.8 %collective-permute-done.10.b2 = bf16[2048,2560]{1,0:T(8,128)(2,1)} collective-permute-done((bf16[2048,2560]{1,0:T(8,128)(2,1)}, bf16[2048,2560]{1,0:T(8,128)(2,1)}, u32[]{:S(2)}, u32[]{:S(2)}) %collective-permute-start.10) | collective-permute-done | bytes 10485792 | tf_op jit(solution)/shard_map/ppermute | solution.py:211
  916.5 8.3 slice.75
  926.2 6.4 collective-permute-done.15.b3
  932.6 104.3 %shard_map.33.rest_0_ = bf16[2048,14336]{1,0:T(8,128)(2,1)} custom-call(bf16[2048,2048]{1,0:T(8,128)(2,1)} %get-tuple-element.58.a0, bf16[2048,2048]{1,0:T(8,128)(2,1)} %get-tuple-element.90.a1, bf16[2048,2048]{1,0:T(8,128)(2,1)} %copy-done, bf16[2048,2048]{1,0:T(8,128)(2,1)} %copy-done.4, bf16[2048,14336]{1,0:T(8,128)(2,1)} %b0.19, ...), custom_call_target="tpu_custom_call", output_to_operand_aliasing={{}: (8, {})} | custom-call | flops 85899345920 | bytes 220200960 | tf_op jit(solution)/shard_map/pallas_call | solution.py:64
  1036.9 70.6 %collective-permute-done.17.b2 = bf16[2048,2048]{1,0:T(8,128)(2,1)} collective-permute-done((bf16[2048,2048]{1,0:T(8,128)(2,1)}, bf16[2048,2048]{1,0:T(8,128)(2,1)}, u32[]{:S(2)}, u32[]{:S(2)}) %collective-permute-start.17) | collective-permute-done | bytes 8388640 | tf_op jit(solution)/shard_map/ppermute | solution.py:211
  1107.7 5.8 slice.74
  1115.1 5.9 collective-permute-done.18.b3
  1121.0 84.5 %shard_map.34.rest_0_ = bf16[2048,14336]{1,0:T(8,128)(2,1)} custom-call(bf16[2048,2048]{1,0:T(8,128)(2,1)} %get-tuple-element.58.a0, bf16[2048,2048]{1,0:T(8,128)(2,1)} %get-tuple-element.90.a1, bf16[2048,2048]{1,0:T(8,128)(2,1)} %copy-done, bf16[2048,2048]{1,0:T(8,128)(2,1)} %copy-done.4, bf16[2048,14336]{1,0:T(8,128)(2,1)} %b0.19, ...), custom_call_target="tpu_custom_call", output_to_operand_aliasing={{}: (8, {})} | custom-call | flops 68719476736 | bytes 176160768 | tf_op jit(solution)/shard_map/pallas_call | solution.py:64
  1205.5 45.5 %collective-permute-done.16.b2 = bf16[2048,1536]{1,0:T(8,128)(2,1)} collective-permute-done((bf16[2048,1536]{1,0:T(8,128)(2,1)}, bf16[2048,1536]{1,0:T(8,128)(2,1)}, u32[]{:S(2)}, u32[]{:S(2)}) %collective-permute-start.16) | collective-permute-done | bytes 6291488 | tf_op jit(solution)/shard_map/ppermute | solution.py:211
  1251.4 4.6 slice.70
  1257.5 4.1 collective-permute-done.19.b3
  1261.5 64.5 %shard_map.35.refs_5_ = bf16[2048,14336]{1,0:T(8,128)(2,1)} custom-call(bf16[2048,2048]{1,0:T(8,128)(2,1)} %get-tuple-element.58.a0, bf16[2048,2048]{1,0:T(8,128)(2,1)} %get-tuple-element.90.a1, bf16[2048,2048]{1,0:T(8,128)(2,1)} %copy-done, bf16[2048,2048]{1,0:T(8,128)(2,1)} %copy-done.4, bf16[2048,14336]{1,0:T(8,128)(2,1)} %b0.19, ...), custom_call_target="tpu_custom_call", output_to_operand_aliasing={{}: (8, {})} | custom-call | flops 51539607552 | bytes 132120576 | tf_op jit(solution)/shard_map/pallas_call | solution.py:64
  1326.1 22.8 %collective-permute-done.9.refs_2_ = bf16[2048,1024]{1,0:T(8,128)(2,1)} collective-permute-done((bf16[2048,1024]{1,0:T(8,128)(2,1)}, bf16[2048,1024]{1,0:T(8,128)(2,1)}, u32[]{:S(2)}, u32[]{:S(2)}) %collective-permute-start.9) | collective-permute-done | bytes 4194336 | tf_op jit(solution)/shard_map/ppermute | solution.py:211
  1349.0 3.0 slice.69
  1353.7 51.6 %shard_map.36.refs_4_ = f32[2048,1536]{1,0:T(8,128)} custom-call(bf16[2048,2048]{1,0:T(8,128)(2,1)} %get-tuple-element.58.a0, bf16[2048,2048]{1,0:T(8,128)(2,1)} %get-tuple-element.90.a1, bf16[2048,14336]{1,0:T(8,128)(2,1)} %b0.19, bf16[2048,14336]{1,0:T(8,128)(2,1)} %collective-permute-done.1.b1), custom_call_target="tpu_custom_call" | custom-call | flops 25769803776 | bytes 119537664 | tf_op jit(solution)/shard_map/pallas_call | solution.py:94
  1405.3 3.4 copy-done.1
  1408.7 3.4 copy-done.5
  1412.1 21.6 %shard_map.37.refs_5_ = bf16[2048,14336]{1,0:T(8,128)(2,1)} custom-call(bf16[2048,2048]{1,0:T(8,128)(2,1)S(1)} %copy-done.1, bf16[2048,2048]{1,0:T(8,128)(2,1)S(1)} %copy-done.5, bf16[2048,1024]{1,0:T(8,128)(2,1)} %collective-permute-done.9.refs_2_, bf16[2048,1024]{1,0:T(8,128)(2,1)} %collective-permute-done.20.refs_3_, ...), custom_call_target="tpu_custom_call", output_to_operand_aliasing={{}: (5, {})} | custom-call | flops 17179869184 | bytes 79691776 | tf_op jit(solution)/shard_map/pallas_call | solution.py:143
  1435.4 2.6 collective-permute-done.21.refs_3_
  1438.0 11.8 shard_map.38.refs_5_
  1449.9 10.3 collective-permute-done.25.refs_2_
  1460.5 10.1 shard_map.39.refs_4_
  1475.1 3.4 copy-done.2
  1478.5 3.4 copy-done.6
  1483.5 7.0 shard_map.40.c_prev
  1490.6 11.1 shard_map.41.refs_4_
  1501.7 3.4 copy-done.3
  1505.1 3.4 copy-done.7
  1510.1 3.1 shard_map.42.refs_4_
  1515.0 2.5 shard_map.43.refs_2_
  1517.5 3.9 collective-permute-done.22.refs_1_
  (70 shorter events, 39.8 us)
Async XLA Ops:
  0.0 393.2 %collective-permute-start.1 = (bf16[2048,14336]{1,0:T(8,128)(2,1)}, bf16[2048,14336]{1,0:T(8,128)(2,1)}, u32[]{:S(2)}, u32[]{:S(2)}) collective-permute-start(bf16[2048,14336]{1,0:T(8,128)(2,1)} %b0.19), channel_id=1, source_target_pairs={{0,1},{1,0},{2,3},{3,2},{4,5},{5,4},{6,7},{7,6}} | collective-permute-start | bytes 176160768 | tf_op jit(solution)/shard_map/ppermute | solution.py:224
  0.8 363.7 %collective-permute-start = (bf16[2048,4096]{1,0:T(8,128)(2,1)}, bf16[2048,4096]{1,0:T(8,128)(2,1)}, u32[]{:S(2)}, u32[]{:S(2)}) collective-permute-start(bf16[2048,4096]{1,0:T(8,128)(2,1)} %param.2), channel_id=1, source_target_pairs={{0,4},{4,0},{1,5},{5,1},{2,6},{6,2},{3,7},{7,3}} | collective-permute-start | bytes 50331656 | tf_op jit(solution)/shard_map/ppermute | solution.py:223
  25.6 434.9 %collective-permute-start.12 = (bf16[2048,2560]{1,0:T(8,128)(2,1)}, bf16[2048,2560]{1,0:T(8,128)(2,1)}, u32[]{:S(2)}, u32[]{:S(2)}) collective-permute-start(bf16[2048,2560]{1,0:T(8,128)(2,1)} %get-tuple-element.85), channel_id=1, source_target_pairs={{0,3},{3,0},{1,2},{2,1},{4,7},{7,4},{5,6},{6,5}} | collective-permute-start | bytes 31457288 | tf_op jit(solution)/shard_map/ppermute | solution.py:211
  27.8 229.4 %collective-permute-start.4 = (bf16[384,256]{1,0:T(8,128)(2,1)S(1)}, bf16[384,256]{1,0:T(8,128)(2,1)S(1)}, u32[]{:S(2)}, u32[]{:S(2)}) collective-permute-start(bf16[384,256]{1,0:T(8,128)(2,1)S(1)} %slice.67), channel_id=1, source_target_pairs={{0,3},{3,0},{1,2},{2,1},{4,7},{7,4},{5,6},{6,5}} | collective-permute-start | bytes 589832 | tf_op jit(solution)/shard_map/ppermute | solution.py:211
  29.6 359.9 %collective-permute-start.3 = (bf16[2048,256]{1,0:T(8,128)(2,1)S(1)}, bf16[2048,256]{1,0:T(8,128)(2,1)S(1)}, u32[]{:S(2)}, u32[]{:S(2)}) collective-permute-start(bf16[2048,256]{1,0:T(8,128)(2,1)S(1)} %slice.66), channel_id=1, source_target_pairs={{0,3},{3,0},{1,2},{2,1},{4,7},{7,4},{5,6},{6,5}} | collective-permute-start | bytes 3145736 | tf_op jit(solution)/shard_map/ppermute | solution.py:211
  257.3 152.9 %collective-permute-start.2 = (bf16[2048,768]{1,0:T(8,128)(2,1)}, bf16[2048,768]{1,0:T(8,128)(2,1)}, u32[]{:S(2)}, u32[]{:S(2)}) collective-permute-start(bf16[2048,768]{1,0:T(8,128)(2,1)} %slice.65), channel_id=1, source_target_pairs={{0,3},{3,0},{1,2},{2,1},{4,7},{7,4},{5,6},{6,5}} | collective-permute-start | bytes 9437192 | tf_op jit(solution)/shard_map/ppermute | solution.py:211
  364.5 17.8 %collective-permute-start.5 = (bf16[384,256]{1,0:T(8,128)(2,1)S(1)}, bf16[384,256]{1,0:T(8,128)(2,1)S(1)}, u32[]{:S(2)}, u32[]{:S(2)}) collective-permute-start(bf16[384,256]{1,0:T(8,128)(2,1)S(1)} %collective-permute-done.4.refs_2_), channel_id=1, source_target_pairs={{0,1},{1,0},{2,3},{3,2},{4,5},{5,4},{6,7},{7,6}} | collective-permute-start | bytes 589832 | tf_op jit(solution)/shard_map/ppermute | solution.py:225
  382.3 3.3 copy-start
  382.3 5.8 copy-start.4
  388.1 1.3 copy-start.10
  389.4 3.8 copy-start.11
  389.4 2.8 collective-permute-start.6
  392.2 1.0 copy-start.12
  410.1 6.0 collective-permute-start.7
  460.4 16.5 %collective-permute-start.13 = (bf16[2048,2560]{1,0:T(8,128)(2,1)}, bf16[2048,2560]{1,0:T(8,128)(2,1)}, u32[]{:S(2)}, u32[]{:S(2)}) collective-permute-start(bf16[2048,2560]{1,0:T(8,128)(2,1)} %collective-permute-done.12.b2), channel_id=1, source_target_pairs={{0,1},{1,0},{2,3},{3,2},{4,5},{5,4},{6,7},{7,6}} | collective-permute-start | bytes 31457288 | tf_op jit(solution)/shard_map/ppermute | solution.py:215
  460.8 227.7 %collective-permute-start.11 = (bf16[2048,2560]{1,0:T(8,128)(2,1)}, bf16[2048,2560]{1,0:T(8,128)(2,1)}, u32[]{:S(2)}, u32[]{:S(2)}) collective-permute-start(bf16[2048,2560]{1,0:T(8,128)(2,1)} %get-tuple-element.86), channel_id=1, source_target_pairs={{0,3},{3,0},{1,2},{2,1},{4,7},{7,4},{5,6},{6,5}} | collective-permute-start | bytes 31457288 | tf_op jit(solution)/shard_map/ppermute | solution.py:211
  688.5 16.5 %collective-permute-start.14 = (bf16[2048,2560]{1,0:T(8,128)(2,1)}, bf16[2048,2560]{1,0:T(8,128)(2,1)}, u32[]{:S(2)}, u32[]{:S(2)}) collective-permute-start(bf16[2048,2560]{1,0:T(8,128)(2,1)} %collective-permute-done.11.b2), channel_id=1, source_target_pairs={{0,1},{1,0},{2,3},{3,2},{4,5},{5,4},{6,7},{7,6}} | collective-permute-start | bytes 31457288 | tf_op jit(solution)/shard_map/ppermute | solution.py:215
  688.7 227.5 %collective-permute-start.10 = (bf16[2048,2560]{1,0:T(8,128)(2,1)}, bf16[2048,2560]{1,0:T(8,128)(2,1)}, u32[]{:S(2)}, u32[]{:S(2)}) collective-permute-start(bf16[2048,2560]{1,0:T(8,128)(2,1)} %get-tuple-element.87), channel_id=1, source_target_pairs={{0,3},{3,0},{1,2},{2,1},{4,7},{7,4},{5,6},{6,5}} | collective-permute-start | bytes 31457288 | tf_op jit(solution)/shard_map/ppermute | solution.py:211
  916.1 16.5 %collective-permute-start.15 = (bf16[2048,2560]{1,0:T(8,128)(2,1)}, bf16[2048,2560]{1,0:T(8,128)(2,1)}, u32[]{:S(2)}, u32[]{:S(2)}) collective-permute-start(bf16[2048,2560]{1,0:T(8,128)(2,1)} %collective-permute-done.10.b2), channel_id=1, source_target_pairs={{0,1},{1,0},{2,3},{3,2},{4,5},{5,4},{6,7},{7,6}} | collective-permute-start | bytes 31457288 | tf_op jit(solution)/shard_map/ppermute | solution.py:215
  924.8 182.8 %collective-permute-start.17 = (bf16[2048,2048]{1,0:T(8,128)(2,1)}, bf16[2048,2048]{1,0:T(8,128)(2,1)}, u32[]{:S(2)}, u32[]{:S(2)}) collective-permute-start(bf16[2048,2048]{1,0:T(8,128)(2,1)} %slice.75), channel_id=1, source_target_pairs={{0,3},{3,0},{1,2},{2,1},{4,7},{7,4},{5,6},{6,5}} | collective-permute-start | bytes 25165832 | tf_op jit(solution)/shard_map/ppermute | solution.py:211
  1107.5 13.5 collective-permute-start.18
  1113.4 137.6 %collective-permute-start.16 = (bf16[2048,1536]{1,0:T(8,128)(2,1)}, bf16[2048,1536]{1,0:T(8,128)(2,1)}, u32[]{:S(2)}, u32[]{:S(2)}) collective-permute-start(bf16[2048,1536]{1,0:T(8,128)(2,1)} %slice.74), channel_id=1, source_target_pairs={{0,3},{3,0},{1,2},{2,1},{4,7},{7,4},{5,6},{6,5}} | collective-permute-start | bytes 18874376 | tf_op jit(solution)/shard_map/ppermute | solution.py:211
  1251.0 10.5 collective-permute-start.19
  1256.0 92.9 %collective-permute-start.9 = (bf16[2048,1024]{1,0:T(8,128)(2,1)}, bf16[2048,1024]{1,0:T(8,128)(2,1)}, u32[]{:S(2)}, u32[]{:S(2)}) collective-permute-start(bf16[2048,1024]{1,0:T(8,128)(2,1)} %slice.70), channel_id=1, source_target_pairs={{0,3},{3,0},{1,2},{2,1},{4,7},{7,4},{5,6},{6,5}} | collective-permute-start | bytes 12582920 | tf_op jit(solution)/shard_map/ppermute | solution.py:211
  1348.9 56.4 %collective-permute-start.20 = (bf16[2048,1024]{1,0:T(8,128)(2,1)}, bf16[2048,1024]{1,0:T(8,128)(2,1)}, u32[]{:S(2)}, u32[]{:S(2)}) collective-permute-start(bf16[2048,1024]{1,0:T(8,128)(2,1)} %collective-permute-done.9.refs_2_), channel_id=1, source_target_pairs={{0,1},{1,0},{2,3},{3,2},{4,5},{5,4},{6,7},{7,6}} | collective-permute-start | bytes 12582920 | tf_op jit(solution)/shard_map/ppermute | solution.py:215
  1352.1 81.6 %collective-permute-start.8 = (bf16[2048,512]{1,0:T(8,128)(2,1)}, bf16[2048,512]{1,0:T(8,128)(2,1)}, u32[]{:S(2)}, u32[]{:S(2)}) collective-permute-start(bf16[2048,512]{1,0:T(8,128)(2,1)} %slice.69), channel_id=1, source_target_pairs={{0,3},{3,0},{1,2},{2,1},{4,7},{7,4},{5,6},{6,5}} | collective-permute-start | bytes 6291464 | tf_op jit(solution)/shard_map/ppermute | solution.py:211
  1405.3 3.4 copy-start.1
  1408.7 3.4 copy-start.5
  1433.7 4.4 collective-permute-start.21
  1435.1 25.0 %collective-permute-start.25 = (bf16[2048,256]{1,0:T(8,128)(2,1)S(1)}, bf16[2048,256]{1,0:T(8,128)(2,1)}, u32[]{:S(2)}, u32[]{:S(2)}) collective-permute-start(bf16[2048,256]{1,0:T(8,128)(2,1)S(1)} %slice.79), channel_id=1, source_target_pairs={{0,3},{3,0},{1,2},{2,1},{4,7},{7,4},{5,6},{6,5}} | collective-permute-start | bytes 3145736 | tf_op jit(solution)/shard_map/ppermute | solution.py:211
  1460.2 15.0 collective-permute-start.26
  1471.7 18.8 %collective-permute-start.24 = (bf16[768,256]{1,0:T(8,128)(2,1)S(1)}, bf16[768,256]{1,0:T(8,128)(2,1)S(1)}, u32[]{:S(2)}, u32[]{:S(2)}) collective-permute-start(bf16[768,256]{1,0:T(8,128)(2,1)S(1)} %slice.78), channel_id=1, source_target_pairs={{0,3},{3,0},{1,2},{2,1},{4,7},{7,4},{5,6},{6,5}} | collective-permute-start | bytes 1179656 | tf_op jit(solution)/shard_map/ppermute | solution.py:211
  1473.4 39.8 %collective-permute-start.23 = (bf16[512,256]{1,0:T(8,128)(2,1)}, bf16[512,256]{1,0:T(8,128)(2,1)}, u32[]{:S(2)}, u32[]{:S(2)}) collective-permute-start(bf16[512,256]{1,0:T(8,128)(2,1)} %slice.77), channel_id=1, source_target_pairs={{0,3},{3,0},{1,2},{2,1},{4,7},{7,4},{5,6},{6,5}} | collective-permute-start | bytes 786440 | tf_op jit(solution)/shard_map/ppermute | solution.py:211
  1475.1 3.4 copy-start.2
  1478.5 3.4 copy-start.6
  1481.9 1.6 copy-start.9
  1490.5 11.2 collective-permute-start.27
  1501.7 3.4 copy-start.3
  1505.1 3.4 copy-start.7
  1508.5 1.6 copy-start.8
  1513.2 1.8 collective-permute-start.28
  1514.5 6.9 collective-permute-start.22
  1521.4 1.4 collective-permute-start.29

commit v8 on v7

--- a/solution.py
+++ b/solution.py
@@ -46,7 +46,7 @@
     c_ref[...] = total.astype(c_ref.dtype)
 
 
-def whole_product(a_parts, b_own, b_pair, x_own, x_pair, c_prev, start, tm=512):
+def whole_product(a_parts, b_own, b_pair, x_own, x_pair, c_prev, start, vmem, tm=512):
     rows, depth = a_parts[0].shape
     columns = b_own.shape[1]
     width = x_own.shape[1]
@@ -69,7 +69,7 @@
         out_shape=jax.ShapeDtypeStruct((rows, columns), jnp.bfloat16),
         input_output_aliases=aliases,
         cost_estimate=matmul_cost(rows, 4 * depth, width, width // tn),
-        compiler_params=pltpu.CompilerParams(vmem_limit_bytes=62 * MIB),
+        compiler_params=pltpu.CompilerParams(vmem_limit_bytes=vmem * MIB),
     )(*args)
 
 
@@ -154,11 +154,11 @@
     )(*args)
 
 
-def last_body(start, block, a_ref, x_ref, s_ref, c_prev, c_ref, held, sems):
-    rows, width = held.shape
+def last_body(start, blocks, a_ref, x_ref, s_ref, c_prev, c_ref, held, sems):
+    width = held.shape[1]
     copies = []
-    for i in range(rows // block):
-        part = pl.ds(i * block, block)
+    for i, block in enumerate(blocks):
+        part = pl.ds(sum(blocks[:i]), block)
         total = s_ref[part, :] + jnp.dot(a_ref[part, :], x_ref[...], preferred_element_type=jnp.float32)
         held[part, :] = total.astype(held.dtype)
         copy = pltpu.make_async_copy(held.at[part, :], c_ref.at[part, pl.ds(start, width)], sems.at[i])
@@ -168,11 +168,11 @@
         copy.wait()
 
 
-def last_product(a, x, sums, c_prev, start, block=512):
+def last_product(a, x, sums, c_prev, start, eighths=(3, 3, 1, 1)):
     rows = a.shape[0]
     depth, width = x.shape
     return pl.pallas_call(
-        functools.partial(last_body, start, block),
+        functools.partial(last_body, start, [rows // 8 * n for n in eighths]),
         grid=(1,),
         in_specs=[
             pl.BlockSpec((rows, depth), lambda n: (0, 0)),
@@ -182,7 +182,7 @@
         ],
         out_specs=pl.BlockSpec(memory_space=pl.ANY),
         out_shape=jax.ShapeDtypeStruct(c_prev.shape, c_prev.dtype),
-        scratch_shapes=[pltpu.VMEM((rows, width), c_prev.dtype), pltpu.SemaphoreType.DMA((rows // block,))],
+        scratch_shapes=[pltpu.VMEM((rows, width), c_prev.dtype), pltpu.SemaphoreType.DMA((len(eighths),))],
         input_output_aliases={3: 0},
         cost_estimate=matmul_cost(rows, depth, width, 1),
         compiler_params=pltpu.CompilerParams(vmem_limit_bytes=FAR_VMEM * MIB),
@@ -250,7 +250,8 @@
             else:
                 c = pass_on(j, c)
             if j < TAIL:
-                c = whole_product(a_near + a_far, b_blk, b_pair, x_own[j], x_pair[j], c, start)
+                vmem = 44 if j == TAIL - 1 else 62
+                c = whole_product(a_near + a_far, b_blk, b_pair, x_own[j], x_pair[j], c, start, vmem)
             else:
                 near, near_start = (sums_before, before) if j == LATE else (sums, tail)
                 c = far_product(a_far, both(j), near, start - near_start, c, start)

time: 1530 us -> 1520 us (level)
    unnamed x26 -> x28, local copies, waits for them, and re-layouts: 30.1 us -> 32.8 us
where the time goes in v8:
time: 1520 us
  waiting for transfers between devices  749 us (49%)
  Pallas kernels  644 us (42%)
  local copies, waits for them, and re-layouts  87.2 us (6%)
  starting transfers between devices  23.8 us (2%)
  other arithmetic  17.8 us (1%)
    ppermute x14, waiting for transfers between devices, send(): x_own[j] = lax.ppermute(piece, 'row', across)  585 us
    pallas_call x7, Pallas kernels, whole_product(): pl.pallas_call(whole_body, grid=(width // tn, rows // tm), in_specs=in_sp...  521 us
    ppermute x1, waiting for transfers between devices, local_product(): a_recv = lax.ppermute(a_blk, 'col', [(0, 1), (1, 0)])  105 us
    pallas_call x3, Pallas kernels, near_sums(): pl.pallas_call(near_body, grid=(width // tn, rows // tm), in_specs=in_spe...  72.9 us
    ppermute x13, waiting for transfers between devices, pass_on(): x_pair[j] = lax.ppermute(x_own[j], 'row', beside)  58.7 us
    slice x12, local copies, waits for them, and re-layouts, send(): lax.slice(block, (row_of[j], start), (row_of[j] + rows * depth // 16, sta...  52.9 us
    pallas_call x7, Pallas kernels, far_product(): pl.pallas_call(functools.partial(far_body, [used.index(i) for i, _, _ in...  48.5 us
    unnamed x28, local copies, waits for them, and re-layouts  32.8 us
  transfers between devices with their start and end apart: 30, of which 19 were waited for; matrix products, arithmetic and copies ran while one was open for 5% of the time, Pallas kernels for 42%

profile of v8, /device:TPU:0, one launch (start us, length us, event | category | flops | bytes accessed | tf_op | source)
XLA Modules:
  0.0 1522.5 jit_solution(13419269426822861381)
XLA Ops:
  0.8 2.5 collective-permute-start
  3.3 22.2 %fusion = (bf16[2048,2560]{1,0:T(8,128)(2,1)}, bf16[2048,2560]{1,0:T(8,128)(2,1)}, bf16[2048,2560]{1,0:T(8,128)(2,1)}) fusion(bf16[2048,14336]{1,0:T(8,128)(2,1)} %b0.19), kind=kLoop, calls=%fused_computation.8 | loop fusion | bytes 62914560 | tf_op jit(solution)/shard_map/slice | solution.py:210
  30.9 3.8 slice.65
  34.7 222.6 %collective-permute-done.4.refs_2_ = bf16[384,256]{1,0:T(8,128)(2,1)S(1)} collective-permute-done((bf16[384,256]{1,0:T(8,128)(2,1)S(1)}, bf16[384,256]{1,0:T(8,128)(2,1)S(1)}, u32[]{:S(2)}, u32[]{:S(2)}) %collective-permute-start.4) | collective-permute-done | bytes 196640 | tf_op jit(solution)/shard_map/ppermute | solution.py:211
  259.4 105.2 %collective-permute-done = bf16[2048,4096]{1,0:T(8,128)(2,1)} collective-permute-done((bf16[2048,4096]{1,0:T(8,128)(2,1)}, bf16[2048,4096]{1,0:T(8,128)(2,1)}, u32[]{:S(2)}, u32[]{:S(2)}) %collective-permute-start) | collective-permute-done | bytes 16777248 | tf_op jit(solution)/shard_map/ppermute | solution.py:223
  364.5 17.8 %broadcast_select_fusion.4 = (bf16[2048,2048]{1,0:T(8,128)(2,1)S(1)}, bf16[2048,2048]{1,0:T(8,128)(2,1)}, bf16[2048,2048]{1,0:T(8,128)(2,1)}, bf16[2048,2048]{1,0:T(8,128)(2,1)S(1)}) fusion(pred[]{:T(512)S(6)} %eq.9, bf16[2048,4096]{1,0:T(8,128)(2,1)} %param.2, pred[]{:T(512)S(6)} %eq.11, bf16[2048,4096]{1,0:T(8,128)(2,1)} %collective-permute-done, pred[]{:T(512)S(6)} %eq.10), kind=kLoop, calls=%fused_computation.4 | loop fusion | flops 33554432 | bytes 67108864 | tf_op jit(solution)/shard_map/jit(_where)/select_n | solution.py:232
  385.6 2.5 copy-done.4
  390.0 2.3 collective-permute-done.6.b3
  393.2 16.9 %shard_map.29.rest_0_ = bf16[2048,14336]{1,0:T(8,128)(2,1)} custom-call(bf16[2048,2048]{1,0:T(8,128)(2,1)} %get-tuple-element.58.a0, bf16[2048,2048]{1,0:T(8,128)(2,1)} %get-tuple-element.90.a1, bf16[2048,2048]{1,0:T(8,128)(2,1)} %copy-done, bf16[2048,2048]{1,0:T(8,128)(2,1)} %copy-done.4, bf16[2048,14336]{1,0:T(8,128)(2,1)} %b0.19, ...), custom_call_target="tpu_custom_call" | custom-call | flops 8589934592 | bytes 38797312 | tf_op jit(solution)/shard_map/pallas_call | solution.py:64
  410.5 5.6 collective-permute-done.7.b3
  416.2 42.7 %shard_map.30.rest_0_ = bf16[2048,14336]{1,0:T(8,128)(2,1)} custom-call(bf16[2048,2048]{1,0:T(8,128)(2,1)} %get-tuple-element.58.a0, bf16[2048,2048]{1,0:T(8,128)(2,1)} %get-tuple-element.90.a1, bf16[2048,2048]{1,0:T(8,128)(2,1)} %copy-done, bf16[2048,2048]{1,0:T(8,128)(2,1)} %copy-done.4, bf16[2048,14336]{1,0:T(8,128)(2,1)} %b0.19, ...), custom_call_target="tpu_custom_call", output_to_operand_aliasing={{}: (8, {})} | custom-call | flops 25769803776 | bytes 116391936 | tf_op jit(solution)/shard_map/pallas_call | solution.py:64
  462.3 14.7 collective-permute-done.13.b3
  476.9 104.3 %shard_map.31.rest_0_ = bf16[2048,14336]{1,0:T(8,128)(2,1)} custom-call(bf16[2048,2048]{1,0:T(8,128)(2,1)} %get-tuple-element.58.a0, bf16[2048,2048]{1,0:T(8,128)(2,1)} %get-tuple-element.90.a1, bf16[2048,2048]{1,0:T(8,128)(2,1)} %copy-done, bf16[2048,2048]{1,0:T(8,128)(2,1)} %copy-done.4, bf16[2048,14336]{1,0:T(8,128)(2,1)} %b0.19, ...), custom_call_target="tpu_custom_call", output_to_operand_aliasing={{}: (8, {})} | custom-call | flops 85899345920 | bytes 220200960 | tf_op jit(solution)/shard_map/pallas_call | solution.py:64
  581.3 107.2 %collective-permute-done.11.b2 = bf16[2048,2560]{1,0:T(8,128)(2,1)} collective-permute-done((bf16[2048,2560]{1,0:T(8,128)(2,1)}, bf16[2048,2560]{1,0:T(8,128)(2,1)}, u32[]{:S(2)}, u32[]{:S(2)}) %collective-permute-start.11) | collective-permute-done | bytes 10485792 | tf_op jit(solution)/shard_map/ppermute | solution.py:211
  690.3 14.7 collective-permute-done.14.b3
  705.0 104.3 %shard_map.32.rest_0_ = bf16[2048,14336]{1,0:T(8,128)(2,1)} custom-call(bf16[2048,2048]{1,0:T(8,128)(2,1)} %get-tuple-element.58.a0, bf16[2048,2048]{1,0:T(8,128)(2,1)} %get-tuple-element.90.a1, bf16[2048,2048]{1,0:T(8,128)(2,1)} %copy-done, bf16[2048,2048]{1,0:T(8,128)(2,1)} %copy-done.4, bf16[2048,14336]{1,0:T(8,128)(2,1)} %b0.19, ...), custom_call_target="tpu_custom_call", output_to_operand_aliasing={{}: (8, {})} | custom-call | flops 85899345920 | bytes 220200960 | tf_op jit(solution)/shard_map/pallas_call | solution.py:64
  809.3 106.8 %collective-permute-done.10.b2 = bf16[2048,2560]{1,0:T(8,128)(2,1)} collective-permute-done((bf16[2048,2560]{1,0:T(8,128)(2,1)}, bf16[2048,2560]{1,0:T(8,128)(2,1)}, u32[]{:S(2)}, u32[]{:S(2)}) %collective-permute-start.10) | collective-permute-done | bytes 10485792 | tf_op jit(solution)/shard_map/ppermute | solution.py:211
  916.5 8.3 slice.75
  926.2 6.4 collective-permute-done.15.b3
  932.6 104.3 %shard_map.33.rest_0_ = bf16[2048,14336]{1,0:T(8,128)(2,1)} custom-call(bf16[2048,2048]{1,0:T(8,128)(2,1)} %get-tuple-element.58.a0, bf16[2048,2048]{1,0:T(8,128)(2,1)} %get-tuple-element.90.a1, bf16[2048,2048]{1,0:T(8,128)(2,1)} %copy-done, bf16[2048,2048]{1,0:T(8,128)(2,1)} %copy-done.4, bf16[2048,14336]{1,0:T(8,128)(2,1)} %b0.19, ...), custom_call_target="tpu_custom_call", output_to_operand_aliasing={{}: (8, {})} | custom-call | flops 85899345920 | bytes 220200960 | tf_op jit(solution)/shard_map/pallas_call | solution.py:64
  1036.9 70.6 %collective-permute-done.17.b2 = bf16[2048,2048]{1,0:T(8,128)(2,1)} collective-permute-done((bf16[2048,2048]{1,0:T(8,128)(2,1)}, bf16[2048,2048]{1,0:T(8,128)(2,1)}, u32[]{:S(2)}, u32[]{:S(2)}) %collective-permute-start.17) | collective-permute-done | bytes 8388640 | tf_op jit(solution)/shard_map/ppermute | solution.py:211
  1107.6 5.8 slice.74
  1115.1 5.9 collective-permute-done.18.b3
  1121.0 84.4 %shard_map.34.rest_0_ = bf16[2048,14336]{1,0:T(8,128)(2,1)} custom-call(bf16[2048,2048]{1,0:T(8,128)(2,1)} %get-tuple-element.58.a0, bf16[2048,2048]{1,0:T(8,128)(2,1)} %get-tuple-element.90.a1, bf16[2048,2048]{1,0:T(8,128)(2,1)} %copy-done, bf16[2048,2048]{1,0:T(8,128)(2,1)} %copy-done.4, bf16[2048,14336]{1,0:T(8,128)(2,1)} %b0.19, ...), custom_call_target="tpu_custom_call", output_to_operand_aliasing={{}: (8, {})} | custom-call | flops 68719476736 | bytes 176160768 | tf_op jit(solution)/shard_map/pallas_call | solution.py:64
  1205.4 45.6 %collective-permute-done.16.b2 = bf16[2048,1536]{1,0:T(8,128)(2,1)} collective-permute-done((bf16[2048,1536]{1,0:T(8,128)(2,1)}, bf16[2048,1536]{1,0:T(8,128)(2,1)}, u32[]{:S(2)}, u32[]{:S(2)}) %collective-permute-start.16) | collective-permute-done | bytes 6291488 | tf_op jit(solution)/shard_map/ppermute | solution.py:211
  1251.4 2.6 slice.70
  1255.5 5.9 collective-permute-done.19.b3
  1261.4 2.7 copy-done.11
  1264.1 64.5 %shard_map.35.refs_5_ = bf16[2048,14336]{1,0:T(8,128)(2,1)} custom-call(bf16[2048,2048]{1,0:T(8,128)(2,1)} %get-tuple-element.58.a0, bf16[2048,2048]{1,0:T(8,128)(2,1)} %get-tuple-element.90.a1, bf16[2048,2048]{1,0:T(8,128)(2,1)} %copy-done, bf16[2048,2048]{1,0:T(8,128)(2,1)} %copy-done.4, bf16[2048,14336]{1,0:T(8,128)(2,1)} %b0.19, ...), custom_call_target="tpu_custom_call", output_to_operand_aliasing={{}: (8, {})} | custom-call | flops 51539607552 | bytes 132120576 | tf_op jit(solution)/shard_map/pallas_call | solution.py:64
  1328.6 18.1 %collective-permute-done.9.refs_2_ = bf16[2048,1024]{1,0:T(8,128)(2,1)} collective-permute-done((bf16[2048,1024]{1,0:T(8,128)(2,1)S(1)}, bf16[2048,1024]{1,0:T(8,128)(2,1)}, u32[]{:S(2)}, u32[]{:S(2)}) %collective-permute-start.9) | collective-permute-done | bytes 4194336 | tf_op jit(solution)/shard_map/ppermute | solution.py:211
  1346.8 3.1 slice.69
  1351.6 51.6 %shard_map.36.refs_4_ = f32[2048,1536]{1,0:T(8,128)} custom-call(bf16[2048,2048]{1,0:T(8,128)(2,1)} %get-tuple-element.58.a0, bf16[2048,2048]{1,0:T(8,128)(2,1)} %get-tuple-element.90.a1, bf16[2048,14336]{1,0:T(8,128)(2,1)} %b0.19, bf16[2048,14336]{1,0:T(8,128)(2,1)} %collective-permute-done.1.b1), custom_call_target="tpu_custom_call" | custom-call | flops 25769803776 | bytes 119537664 | tf_op jit(solution)/shard_map/pallas_call | solution.py:94
  1403.1 3.4 copy-done.1
  1406.5 3.4 copy-done.5
  1409.9 21.6 %shard_map.37.refs_5_ = bf16[2048,14336]{1,0:T(8,128)(2,1)} custom-call(bf16[2048,2048]{1,0:T(8,128)(2,1)S(1)} %copy-done.1, bf16[2048,2048]{1,0:T(8,128)(2,1)S(1)} %copy-done.5, bf16[2048,1024]{1,0:T(8,128)(2,1)} %collective-permute-done.9.refs_2_, bf16[2048,1024]{1,0:T(8,128)(2,1)} %collective-permute-done.20.refs_3_, ...), custom_call_target="tpu_custom_call", output_to_operand_aliasing={{}: (5, {})} | custom-call | flops 17179869184 | bytes 79691776 | tf_op jit(solution)/shard_map/pallas_call | solution.py:143
  1433.2 2.6 collective-permute-done.21.refs_3_
  1435.8 11.8 shard_map.38.refs_5_
  1447.7 10.3 collective-permute-done.25.refs_2_
  1458.3 10.1 shard_map.39.refs_4_
  1472.9 3.4 copy-done.2
  1476.3 3.4 copy-done.6
  1481.3 7.0 shard_map.40.c_prev
  1488.4 11.2 shard_map.41.refs_4_
  1499.6 3.4 copy-done.3
  1503.0 3.4 copy-done.7
  1508.0 3.1 shard_map.42.refs_4_
  1512.9 2.5 shard_map.43.refs_2_
  1515.4 3.9 collective-permute-done.22.refs_1_
  (72 shorter events, 42.0 us)
Async XLA Ops:
  0.0 393.2 %collective-permute-start.1 = (bf16[2048,14336]{1,0:T(8,128)(2,1)}, bf16[2048,14336]{1,0:T(8,128)(2,1)}, u32[]{:S(2)}, u32[]{:S(2)}) collective-permute-start(bf16[2048,14336]{1,0:T(8,128)(2,1)} %b0.19), channel_id=1, source_target_pairs={{0,1},{1,0},{2,3},{3,2},{4,5},{5,4},{6,7},{7,6}} | collective-permute-start | bytes 176160768 | tf_op jit(solution)/shard_map/ppermute | solution.py:224
  0.8 363.7 %collective-permute-start = (bf16[2048,4096]{1,0:T(8,128)(2,1)}, bf16[2048,4096]{1,0:T(8,128)(2,1)}, u32[]{:S(2)}, u32[]{:S(2)}) collective-permute-start(bf16[2048,4096]{1,0:T(8,128)(2,1)} %param.2), channel_id=1, source_target_pairs={{0,4},{4,0},{1,5},{5,1},{2,6},{6,2},{3,7},{7,3}} | collective-permute-start | bytes 50331656 | tf_op jit(solution)/shard_map/ppermute | solution.py:223
  25.5 434.9 %collective-permute-start.12 = (bf16[2048,2560]{1,0:T(8,128)(2,1)}, bf16[2048,2560]{1,0:T(8,128)(2,1)}, u32[]{:S(2)}, u32[]{:S(2)}) collective-permute-start(bf16[2048,2560]{1,0:T(8,128)(2,1)} %get-tuple-element.85), channel_id=1, source_target_pairs={{0,3},{3,0},{1,2},{2,1},{4,7},{7,4},{5,6},{6,5}} | collective-permute-start | bytes 31457288 | tf_op jit(solution)/shard_map/ppermute | solution.py:211
  27.8 229.4 %collective-permute-start.4 = (bf16[384,256]{1,0:T(8,128)(2,1)S(1)}, bf16[384,256]{1,0:T(8,128)(2,1)S(1)}, u32[]{:S(2)}, u32[]{:S(2)}) collective-permute-start(bf16[384,256]{1,0:T(8,128)(2,1)S(1)} %slice.67), channel_id=1, source_target_pairs={{0,3},{3,0},{1,2},{2,1},{4,7},{7,4},{5,6},{6,5}} | collective-permute-start | bytes 589832 | tf_op jit(solution)/shard_map/ppermute | solution.py:211
  29.5 359.9 %collective-permute-start.3 = (bf16[2048,256]{1,0:T(8,128)(2,1)S(1)}, bf16[2048,256]{1,0:T(8,128)(2,1)S(1)}, u32[]{:S(2)}, u32[]{:S(2)}) collective-permute-start(bf16[2048,256]{1,0:T(8,128)(2,1)S(1)} %slice.66), channel_id=1, source_target_pairs={{0,3},{3,0},{1,2},{2,1},{4,7},{7,4},{5,6},{6,5}} | collective-permute-start | bytes 3145736 | tf_op jit(solution)/shard_map/ppermute | solution.py:211
  257.2 152.9 %collective-permute-start.2 = (bf16[2048,768]{1,0:T(8,128)(2,1)}, bf16[2048,768]{1,0:T(8,128)(2,1)}, u32[]{:S(2)}, u32[]{:S(2)}) collective-permute-start(bf16[2048,768]{1,0:T(8,128)(2,1)} %slice.65), channel_id=1, source_target_pairs={{0,3},{3,0},{1,2},{2,1},{4,7},{7,4},{5,6},{6,5}} | collective-permute-start | bytes 9437192 | tf_op jit(solution)/shard_map/ppermute | solution.py:211
  364.5 17.8 %collective-permute-start.5 = (bf16[384,256]{1,0:T(8,128)(2,1)S(1)}, bf16[384,256]{1,0:T(8,128)(2,1)S(1)}, u32[]{:S(2)}, u32[]{:S(2)}) collective-permute-start(bf16[384,256]{1,0:T(8,128)(2,1)S(1)} %collective-permute-done.4.refs_2_), channel_id=1, source_target_pairs={{0,1},{1,0},{2,3},{3,2},{4,5},{5,4},{6,7},{7,6}} | collective-permute-start | bytes 589832 | tf_op jit(solution)/shard_map/ppermute | solution.py:225
  382.3 3.3 copy-start
  382.3 5.8 copy-start.4
  388.2 1.3 copy-start.10
  389.5 3.8 copy-start.12
  389.5 2.8 collective-permute-start.6
  392.3 1.0 copy-start.13
  410.1 6.0 collective-permute-start.7
  460.4 16.5 %collective-permute-start.13 = (bf16[2048,2560]{1,0:T(8,128)(2,1)}, bf16[2048,2560]{1,0:T(8,128)(2,1)}, u32[]{:S(2)}, u32[]{:S(2)}) collective-permute-start(bf16[2048,2560]{1,0:T(8,128)(2,1)} %collective-permute-done.12.b2), channel_id=1, source_target_pairs={{0,1},{1,0},{2,3},{3,2},{4,5},{5,4},{6,7},{7,6}} | collective-permute-start | bytes 31457288 | tf_op jit(solution)/shard_map/ppermute | solution.py:215
  460.8 227.7 %collective-permute-start.11 = (bf16[2048,2560]{1,0:T(8,128)(2,1)}, bf16[2048,2560]{1,0:T(8,128)(2,1)}, u32[]{:S(2)}, u32[]{:S(2)}) collective-permute-start(bf16[2048,2560]{1,0:T(8,128)(2,1)} %get-tuple-element.86), channel_id=1, source_target_pairs={{0,3},{3,0},{1,2},{2,1},{4,7},{7,4},{5,6},{6,5}} | collective-permute-start | bytes 31457288 | tf_op jit(solution)/shard_map/ppermute | solution.py:211
  688.5 16.5 %collective-permute-start.14 = (bf16[2048,2560]{1,0:T(8,128)(2,1)}, bf16[2048,2560]{1,0:T(8,128)(2,1)}, u32[]{:S(2)}, u32[]{:S(2)}) collective-permute-start(bf16[2048,2560]{1,0:T(8,128)(2,1)} %collective-permute-done.11.b2), channel_id=1, source_target_pairs={{0,1},{1,0},{2,3},{3,2},{4,5},{5,4},{6,7},{7,6}} | collective-permute-start | bytes 31457288 | tf_op jit(solution)/shard_map/ppermute | solution.py:215
  688.6 227.5 %collective-permute-start.10 = (bf16[2048,2560]{1,0:T(8,128)(2,1)}, bf16[2048,2560]{1,0:T(8,128)(2,1)}, u32[]{:S(2)}, u32[]{:S(2)}) collective-permute-start(bf16[2048,2560]{1,0:T(8,128)(2,1)} %get-tuple-element.87), channel_id=1, source_target_pairs={{0,3},{3,0},{1,2},{2,1},{4,7},{7,4},{5,6},{6,5}} | collective-permute-start | bytes 31457288 | tf_op jit(solution)/shard_map/ppermute | solution.py:211
  916.1 16.5 %collective-permute-start.15 = (bf16[2048,2560]{1,0:T(8,128)(2,1)}, bf16[2048,2560]{1,0:T(8,128)(2,1)}, u32[]{:S(2)}, u32[]{:S(2)}) collective-permute-start(bf16[2048,2560]{1,0:T(8,128)(2,1)} %collective-permute-done.10.b2), channel_id=1, source_target_pairs={{0,1},{1,0},{2,3},{3,2},{4,5},{5,4},{6,7},{7,6}} | collective-permute-start | bytes 31457288 | tf_op jit(solution)/shard_map/ppermute | solution.py:215
  924.7 182.8 %collective-permute-start.17 = (bf16[2048,2048]{1,0:T(8,128)(2,1)}, bf16[2048,2048]{1,0:T(8,128)(2,1)}, u32[]{:S(2)}, u32[]{:S(2)}) collective-permute-start(bf16[2048,2048]{1,0:T(8,128)(2,1)} %slice.75), channel_id=1, source_target_pairs={{0,3},{3,0},{1,2},{2,1},{4,7},{7,4},{5,6},{6,5}} | collective-permute-start | bytes 25165832 | tf_op jit(solution)/shard_map/ppermute | solution.py:211
  1107.5 13.5 collective-permute-start.18
  1113.4 137.6 %collective-permute-start.16 = (bf16[2048,1536]{1,0:T(8,128)(2,1)}, bf16[2048,1536]{1,0:T(8,128)(2,1)}, u32[]{:S(2)}, u32[]{:S(2)}) collective-permute-start(bf16[2048,1536]{1,0:T(8,128)(2,1)} %slice.74), channel_id=1, source_target_pairs={{0,3},{3,0},{1,2},{2,1},{4,7},{7,4},{5,6},{6,5}} | collective-permute-start | bytes 18874376 | tf_op jit(solution)/shard_map/ppermute | solution.py:211
  1251.0 10.4 collective-permute-start.19
  1254.0 92.7 %collective-permute-start.9 = (bf16[2048,1024]{1,0:T(8,128)(2,1)S(1)}, bf16[2048,1024]{1,0:T(8,128)(2,1)}, u32[]{:S(2)}, u32[]{:S(2)}) collective-permute-start(bf16[2048,1024]{1,0:T(8,128)(2,1)S(1)} %slice.70), channel_id=1, source_target_pairs={{0,3},{3,0},{1,2},{2,1},{4,7},{7,4},{5,6},{6,5}} | collective-permute-start | bytes 12582920 | tf_op jit(solution)/shard_map/ppermute | solution.py:211
  1261.4 2.7 copy-start.11
  1346.7 56.4 %collective-permute-start.20 = (bf16[2048,1024]{1,0:T(8,128)(2,1)}, bf16[2048,1024]{1,0:T(8,128)(2,1)}, u32[]{:S(2)}, u32[]{:S(2)}) collective-permute-start(bf16[2048,1024]{1,0:T(8,128)(2,1)} %collective-permute-done.9.refs_2_), channel_id=1, source_target_pairs={{0,1},{1,0},{2,3},{3,2},{4,5},{5,4},{6,7},{7,6}} | collective-permute-start | bytes 12582920 | tf_op jit(solution)/shard_map/ppermute | solution.py:215
  1349.9 81.6 %collective-permute-start.8 = (bf16[2048,512]{1,0:T(8,128)(2,1)}, bf16[2048,512]{1,0:T(8,128)(2,1)}, u32[]{:S(2)}, u32[]{:S(2)}) collective-permute-start(bf16[2048,512]{1,0:T(8,128)(2,1)} %slice.69), channel_id=1, source_target_pairs={{0,3},{3,0},{1,2},{2,1},{4,7},{7,4},{5,6},{6,5}} | collective-permute-start | bytes 6291464 | tf_op jit(solution)/shard_map/ppermute | solution.py:211
  1403.1 3.4 copy-start.1
  1406.5 3.4 copy-start.5
  1431.5 4.4 collective-permute-start.21
  1432.9 25.0 %collective-permute-start.25 = (bf16[2048,256]{1,0:T(8,128)(2,1)S(1)}, bf16[2048,256]{1,0:T(8,128)(2,1)}, u32[]{:S(2)}, u32[]{:S(2)}) collective-permute-start(bf16[2048,256]{1,0:T(8,128)(2,1)S(1)} %slice.79), channel_id=1, source_target_pairs={{0,3},{3,0},{1,2},{2,1},{4,7},{7,4},{5,6},{6,5}} | collective-permute-start | bytes 3145736 | tf_op jit(solution)/shard_map/ppermute | solution.py:211
  1458.0 15.0 collective-permute-start.26
  1469.5 18.8 %collective-permute-start.24 = (bf16[768,256]{1,0:T(8,128)(2,1)S(1)}, bf16[768,256]{1,0:T(8,128)(2,1)S(1)}, u32[]{:S(2)}, u32[]{:S(2)}) collective-permute-start(bf16[768,256]{1,0:T(8,128)(2,1)S(1)} %slice.78), channel_id=1, source_target_pairs={{0,3},{3,0},{1,2},{2,1},{4,7},{7,4},{5,6},{6,5}} | collective-permute-start | bytes 1179656 | tf_op jit(solution)/shard_map/ppermute | solution.py:211
  1471.2 39.9 %collective-permute-start.23 = (bf16[512,256]{1,0:T(8,128)(2,1)}, bf16[512,256]{1,0:T(8,128)(2,1)}, u32[]{:S(2)}, u32[]{:S(2)}) collective-permute-start(bf16[512,256]{1,0:T(8,128)(2,1)} %slice.77), channel_id=1, source_target_pairs={{0,3},{3,0},{1,2},{2,1},{4,7},{7,4},{5,6},{6,5}} | collective-permute-start | bytes 786440 | tf_op jit(solution)/shard_map/ppermute | solution.py:211
  1472.9 3.4 copy-start.2
  1476.3 3.4 copy-start.6
  1479.7 1.6 copy-start.9
  1488.3 11.3 collective-permute-start.27
  1499.6 3.4 copy-start.3
  1503.0 3.4 copy-start.7
  1506.4 1.6 copy-start.8
  1511.1 1.8 collective-permute-start.28
  1512.5 6.9 collective-permute-start.22
  1519.3 1.4 collective-permute-start.29
